TPU v7x, 32 devices: a whole 2x2x4 slice. The times are simulated.
32 devices in a mesh: req: 16 (over z, y, x), tp: 2 (over core).
Axes of the slice: x: 2, y: 2, z: 4, core: 2. Of those that a mesh axis runs over, the one named last changes fastest.
Arguments:
- tree_queries: bfloat16 [16, 512, 4096], P('req', None, 'tp'), may hold values from -512 to 512
- tree_keys: bfloat16 [16, 512, 512], P('req', None, 'tp'), may hold values from -6 to 6
- tree_values: bfloat16 [16, 512, 512], P('req', None, 'tp'), may hold values from -6 to 6
- cache_keys: bfloat16 [16, 1024, 512], P('req', None, 'tp'), may hold values from -6 to 6
- cache_values: bfloat16 [16, 1024, 512], P('req', None, 'tp'), may hold values from -6 to 6
- sinks: float32 [64], P('tp'), may hold values from 7 to 11
- parents: int32 [16, 512], P('req'), may hold values from 0 to 510, as said below
- tile_counts: int32 [16], P('req'), may hold values from 1 to 4, 32 in all
- out_weight: bfloat16 [4096, 2880], P('tp', 'req'), may hold values from -0.71875 to 0.71875
Outputs:
- mixed: bfloat16 [16, 512, 2880], P('req', 'tp')
Inputs may be any that keep to these rules, and one draw needn't show every extreme that they name: `parents`: each position's parent stands before it; position 0 is its own parent. `tile_counts`: the counts sum to 32.
All inputs are finite; a program needn't handle non-finite values. No bound on the sum of `tile_counts` on one device may be relied on, other than what follows from the above.
Results may differ from a plain program's by a relative error of at most 0.024.
Values may be sent and summed in bfloat16 or wider, within the bound.
No kernel may reach another device: no remote copies, remote signals or barrier semaphores. Data moves between devices by JAX's collectives and lax.ppermute only.
A program may use at most 128 MiB of HBM per device.

v0:
```python
import functools

import jax
import jax.numpy as jnp
from jax import lax
from jax.experimental import pallas as pl
from jax.experimental.pallas import tpu as pltpu
from jax.sharding import PartitionSpec as P


HEADS = 64
KV_HEADS = 8
HEAD_DIM = 64
TREE = 512
TILE = 128
WIDE = 2 * HEAD_DIM
LOG2_E = 1.4426950408889634
masked_score = -1e30


def product(left, right):
    return jnp.dot(left, right, preferred_element_type=jnp.float32)


def ancestry_kernel(parent_ref, bias_ref, seen):
    tiles = TREE // TILE
    lane = lax.broadcasted_iota(jnp.int32, (TILE, TILE), 1)
    key = lax.broadcasted_iota(jnp.int32, (TILE, TILE), 0)

    def hop(key_tile, row_tile):
        parent = parent_ref[:, row_tile * TILE : (row_tile + 1) * TILE]
        return jnp.broadcast_to(parent, (TILE, TILE)) == key + key_tile * TILE

    inner = [(hop(t, t) | (lane == key)).astype(jnp.bfloat16) for t in range(tiles)]
    reach = 1
    while reach < TILE:
        inner = [jnp.minimum(product(r, r), 1.0).astype(jnp.bfloat16) for r in inner]
        reach *= 2
    seen[...] = jnp.zeros_like(seen)
    for t in range(tiles):
        rows = slice(t * TILE, (t + 1) * TILE)
        if t:
            up = jnp.concatenate([hop(u, t).astype(jnp.bfloat16) for u in range(t)], 0)
            last = product(up, inner[t]).astype(jnp.bfloat16)
            seen[: t * TILE, rows] = product(seen[: t * TILE, : t * TILE], last).astype(jnp.bfloat16)
        seen[rows, rows] = inner[t]
    bias_ref[...] = jnp.where(seen[...].astype(jnp.float32) > 0.5, 0.0, masked_score)


def ancestry(parents):
    return pl.pallas_call(
        ancestry_kernel,
        out_shape=jax.ShapeDtypeStruct((TREE, TREE), jnp.float32),
        in_specs=[pl.BlockSpec(memory_space=pltpu.VMEM)],
        out_specs=pl.BlockSpec(memory_space=pltpu.VMEM),
        scratch_shapes=[pltpu.VMEM((TREE, TREE), jnp.bfloat16)],
        compiler_params=pltpu.CompilerParams(vmem_limit_bytes=8 << 20),
        name="ancestry",
        cost_estimate=pl.CostEstimate(
            flops=2 * TREE**3, bytes_accessed=4 * TREE * TREE, transcendentals=0
        ),
    )(parents)


ONES = 16


def attend_kernel(
    kv_head,
    first,
    live_ref,
    sink_ref,
    query_ref,
    tree_k_ref,
    tree_v_ref,
    cache_k_ref,
    cache_v_ref,
    bias_ref,
    out_ref,
    key_left,
    key_right,
    values,
    score_left,
    score_right,
):
    ctx = cache_k_ref.shape[0]
    pairs = out_ref.shape[0] // WIDE
    factor = LOG2_E * HEAD_DIM**-0.5
    sink_scale = HEAD_DIM**0.5
    near = kv_head % 2
    columns = slice(kv_head // 2 * WIDE, kv_head // 2 * WIDE + WIDE)
    for start, key_src, value_src in (
        (0, cache_k_ref, cache_v_ref),
        (ctx, tree_k_ref, tree_v_ref),
    ):
        rows = key_src.shape[0]
        span = slice(start, start + rows)
        right = lax.broadcasted_iota(jnp.int32, (rows, WIDE), 1) >= HEAD_DIM
        own = right if near else jnp.logical_not(right)
        key = jnp.where(own, key_src[:, columns].astype(jnp.float32), 0.0)
        moved = pltpu.roll(key, HEAD_DIM, 1)
        key_left[span] = (moved if near else key).astype(jnp.bfloat16)
        key_right[span] = (key if near else moved).astype(jnp.bfloat16)
        turned = value_src[:, columns].astype(jnp.float32).T
        values[:HEAD_DIM, span] = turned[near * HEAD_DIM : (near + 1) * HEAD_DIM].astype(jnp.bfloat16)
    values[HEAD_DIM:] = jnp.ones((ONES, values.shape[1]), jnp.bfloat16)
    live = live_ref[0]

    def score(tile, keys, store):
        rows = pl.ds(pl.multiple_of(tile * TILE, TILE), TILE)
        start = first * HEAD_DIM
        query = jnp.concatenate(
            [query_ref[rows, start + p * WIDE : start + (p + 1) * WIDE] for p in range(pairs)], 0
        )
        store[...] = lax.dot_general(
            keys[...], query, (((1,), (1,)), ((), ())), preferred_element_type=jnp.float32
        )

    def mix(tile, side, store):
        rows = pl.ds(pl.multiple_of(tile * TILE, TILE), TILE)
        bias = bias_ref[:, rows]
        bias = jnp.concatenate([bias] * pairs, 1)
        scores = jnp.concatenate([store[:ctx], store[ctx:] + bias], 0)
        sinks = [sink_ref[:, first + 2 * p + side : first + 2 * p + side + 1] for p in range(pairs)]
        sink = jnp.concatenate([jnp.broadcast_to(s, (1, TILE)) for s in sinks], 1) * sink_scale
        peak = jnp.maximum(scores.max(0, keepdims=True), sink)
        probs = jnp.exp2((scores - peak) * factor).astype(jnp.bfloat16)
        sums = product(values[...], probs)
        below = sums[HEAD_DIM : HEAD_DIM + 1] + jnp.exp2((sink - peak) * factor)
        mixed = (sums[:HEAD_DIM] / below).astype(out_ref.dtype)
        for p in range(pairs):
            top = p * WIDE + side * HEAD_DIM
            out_ref[top : top + HEAD_DIM, rows] = mixed[:, p * TILE : (p + 1) * TILE]

    out_ref[...] = jnp.zeros_like(out_ref)
    score(0, key_left, score_left)

    @pl.loop(0, live)
    def tile_step(tile):
        score(tile, key_right, score_right)
        mix(tile, 0, score_left)
        score(jnp.minimum(tile + 1, live - 1), key_left, score_left)
        mix(tile, 1, score_right)


def attend(part, parts, live, sinks, queries, tree_k, tree_v, cache_k, cache_v, bias):
    width = queries.shape[1] // parts
    first = part * width // HEAD_DIM
    kv_head = first // (HEADS // KV_HEADS)
    keys = cache_k.shape[0] + tree_k.shape[0]
    smem = pl.BlockSpec(memory_space=pltpu.SMEM)
    vmem = pl.BlockSpec(memory_space=pltpu.VMEM)
    rows = width // WIDE * TILE
    return pl.pallas_call(
        functools.partial(attend_kernel, kv_head, first),
        out_shape=jax.ShapeDtypeStruct((width, TREE), jnp.bfloat16),
        in_specs=[smem] + [vmem] * 7,
        out_specs=vmem,
        scratch_shapes=[
            pltpu.VMEM((keys, WIDE), jnp.bfloat16),
            pltpu.VMEM((keys, WIDE), jnp.bfloat16),
            pltpu.VMEM((HEAD_DIM + ONES, keys), jnp.bfloat16),
            pltpu.VMEM((keys, rows), jnp.float32),
            pltpu.VMEM((keys, rows), jnp.float32),
        ],
        compiler_params=pltpu.CompilerParams(vmem_limit_bytes=16 << 20),
        cost_estimate=pl.CostEstimate(
            flops=16 * TREE * keys * width, bytes_accessed=3 << 20, transcendentals=0
        ),
    )(live, sinks, queries, tree_k, tree_v, cache_k, cache_v, bias)


def project_kernel(line, parts, ranks, whom_ref, *refs):
    blocks = sum(len(candidates) for candidates in line)
    weights, refs = refs[:blocks], refs[blocks:]
    requests, outs, (held, sems) = refs[: 2 * parts], refs[2 * parts : -2], refs[-2:]
    place, rank = whom_ref[0] // 4, whom_ref[1]
    offset = 0
    for n, candidates in enumerate(line):
        for i, places in enumerate(candidates):
            copy = pltpu.make_async_copy(weights[offset + i], held.at[n], sems.at[n])
            if len(candidates) == 1:
                copy.start()
            else:
                here = functools.reduce(jnp.logical_or, [place == p for p in places])
                pl.when(here)(copy.start)
        offset += len(candidates)
    rows = outs[0].shape[-1]
    for n in range(len(line)):
        pltpu.make_async_copy(weights[0], held.at[n], sems.at[n]).wait()
        for which in range(2):
            for shift, out_ref in enumerate(outs):
                span = slice(None)
                if len(outs) > 1:
                    span = pl.ds(pl.multiple_of((rank + shift) % ranks * rows, rows), rows)
                total = 0.0
                for part in range(parts):
                    attention = requests[which * parts + part]
                    depth = attention.shape[0]
                    lanes = slice(part * depth, (part + 1) * depth)
                    total = total + product(held[n, :, lanes], attention[:, span])
                out_ref[which, n] = total.astype(out_ref.dtype)


def project(whom, ranks, line, own, partner):
    blocks = [block for candidates in line for block, _ in candidates]
    columns, depth = blocks[0].shape
    count = len(line)
    rows = TREE // ranks
    cut = rows % 128 == 0
    shape = (2, count, columns, rows if cut else TREE)
    vmem = pl.BlockSpec(memory_space=pltpu.VMEM)
    outs = pl.pallas_call(
        functools.partial(
            project_kernel, [[p for _, p in candidates] for candidates in line], len(own), ranks
        ),
        out_shape=[jax.ShapeDtypeStruct(shape, jnp.bfloat16)] * (ranks if cut else 1),
        in_specs=[pl.BlockSpec(memory_space=pltpu.SMEM)]
        + [pl.BlockSpec(memory_space=pl.ANY)] * len(blocks)
        + [vmem] * (2 * len(own)),
        out_specs=[vmem] * (ranks if cut else 1),
        scratch_shapes=[
            pltpu.VMEM((count, columns, depth), jnp.bfloat16),
            pltpu.SemaphoreType.DMA((count,)),
        ],
        compiler_params=pltpu.CompilerParams(vmem_limit_bytes=16 << 20),
        cost_estimate=pl.CostEstimate(
            flops=8 * count * columns * depth * TREE,
            bytes_accessed=2 * count * columns * (depth + 2 * TREE),
            transcendentals=0,
        ),
    )(whom, *blocks, *own, *partner)
    if cut:
        return list(outs)
    rank = whom[1]
    return [
        lax.dynamic_slice_in_dim(outs[0], (rank + shift) % ranks * rows, rows, 3)
        for shift in range(ranks)
    ]


def settle_kernel(count, *refs):
    for which in range(2):
        total = refs[0][which].astype(jnp.float32)
        for term in refs[1:count]:
            total = total + term[which].astype(jnp.float32)
        refs[count + which][...] = total.astype(jnp.bfloat16)


def settle(terms):
    vmem = pl.BlockSpec(memory_space=pltpu.VMEM)
    shape = jax.ShapeDtypeStruct(terms[0].shape[1:], jnp.bfloat16)
    return pl.pallas_call(
        functools.partial(settle_kernel, len(terms)),
        out_shape=[shape] * 2,
        in_specs=[vmem] * len(terms),
        out_specs=[vmem] * 2,
        compiler_params=pltpu.CompilerParams(vmem_limit_bytes=16 << 20),
    )(*terms)


def arrange_kernel(homes, groups, whom_ref, *refs):
    parts, (out_ref, held) = refs[: 2 * groups], refs[2 * groups :]
    request = whom_ref[0]
    place, side, member = request // 4, request // 2 % 2, request % 2
    slots = len(homes[0]) * 2
    for which in range(2):
        at = 0
        for part in parts[which * groups : (which + 1) * groups]:
            held[which * slots + at : which * slots + at + part.shape[0]] = part[...]
            at += part.shape[0]
    columns = held.shape[1]

    def block(index):
        slot = 0
        for p, row in enumerate(homes):
            slot = jnp.where(place == p, row[index // 4], slot)
        slot = slot * 2 + jnp.where(side == index // 2 % 2, 0, 1)
        return held[slot + jnp.where(member == index % 2, 0, slots)].astype(jnp.float32)

    for pair in range(slots):
        both = jnp.concatenate([block(2 * pair), block(2 * pair + 1)], 0)
        out_ref[2 * pair * columns : 2 * (pair + 1) * columns] = both.astype(out_ref.dtype)


def arrange(whom, homes, mine, other):
    vmem = pl.BlockSpec(memory_space=pltpu.VMEM)
    columns, rows = mine[0].shape[1:]
    count = sum(part.shape[0] for part in mine + other)
    return pl.pallas_call(
        functools.partial(arrange_kernel, homes, len(mine)),
        out_shape=jax.ShapeDtypeStruct((count * columns, rows), jnp.bfloat16),
        in_specs=[pl.BlockSpec(memory_space=pltpu.SMEM)] + [vmem] * (2 * len(mine)),
        out_specs=vmem,
        scratch_shapes=[pltpu.VMEM((count, columns, rows), jnp.bfloat16)],
        compiler_params=pltpu.CompilerParams(vmem_limit_bytes=16 << 20),
        name="arrange",
    )(whom, *mine, *other)


def arrivals(place, length):
    below = [(place - step, "up", step) for step in range(1, place + 1)]
    above = [(place + step, "down", step) for step in range(1, length - place)]
    return sorted(below + above, key=lambda item: (item[2], item[1] == "down"))


def timetable(length, parts):
    plan = {}
    at = 2
    for step in range(1, length):
        plan.setdefault(min(at, parts), []).append(("face", step))
        if step + 1 < length:
            plan.setdefault(min(at + 1, parts), []).append(("line", step + 1))
        at += 3
    return plan


def per_device(
    reqs,
    ranks,
    tree_queries,
    tree_keys,
    tree_values,
    cache_keys,
    cache_values,
    sinks,
    parents,
    tile_counts,
    out_weight,
):
    length = reqs // 4
    whom = jnp.stack([lax.axis_index("req"), lax.axis_index("tp")]).astype(jnp.int32)
    order = [arrivals(p, length) for p in range(length)]

    def along(step):
        return [
            (p * 4 + low, (p + step) * 4 + low)
            for p in range(length)
            for low in range(4)
            if 0 <= p + step < length
        ]

    def restrict(hops, keep):
        return [hop for hop in hops if keep(hop[0] // 4)]

    across = [(i, i ^ 2) for i in range(reqs)]
    swap = [(i, i ^ 1) for i in range(reqs)]
    columns = out_weight.T
    line = {("up", 0): columns, ("down", 0): columns}
    facing = {("up", 0): lax.ppermute(columns, "req", across)}

    def forward(kind, step):
        for way, sign in (("up", 1), ("down", -1)):
            if kind == "face":
                hops = restrict(across, lambda p: 0 <= p - sign * step < length)
                facing[way, step] = lax.ppermute(line[way, step], "req", hops)
                continue

            def sends(p):
                return 0 <= p - sign * (step - 1) < length and 0 <= p + sign < length

            hops = restrict(along(sign), sends)
            line[way, step] = lax.ppermute(line[way, step - 1], "req", hops)

    kv_local = cache_keys.shape[2] // HEAD_DIM
    odd = kv_local % 2 * HEAD_DIM
    tree_k, tree_v, cache_k, cache_v = (
        jnp.pad(array[0], ((0, 0), (0, odd)))
        for array in (tree_keys, tree_values, cache_keys, cache_values)
    )
    forward("line", 1)
    bias = ancestry(parents)
    own, partner = [], []
    parts = 2 * kv_local
    plan = timetable(length, parts)
    live = tile_counts
    for part in range(parts + 1):
        for kind, step in plan.get(part, []):
            if part < parts:
                needed = step if kind == "face" else step - 1
                live, *_ = lax.optimization_barrier((live, line["up", needed], line["down", needed]))
            forward(kind, step)
        if part == parts:
            break
        chunk = attend(
            part,
            parts,
            live,
            sinks[None],
            tree_queries[0],
            tree_k,
            tree_v,
            cache_k,
            cache_v,
            bias,
        )
        live, chunk = lax.optimization_barrier((live, chunk))
        own.append(chunk)
        partner.append(lax.ppermute(chunk, "req", swap))

    table = [
        [(("up", 0), p)] + [((way, step), source) for source, way, step in order[p]]
        for p in range(length)
    ]
    homes = [[0] * length for _ in range(length)]
    for p, row in enumerate(table):
        for n, (_, source) in enumerate(row):
            homes[p][source] = n

    def candidates(store, n):
        keys = sorted({row[n][0] for row in table})
        return [(store[k], [p for p, row in enumerate(table) if row[n][0] == k]) for k in keys]

    slots = [(store, n) for n in range(length) for store in (line, facing)]
    groups = [g for g in (slots[:3], slots[3:-2], slots[-2:-1], slots[-1:]) if g]
    mine, other = [], []
    for group in groups:
        terms = project(whom, ranks, [candidates(*slot) for slot in group], own, partner)
        for shift in range(1, ranks):
            hops = [(r, (r + shift) % ranks) for r in range(ranks)]
            terms[shift] = lax.ppermute(terms[shift], "tp", hops)
        kept, given = settle(terms)
        mine.append(kept)
        other.append(lax.ppermute(given, "req", swap))
    return arrange(whom, homes, mine, other).T[None]


def solution(mesh):
    in_specs = (
        P("req", None, "tp"),
        P("req", None, "tp"),
        P("req", None, "tp"),
        P("req", None, "tp"),
        P("req", None, "tp"),
        P("tp"),
        P("req", None),
        P("req"),
        P("tp", "req"),
    )
    out_specs = P("req", "tp", None)
    return jax.shard_map(
        functools.partial(per_device, mesh.shape["req"], mesh.shape["tp"]),
        mesh=mesh,
        in_specs=in_specs,
        out_specs=out_specs,
        check_vma=False,
    )
```

profile of v0, /device:TPU:28, one launch (start us, length us, event | category | flops | bytes accessed | tf_op | source)
XLA Modules:
  0.0 151.9 jit_solution(1499640205850270612)
XLA Ops:
  0.5 2.4 %collective-permute-start.1 = (bf16[180,2048]{1,0:T(8,128)(2,1)}, bf16[180,2048]{1,0:T(8,128)(2,1)S(1)}, u32[]{:S(2)}, u32[]{:S(2)}) collective-permute-start(bf16[180,2048]{1,0:T(8,128)(2,1)} %bitcast.21), channel_id=1, source_target_pairs={{8,0},{10,2},{12,4},{14,6},{16,8},{18,10},{20,12},{22,14},{24,16},... | collective-permute-start | bytes 2211848 | tf_op jit(solution)/shard_map/ppermute | solution.py:363
  2.9 1.3 collective-permute-start.2
  5.5 1.6 %ancestry.1.bias_ref = f32[512,512]{1,0:T(8,128)S(1)} custom-call(s32[1,512]{1,0:T(1,128)S(1)} %copy-done.9), custom_call_target="tpu_custom_call" | custom-call | flops 268435456 | bytes 1048576 | tf_op jit(solution)/shard_map/ancestry/pallas_call | solution.py:51
  7.2 1.6 %copy-done.10 = bf16[1,512,2048]{2,1,0:T(8,128)(2,1)S(1)} copy-done((bf16[1,512,2048]{2,1,0:T(8,128)(2,1)S(1)}, bf16[1,512,2048]{2,1,0:T(8,128)(2,1)}, u32[]{:S(2)}) %copy-start.10) | copy-done | bytes 2097176
  8.8 1.0 copy-done.18
  9.8 1.0 copy-done.19
  10.9 0.9 copy-done.20
  11.8 0.9 copy-done.21
  13.4 4.2 %shard_map.91.refs_4_.refs_8_ = bf16[256,512]{1,0:T(8,128)(2,1)S(1)} custom-call(s32[1]{0:T(128)S(6)} %copy.14.live_ref, f32[1,32]{1,0:T(1,128)S(1)} %bitcast.56, bf16[512,2048]{1,0:T(8,128)(2,1)S(1)} %bitcast.12, bf16[512,256]{1,0:T(8,128)(2,1)S(1)} %bitcast.40, bf16[512,256]{1,0:T(8,128)(2,1)S(1)} %bitcast.48, bf16[1024,256]{1,0:T(8,128)(2,1)S(1)} %bitcast.24, ...), custom_call_target="tpu_custom_call" | custom-call | flops 3221225472 | bytes 3145728 | tf_op jit(solution)/shard_map/pallas_call | solution.py:154
  17.9 4.2 %shard_map.92.refs_5_.refs_9_ = bf16[256,512]{1,0:T(8,128)(2,1)S(1)} custom-call(s32[1]{0:T(128)S(6)} %copy.14.live_ref, f32[1,32]{1,0:T(1,128)S(1)} %bitcast.57, bf16[512,2048]{1,0:T(8,128)(2,1)S(1)} %bitcast.13, bf16[512,256]{1,0:T(8,128)(2,1)S(1)} %bitcast.41, bf16[512,256]{1,0:T(8,128)(2,1)S(1)} %bitcast.49, bf16[1024,256]{1,0:T(8,128)(2,1)S(1)} %bitcast.25, ...), custom_call_target="tpu_custom_call" | custom-call | flops 3221225472 | bytes 3145728 | tf_op jit(solution)/shard_map/pallas_call | solution.py:154
  22.1 4.3 %shard_map.93.refs_6_.refs_10_ = bf16[256,512]{1,0:T(8,128)(2,1)S(1)} custom-call(s32[1]{0:T(128)S(6)} %copy.14.live_ref, f32[1,32]{1,0:T(1,128)S(1)} %bitcast.58, bf16[512,2048]{1,0:T(8,128)(2,1)S(1)} %bitcast.14, bf16[512,256]{1,0:T(8,128)(2,1)S(1)} %bitcast.42, bf16[512,256]{1,0:T(8,128)(2,1)S(1)} %bitcast.50, bf16[1024,256]{1,0:T(8,128)(2,1)S(1)} %bitcast.26, ...), custom_call_target="tpu_custom_call" | custom-call | flops 3221225472 | bytes 3145728 | tf_op jit(solution)/shard_map/pallas_call | solution.py:154
  26.4 4.3 %shard_map.94.refs_7_.refs_11_ = bf16[256,512]{1,0:T(8,128)(2,1)S(1)} custom-call(s32[1]{0:T(128)S(6)} %copy.14.live_ref, f32[1,32]{1,0:T(1,128)S(1)} %bitcast.59, bf16[512,2048]{1,0:T(8,128)(2,1)S(1)} %bitcast.15, bf16[512,256]{1,0:T(8,128)(2,1)S(1)} %bitcast.43, bf16[512,256]{1,0:T(8,128)(2,1)S(1)} %bitcast.51, bf16[1024,256]{1,0:T(8,128)(2,1)S(1)} %bitcast.27, ...), custom_call_target="tpu_custom_call" | custom-call | flops 3221225472 | bytes 3145728 | tf_op jit(solution)/shard_map/pallas_call | solution.py:154
  30.7 1.3 collective-permute-start.3
  32.0 1.5 %collective-permute-start.4 = (bf16[180,2048]{1,0:T(8,128)(2,1)S(1)}, bf16[180,2048]{1,0:T(8,128)(2,1)}, u32[]{:S(2)}, u32[]{:S(2)}) collective-permute-start(bf16[180,2048]{1,0:T(8,128)(2,1)S(1)} %collective-permute-done.1.refs_2_), channel_id=1, source_target_pairs={{8,0},{10,2},{12,4},{14,6},{16,8},{18,10},{20,12},{22,14},{9,1},{1... | collective-permute-start | bytes 2211848 | tf_op jit(solution)/shard_map/ppermute | solution.py:363
  33.5 4.2 %shard_map.95.refs_8_.refs_12_ = bf16[256,512]{1,0:T(8,128)(2,1)S(1)} custom-call(s32[1]{0:T(128)S(6)} %copy.14.live_ref, f32[1,32]{1,0:T(1,128)S(1)} %bitcast.60, bf16[512,2048]{1,0:T(8,128)(2,1)S(1)} %bitcast.16, bf16[512,256]{1,0:T(8,128)(2,1)S(1)} %bitcast.44, bf16[512,256]{1,0:T(8,128)(2,1)S(1)} %bitcast.52, bf16[1024,256]{1,0:T(8,128)(2,1)S(1)} %bitcast.28, ...), custom_call_target="tpu_custom_call" | custom-call | flops 3221225472 | bytes 3145728 | tf_op jit(solution)/shard_map/pallas_call | solution.py:154
  37.7 4.2 %shard_map.96.refs_9_.refs_13_ = bf16[256,512]{1,0:T(8,128)(2,1)S(1)} custom-call(s32[1]{0:T(128)S(6)} %copy.14.live_ref, f32[1,32]{1,0:T(1,128)S(1)} %bitcast.61, bf16[512,2048]{1,0:T(8,128)(2,1)S(1)} %bitcast.17, bf16[512,256]{1,0:T(8,128)(2,1)S(1)} %bitcast.45, bf16[512,256]{1,0:T(8,128)(2,1)S(1)} %bitcast.53, bf16[1024,256]{1,0:T(8,128)(2,1)S(1)} %bitcast.29, ...), custom_call_target="tpu_custom_call" | custom-call | flops 3221225472 | bytes 3145728 | tf_op jit(solution)/shard_map/pallas_call | solution.py:154
  42.7 4.5 %shard_map.97.refs_10_.refs_14_ = bf16[256,512]{1,0:T(8,128)(2,1)S(1)} custom-call(s32[1]{0:T(128)S(6)} %copy.14.live_ref, f32[1,32]{1,0:T(1,128)S(1)} %bitcast.62, bf16[512,2048]{1,0:T(8,128)(2,1)S(1)} %bitcast.18, bf16[512,256]{1,0:T(8,128)(2,1)S(1)} %bitcast.46, bf16[512,256]{1,0:T(8,128)(2,1)S(1)} %bitcast.54, bf16[1024,256]{1,0:T(8,128)(2,1)S(1)} %bitcast.30, ...), custom_call_target="tpu_custom_call" | custom-call | flops 3221225472 | bytes 3145728 | tf_op jit(solution)/shard_map/pallas_call | solution.py:154
  47.2 3.5 %collective-permute-done.3.refs_4_.refs_2_ = bf16[180,2048]{1,0:T(8,128)(2,1)} collective-permute-done((bf16[180,2048]{1,0:T(8,128)(2,1)}, bf16[180,2048]{1,0:T(8,128)(2,1)}, u32[]{:S(2)}, u32[]{:S(2)}) %collective-permute-start.3) | collective-permute-done | bytes 737312 | tf_op jit(solution)/shard_map/ppermute | solution.py:363
  50.7 2.0 %collective-permute-start.8 = (bf16[256,512]{1,0:T(8,128)(2,1)S(1)}, bf16[256,512]{1,0:T(8,128)(2,1)S(1)}, u32[]{:S(2)}, u32[]{:S(2)}) collective-permute-start(bf16[256,512]{1,0:T(8,128)(2,1)S(1)} %shard_map.94.refs_7_.refs_11_), channel_id=1, source_target_pairs={{0,2},{2,0},{4,6},{6,4},{8,10},{10,8},{12,14},{14,12},{16,18},{18,... | collective-permute-start | bytes 786440 | tf_op jit(solution)/shard_map/ppermute | solution.py:399
  52.7 4.3 %shard_map.98.refs_11_.refs_15_ = bf16[256,512]{1,0:T(8,128)(2,1)S(1)} custom-call(s32[1]{0:T(128)S(6)} %copy.14.live_ref, f32[1,32]{1,0:T(1,128)S(1)} %bitcast.63, bf16[512,2048]{1,0:T(8,128)(2,1)S(1)} %bitcast.19, bf16[512,256]{1,0:T(8,128)(2,1)S(1)} %bitcast.47, bf16[512,256]{1,0:T(8,128)(2,1)S(1)} %bitcast.55, bf16[1024,256]{1,0:T(8,128)(2,1)S(1)} %bitcast.31, ...), custom_call_target="tpu_custom_call" | custom-call | flops 3221225472 | bytes 3145728 | tf_op jit(solution)/shard_map/pallas_call | solution.py:154
  57.1 0.9 copy-done.14
  57.9 2.0 %collective-permute-start.10 = (bf16[256,512]{1,0:T(8,128)(2,1)S(1)}, bf16[256,512]{1,0:T(8,128)(2,1)S(1)}, u32[]{:S(2)}, u32[]{:S(2)}) collective-permute-start(bf16[256,512]{1,0:T(8,128)(2,1)S(1)} %shard_map.96.refs_9_.refs_13_), channel_id=1, source_target_pairs={{0,2},{2,0},{4,6},{6,4},{8,10},{10,8},{12,14},{14,12},{16,18},{18,... | collective-permute-start | bytes 786440 | tf_op jit(solution)/shard_map/ppermute | solution.py:399
  60.0 2.0 %collective-permute-done.7.refs_14_.refs_18_ = bf16[256,512]{1,0:T(8,128)(2,1)S(1)} collective-permute-done((bf16[256,512]{1,0:T(8,128)(2,1)S(1)}, bf16[256,512]{1,0:T(8,128)(2,1)S(1)}, u32[]{:S(2)}, u32[]{:S(2)}) %collective-permute-start.7) | collective-permute-done | bytes 262176 | tf_op jit(solution)/shard_map/ppermute | solution.py:399
  62.0 5.6 %collective-permute-done.8.refs_15_.refs_19_ = bf16[256,512]{1,0:T(8,128)(2,1)S(1)} collective-permute-done((bf16[256,512]{1,0:T(8,128)(2,1)S(1)}, bf16[256,512]{1,0:T(8,128)(2,1)S(1)}, u32[]{:S(2)}, u32[]{:S(2)}) %collective-permute-start.8) | collective-permute-done | bytes 262176 | tf_op jit(solution)/shard_map/ppermute | solution.py:399
  67.6 5.6 %collective-permute-done.9.refs_16_.refs_20_ = bf16[256,512]{1,0:T(8,128)(2,1)S(1)} collective-permute-done((bf16[256,512]{1,0:T(8,128)(2,1)S(1)}, bf16[256,512]{1,0:T(8,128)(2,1)S(1)}, u32[]{:S(2)}, u32[]{:S(2)}) %collective-permute-start.9) | collective-permute-done | bytes 262176 | tf_op jit(solution)/shard_map/ppermute | solution.py:399
  73.2 12.1 %collective-permute-start.15 = (bf16[180,2048]{1,0:T(8,128)(2,1)}, bf16[180,2048]{1,0:T(8,128)(2,1)}, u32[]{:S(2)}, u32[]{:S(2)}) collective-permute-start(bf16[180,2048]{1,0:T(8,128)(2,1)} %collective-permute-done.2.refs_3_), channel_id=1, source_target_pairs={{8,12},{10,14},{12,8},{14,10},{16,20},{18,22},{20,16},{22,18},{24,... | collective-permute-start | bytes 2211848 | tf_op jit(solution)/shard_map/ppermute | solution.py:356
  85.3 0.9 copy-done.16
  86.2 1.5 %collective-permute-start.19 = (bf16[180,2048]{1,0:T(8,128)(2,1)}, bf16[180,2048]{1,0:T(8,128)(2,1)}, u32[]{:S(2)}, u32[]{:S(2)}) collective-permute-start(bf16[180,2048]{1,0:T(8,128)(2,1)} %collective-permute-done.4.refs_3_.refs_0_), channel_id=1, source_target_pairs={{8,0},{10,2},{12,4},{14,6},{9,1},{11,3},{13,5},{15,7}} | collective-permute-start | bytes 2211848 | tf_op jit(solution)/shard_map/ppermute | solution.py:363
  88.5 1.3 collective-permute-start.20
  90.5 1.6 %collective-permute-start.16 = (bf16[180,2048]{1,0:T(8,128)(2,1)}, bf16[180,2048]{1,0:T(8,128)(2,1)}, u32[]{:S(2)}, u32[]{:S(2)}) collective-permute-start(bf16[180,2048]{1,0:T(8,128)(2,1)} %collective-permute-done.4.refs_3_.refs_0_), channel_id=1, source_target_pairs={{0,4},{2,6},{4,0},{6,2},{8,12},{10,14},{12,8},{14,10},{1,5},{3,7},... | collective-permute-start | bytes 2211848 | tf_op jit(solution)/shard_map/ppermute | solution.py:356
  92.8 8.4 %collective-permute-start.17 = (bf16[180,2048]{1,0:T(8,128)(2,1)}, bf16[180,2048]{1,0:T(8,128)(2,1)}, u32[]{:S(2)}, u32[]{:S(2)}) collective-permute-start(bf16[180,2048]{1,0:T(8,128)(2,1)} %collective-permute-done.3.refs_4_.refs_2_), channel_id=1, source_target_pairs={{16,20},{18,22},{20,16},{22,18},{24,28},{26,30},{28,24},{30,26},{1... | collective-permute-start | bytes 2211848 | tf_op jit(solution)/shard_map/ppermute | solution.py:356
  101.2 0.9 copy-done.1
  102.2 0.9 copy-done.4
  103.1 0.9 copy-done.7
  104.1 1.1 copy-done.11
  105.2 1.1 copy-done.13
  106.3 1.1 copy-done.15
  107.5 4.4 %shard_map.99 = (bf16[2,3,180,256]{3,2,1,0:T(8,128)(2,1)S(1)}, bf16[2,3,180,256]{3,2,1,0:T(8,128)(2,1)S(1)}) custom-call(s32[2]{0:T(128)S(1)} %pad_add_fusion.whom_ref, bf16[180,2048]{1,0:T(8,128)(2,1)S(1)} %bitcast.23, bf16[180,2048]{1,0:T(8,128)(2,1)S(1)} %copy-done.15, bf16[180,2048]{1,0:T(8,128)(2,1)S(1)} %copy-done.13, ...), custom_call_target="tpu_custom_call" | custom-call | flops 4529848320 | bytes 3317760 | tf_op jit(solution)/shard_map/pallas_call | solution.py:213
  113.2 1.9 %collective-permute-start.23 = (bf16[180,2048]{1,0:T(8,128)(2,1)}, bf16[180,2048]{1,0:T(8,128)(2,1)S(1)}, u32[]{:S(2)}, u32[]{:S(2)}) collective-permute-start(bf16[180,2048]{1,0:T(8,128)(2,1)} %collective-permute-done.20.refs_3_), channel_id=1, source_target_pairs={{24,28},{26,30},{28,24},{30,26},{25,29},{27,31},{29,25},{31,27}} | collective-permute-start | bytes 2211848 | tf_op jit(solution)/shard_map/ppermute | solution.py:356
  115.1 1.9 %collective-permute-done.17.refs_7_.refs_2_ = bf16[180,2048]{1,0:T(8,128)(2,1)} collective-permute-done((bf16[180,2048]{1,0:T(8,128)(2,1)}, bf16[180,2048]{1,0:T(8,128)(2,1)}, u32[]{:S(2)}, u32[]{:S(2)}) %collective-permute-start.17) | collective-permute-done | bytes 737312 | tf_op jit(solution)/shard_map/ppermute | solution.py:356
  117.0 4.8 %shard_map.101 = (bf16[2,3,180,256]{3,2,1,0:T(8,128)(2,1)S(1)}, bf16[2,3,180,256]{3,2,1,0:T(8,128)(2,1)S(1)}) custom-call(s32[2]{0:T(128)S(1)} %pad_add_fusion.whom_ref, bf16[180,2048]{1,0:T(8,128)(2,1)S(1)} %copy-done.17, bf16[180,2048]{1,0:T(8,128)(2,1)} %collective-permute-done.15.refs_1_, bf16[180,2048]{1,0:T(8,128)(2,1)S(1)} %copy-done.13, ...), custom_call_target="tpu_custom_call" | custom-call | flops 4529848320 | bytes 3317760 | tf_op jit(solution)/shard_map/pallas_call | solution.py:213
  122.3 2.7 %shard_map.103 = (bf16[2,1,180,256]{3,2,1,0:T(8,128)(2,1)S(1)}, bf16[2,1,180,256]{3,2,1,0:T(8,128)(2,1)S(1)}) custom-call(s32[2]{0:T(128)S(1)} %pad_add_fusion.whom_ref, bf16[180,2048]{1,0:T(8,128)(2,1)} %collective-permute-done.4.refs_3_.refs_0_, bf16[180,2048]{1,0:T(8,128)(2,1)} %collective-permute-done.19.refs_1_, ...), custom_call_target="tpu_custom_call" | custom-call | flops 1509949440 | bytes 1105920 | tf_op jit(solution)/shard_map/pallas_call | solution.py:213
  126.5 8.0 %collective-permute-done.23.refs_3_ = bf16[180,2048]{1,0:T(8,128)(2,1)S(1)} collective-permute-done((bf16[180,2048]{1,0:T(8,128)(2,1)}, bf16[180,2048]{1,0:T(8,128)(2,1)S(1)}, u32[]{:S(2)}, u32[]{:S(2)}) %collective-permute-start.23) | collective-permute-done | bytes 737312 | tf_op jit(solution)/shard_map/ppermute | solution.py:356
  134.5 2.0 %shard_map.105 = (bf16[2,1,180,256]{3,2,1,0:T(8,128)(2,1)S(1)}, bf16[2,1,180,256]{3,2,1,0:T(8,128)(2,1)S(1)}) custom-call(s32[2]{0:T(128)S(1)} %pad_add_fusion.whom_ref, bf16[180,2048]{1,0:T(8,128)(2,1)} %collective-permute-done.16.refs_6_.refs_0_, bf16[180,2048]{1,0:T(8,128)(2,1)S(1)} %collective-permute-done.22.refs_1_, ...), custom_call_target="tpu_custom_call" | custom-call | flops 1509949440 | bytes 1105920 | tf_op jit(solution)/shard_map/pallas_call | solution.py:213
  137.1 1.8 %collective-permute-start.27 = (bf16[1,180,256]{2,1,0:T(8,128)(2,1)S(1)}, bf16[1,180,256]{2,1,0:T(8,128)(2,1)S(1)}, u32[]{:S(2)}, u32[]{:S(2)}) collective-permute-start(bf16[1,180,256]{2,1,0:T(8,128)(2,1)S(1)} %get-tuple-element.73), channel_id=1, source_target_pairs={{0,2},{2,0},{4,6},{6,4},{8,10},{10,8},{12,14},{14,12},{16,18},{18,... | collective-permute-start | bytes 276488 | tf_op jit(solution)/shard_map/ppermute | solution.py:424
  139.3 9.1 %collective-permute-done.27.refs_6_ = bf16[1,180,256]{2,1,0:T(8,128)(2,1)S(1)} collective-permute-done((bf16[1,180,256]{2,1,0:T(8,128)(2,1)S(1)}, bf16[1,180,256]{2,1,0:T(8,128)(2,1)S(1)}, u32[]{:S(2)}, u32[]{:S(2)}) %collective-permute-start.27) | collective-permute-done | bytes 92192 | tf_op jit(solution)/shard_map/ppermute | solution.py:424
  148.4 1.5 %collective-permute-done.28.refs_7_ = bf16[1,180,256]{2,1,0:T(8,128)(2,1)S(1)} collective-permute-done((bf16[1,180,256]{2,1,0:T(8,128)(2,1)S(1)}, bf16[1,180,256]{2,1,0:T(8,128)(2,1)S(1)}, u32[]{:S(2)}, u32[]{:S(2)}) %collective-permute-start.28) | collective-permute-done | bytes 92192 | tf_op jit(solution)/shard_map/ppermute | solution.py:424
  150.0 1.9 %arrange.1 = bf16[2880,256]{1,0:T(8,128)(2,1)} custom-call(s32[2]{0:T(128)S(1)} %pad_add_fusion.whom_ref, bf16[3,180,256]{2,1,0:T(8,128)(2,1)S(1)} %get-tuple-element.61.refs_0_, bf16[3,180,256]{2,1,0:T(8,128)(2,1)S(1)} %get-tuple-element.64.refs_1_, bf16[1,180,256]{2,1,0:T(8,128)(2,1)S(1)} %get-tuple-element.67.refs_2_, ...), custom_call_target="tpu_custom_call" | custom-call | tf_op jit(solution)/shard_map/arrange/pallas_call | solution.py:290
  (79 shorter events, 9.5 us)
Async XLA Ops:
  0.0 57.1 %collective-permute-start = (bf16[180,2048]{1,0:T(8,128)(2,1)}, bf16[180,2048]{1,0:T(8,128)(2,1)S(1)}, u32[]{:S(2)}, u32[]{:S(2)}) collective-permute-start(bf16[180,2048]{1,0:T(8,128)(2,1)} %bitcast.20), channel_id=1, source_target_pairs={{0,4},{2,6},{4,0},{6,2},{8,12},{10,14},{12,8},{14,10},{16,20},{18,... | collective-permute-start | bytes 2211848 | tf_op jit(solution)/shard_map/ppermute | solution.py:350
  0.5 31.5 %collective-permute-start.1 = (bf16[180,2048]{1,0:T(8,128)(2,1)}, bf16[180,2048]{1,0:T(8,128)(2,1)S(1)}, u32[]{:S(2)}, u32[]{:S(2)}) collective-permute-start(bf16[180,2048]{1,0:T(8,128)(2,1)} %bitcast.21), channel_id=1, source_target_pairs={{8,0},{10,2},{12,4},{14,6},{16,8},{18,10},{20,12},{22,14},{24,16},... | collective-permute-start | bytes 2211848 | tf_op jit(solution)/shard_map/ppermute | solution.py:363
  2.9 27.7 %collective-permute-start.2 = (bf16[180,2048]{1,0:T(8,128)(2,1)}, bf16[180,2048]{1,0:T(8,128)(2,1)}, u32[]{:S(2)}, u32[]{:S(2)}) collective-permute-start(bf16[180,2048]{1,0:T(8,128)(2,1)} %bitcast.22), channel_id=1, source_target_pairs={{0,8},{2,10},{4,12},{6,14},{8,16},{10,18},{12,20},{14,22},{16,24},... | collective-permute-start | bytes 2211848 | tf_op jit(solution)/shard_map/ppermute | solution.py:363
  7.2 1.6 %copy-start.10 = (bf16[1,512,2048]{2,1,0:T(8,128)(2,1)S(1)}, bf16[1,512,2048]{2,1,0:T(8,128)(2,1)}, u32[]{:S(2)}) copy-start(bf16[1,512,2048]{2,1,0:T(8,128)(2,1)} %param.9) | copy-start | bytes 6291460
  8.8 1.0 copy-start.18
  9.8 1.0 copy-start.19
  10.8 0.9 copy-start.20
  11.8 0.9 copy-start.21
  17.6 29.5 %collective-permute-start.5 = (bf16[256,512]{1,0:T(8,128)(2,1)S(1)}, bf16[256,512]{1,0:T(8,128)(2,1)S(1)}, u32[]{:S(2)}, u32[]{:S(2)}) collective-permute-start(bf16[256,512]{1,0:T(8,128)(2,1)S(1)} %shard_map.91.refs_4_.refs_8_), channel_id=1, source_target_pairs={{0,2},{2,0},{4,6},{6,4},{8,10},{10,8},{12,14},{14,12},{16,18},{18,... | collective-permute-start | bytes 786440 | tf_op jit(solution)/shard_map/ppermute | solution.py:399
  30.7 20.0 %collective-permute-start.3 = (bf16[180,2048]{1,0:T(8,128)(2,1)}, bf16[180,2048]{1,0:T(8,128)(2,1)}, u32[]{:S(2)}, u32[]{:S(2)}) collective-permute-start(bf16[180,2048]{1,0:T(8,128)(2,1)} %collective-permute-done.2.refs_3_), channel_id=1, source_target_pairs={{8,16},{10,18},{12,20},{14,22},{16,24},{18,26},{20,28},{22,30},{9,... | collective-permute-start | bytes 2211848 | tf_op jit(solution)/shard_map/ppermute | solution.py:363
  32.0 10.0 %copy-start.12 = (bf16[180,2048]{1,0:T(8,128)(2,1)}, bf16[180,2048]{1,0:T(8,128)(2,1)S(1)}, u32[]{:S(2)}) copy-start(bf16[180,2048]{1,0:T(8,128)(2,1)S(1)} %collective-permute-done.1.refs_2_) | copy-start | bytes 2211844
  32.0 18.7 %collective-permute-start.4 = (bf16[180,2048]{1,0:T(8,128)(2,1)S(1)}, bf16[180,2048]{1,0:T(8,128)(2,1)}, u32[]{:S(2)}, u32[]{:S(2)}) collective-permute-start(bf16[180,2048]{1,0:T(8,128)(2,1)S(1)} %collective-permute-done.1.refs_2_), channel_id=1, source_target_pairs={{8,0},{10,2},{12,4},{14,6},{16,8},{18,10},{20,12},{22,14},{9,1},{1... | collective-permute-start | bytes 2211848 | tf_op jit(solution)/shard_map/ppermute | solution.py:363
  41.9 43.4 %collective-permute-start.14 = (bf16[180,2048]{1,0:T(8,128)(2,1)S(1)}, bf16[180,2048]{1,0:T(8,128)(2,1)S(1)}, u32[]{:S(2)}, u32[]{:S(2)}) collective-permute-start(bf16[180,2048]{1,0:T(8,128)(2,1)S(1)} %collective-permute-done.1.refs_2_), channel_id=1, source_target_pairs={{0,4},{2,6},{4,0},{6,2},{8,12},{10,14},{12,8},{14,10},{16,20},{18,... | collective-permute-start | bytes 2211848 | tf_op jit(solution)/shard_map/ppermute | solution.py:356
  47.1 9.9 %collective-permute-start.6 = (bf16[256,512]{1,0:T(8,128)(2,1)S(1)}, bf16[256,512]{1,0:T(8,128)(2,1)S(1)}, u32[]{:S(2)}, u32[]{:S(2)}) collective-permute-start(bf16[256,512]{1,0:T(8,128)(2,1)S(1)} %shard_map.92.refs_5_.refs_9_), channel_id=1, source_target_pairs={{0,2},{2,0},{4,6},{6,4},{8,10},{10,8},{12,14},{14,12},{16,18},{18,... | collective-permute-start | bytes 786440 | tf_op jit(solution)/shard_map/ppermute | solution.py:399
  50.7 11.3 %collective-permute-start.7 = (bf16[256,512]{1,0:T(8,128)(2,1)S(1)}, bf16[256,512]{1,0:T(8,128)(2,1)S(1)}, u32[]{:S(2)}, u32[]{:S(2)}) collective-permute-start(bf16[256,512]{1,0:T(8,128)(2,1)S(1)} %shard_map.93.refs_6_.refs_10_), channel_id=1, source_target_pairs={{0,2},{2,0},{4,6},{6,4},{8,10},{10,8},{12,14},{14,12},{16,18},{18,... | collective-permute-start | bytes 786440 | tf_op jit(solution)/shard_map/ppermute | solution.py:399
  50.7 16.9 %collective-permute-start.8 = (bf16[256,512]{1,0:T(8,128)(2,1)S(1)}, bf16[256,512]{1,0:T(8,128)(2,1)S(1)}, u32[]{:S(2)}, u32[]{:S(2)}) collective-permute-start(bf16[256,512]{1,0:T(8,128)(2,1)S(1)} %shard_map.94.refs_7_.refs_11_), channel_id=1, source_target_pairs={{0,2},{2,0},{4,6},{6,4},{8,10},{10,8},{12,14},{14,12},{16,18},{18,... | collective-permute-start | bytes 786440 | tf_op jit(solution)/shard_map/ppermute | solution.py:399
  57.0 16.2 %collective-permute-start.9 = (bf16[256,512]{1,0:T(8,128)(2,1)S(1)}, bf16[256,512]{1,0:T(8,128)(2,1)S(1)}, u32[]{:S(2)}, u32[]{:S(2)}) collective-permute-start(bf16[256,512]{1,0:T(8,128)(2,1)S(1)} %shard_map.95.refs_8_.refs_12_), channel_id=1, source_target_pairs={{0,2},{2,0},{4,6},{6,4},{8,10},{10,8},{12,14},{14,12},{16,18},{18,... | collective-permute-start | bytes 786440 | tf_op jit(solution)/shard_map/ppermute | solution.py:399
  57.1 0.9 copy-start.14
  57.9 29.8 %collective-permute-start.10 = (bf16[256,512]{1,0:T(8,128)(2,1)S(1)}, bf16[256,512]{1,0:T(8,128)(2,1)S(1)}, u32[]{:S(2)}, u32[]{:S(2)}) collective-permute-start(bf16[256,512]{1,0:T(8,128)(2,1)S(1)} %shard_map.96.refs_9_.refs_13_), channel_id=1, source_target_pairs={{0,2},{2,0},{4,6},{6,4},{8,10},{10,8},{12,14},{14,12},{16,18},{18,... | collective-permute-start | bytes 786440 | tf_op jit(solution)/shard_map/ppermute | solution.py:399
  62.0 27.8 %collective-permute-start.11 = (bf16[256,512]{1,0:T(8,128)(2,1)S(1)}, bf16[256,512]{1,0:T(8,128)(2,1)S(1)}, u32[]{:S(2)}, u32[]{:S(2)}) collective-permute-start(bf16[256,512]{1,0:T(8,128)(2,1)S(1)} %shard_map.97.refs_10_.refs_14_), channel_id=1, source_target_pairs={{0,2},{2,0},{4,6},{6,4},{8,10},{10,8},{12,14},{14,12},{16,18},{18,... | collective-permute-start | bytes 786440 | tf_op jit(solution)/shard_map/ppermute | solution.py:399
  67.6 24.4 %collective-permute-start.12 = (bf16[256,512]{1,0:T(8,128)(2,1)S(1)}, bf16[256,512]{1,0:T(8,128)(2,1)S(1)}, u32[]{:S(2)}, u32[]{:S(2)}) collective-permute-start(bf16[256,512]{1,0:T(8,128)(2,1)S(1)} %shard_map.98.refs_11_.refs_15_), channel_id=1, source_target_pairs={{0,2},{2,0},{4,6},{6,4},{8,10},{10,8},{12,14},{14,12},{16,18},{18,... | collective-permute-start | bytes 786440 | tf_op jit(solution)/shard_map/ppermute | solution.py:399
  73.2 39.1 %collective-permute-start.15 = (bf16[180,2048]{1,0:T(8,128)(2,1)}, bf16[180,2048]{1,0:T(8,128)(2,1)}, u32[]{:S(2)}, u32[]{:S(2)}) collective-permute-start(bf16[180,2048]{1,0:T(8,128)(2,1)} %collective-permute-done.2.refs_3_), channel_id=1, source_target_pairs={{8,12},{10,14},{12,8},{14,10},{16,20},{18,22},{20,16},{22,18},{24,... | collective-permute-start | bytes 2211848 | tf_op jit(solution)/shard_map/ppermute | solution.py:356
  85.3 0.9 copy-start.16
  86.2 26.3 %collective-permute-start.19 = (bf16[180,2048]{1,0:T(8,128)(2,1)}, bf16[180,2048]{1,0:T(8,128)(2,1)}, u32[]{:S(2)}, u32[]{:S(2)}) collective-permute-start(bf16[180,2048]{1,0:T(8,128)(2,1)} %collective-permute-done.4.refs_3_.refs_0_), channel_id=1, source_target_pairs={{8,0},{10,2},{12,4},{14,6},{9,1},{11,3},{13,5},{15,7}} | collective-permute-start | bytes 2211848 | tf_op jit(solution)/shard_map/ppermute | solution.py:363
  87.7 0.7 copy-start
  88.5 24.7 %collective-permute-start.20 = (bf16[180,2048]{1,0:T(8,128)(2,1)}, bf16[180,2048]{1,0:T(8,128)(2,1)}, u32[]{:S(2)}, u32[]{:S(2)}) collective-permute-start(bf16[180,2048]{1,0:T(8,128)(2,1)} %collective-permute-done.3.refs_4_.refs_2_), channel_id=1, source_target_pairs={{16,24},{18,26},{20,28},{22,30},{17,25},{19,27},{21,29},{23,31}} | collective-permute-start | bytes 2211848 | tf_op jit(solution)/shard_map/ppermute | solution.py:363
  90.5 24.6 %collective-permute-start.16 = (bf16[180,2048]{1,0:T(8,128)(2,1)}, bf16[180,2048]{1,0:T(8,128)(2,1)}, u32[]{:S(2)}, u32[]{:S(2)}) collective-permute-start(bf16[180,2048]{1,0:T(8,128)(2,1)} %collective-permute-done.4.refs_3_.refs_0_), channel_id=1, source_target_pairs={{0,4},{2,6},{4,0},{6,2},{8,12},{10,14},{12,8},{14,10},{1,5},{3,7},... | collective-permute-start | bytes 2211848 | tf_op jit(solution)/shard_map/ppermute | solution.py:356
  92.8 24.2 %collective-permute-start.17 = (bf16[180,2048]{1,0:T(8,128)(2,1)}, bf16[180,2048]{1,0:T(8,128)(2,1)}, u32[]{:S(2)}, u32[]{:S(2)}) collective-permute-start(bf16[180,2048]{1,0:T(8,128)(2,1)} %collective-permute-done.3.refs_4_.refs_2_), channel_id=1, source_target_pairs={{16,20},{18,22},{20,16},{22,18},{24,28},{26,30},{28,24},{30,26},{1... | collective-permute-start | bytes 2211848 | tf_op jit(solution)/shard_map/ppermute | solution.py:356
  101.2 1.0 copy-start.1
  102.2 0.9 copy-start.4
  103.1 0.9 copy-start.7
  104.1 1.1 copy-start.11
  105.2 1.1 copy-start.13
  106.3 1.1 copy-start.15
  107.5 9.5 %copy-start.2 = (bf16[256,512]{1,0:T(8,128)(2,1)S(1)}, bf16[256,512]{1,0:T(8,128)(2,1)}, u32[]{:S(2)}) copy-start(bf16[256,512]{1,0:T(8,128)(2,1)} %copy-done) | copy-start | bytes 786436
  107.5 9.5 %copy-start.5 = (bf16[256,512]{1,0:T(8,128)(2,1)S(1)}, bf16[256,512]{1,0:T(8,128)(2,1)}, u32[]{:S(2)}) copy-start(bf16[256,512]{1,0:T(8,128)(2,1)} %copy-done.3) | copy-start | bytes 786436
  107.5 9.5 %copy-start.8 = (bf16[256,512]{1,0:T(8,128)(2,1)S(1)}, bf16[256,512]{1,0:T(8,128)(2,1)}, u32[]{:S(2)}) copy-start(bf16[256,512]{1,0:T(8,128)(2,1)} %copy-done.6) | copy-start | bytes 786436
  107.5 9.5 %copy-start.17 = (bf16[180,2048]{1,0:T(8,128)(2,1)S(1)}, bf16[180,2048]{1,0:T(8,128)(2,1)}, u32[]{:S(2)}) copy-start(bf16[180,2048]{1,0:T(8,128)(2,1)} %copy-done.16) | copy-start | bytes 2211844
  112.4 13.2 %collective-permute-start.13 = (bf16[2,3,180,256]{3,0,2,1:T(2,128)(2,1)S(1)}, bf16[2,3,180,256]{3,0,2,1:T(2,128)(2,1)S(1)}, u32[]{:S(2)}, u32[]{:S(2)}) collective-permute-start(bf16[2,3,180,256]{3,0,2,1:T(2,128)(2,1)S(1)} %copy.10), channel_id=1, source_target_pairs={{0,1},{1,0},{2,3},{3,2},{4,5},{5,4},{6,7},{7,6},{8,9},{9,8},{10,11... | collective-permute-start | bytes 1658888 | tf_op jit(solution)/shard_map/ppermute | solution.py:421
  112.5 14.1 %collective-permute-start.22 = (bf16[180,2048]{1,0:T(8,128)(2,1)}, bf16[180,2048]{1,0:T(8,128)(2,1)S(1)}, u32[]{:S(2)}, u32[]{:S(2)}) collective-permute-start(bf16[180,2048]{1,0:T(8,128)(2,1)} %collective-permute-done.19.refs_1_), channel_id=1, source_target_pairs={{0,4},{2,6},{4,0},{6,2},{1,5},{3,7},{5,1},{7,3}} | collective-permute-start | bytes 2211848 | tf_op jit(solution)/shard_map/ppermute | solution.py:356
  113.2 21.3 %collective-permute-start.23 = (bf16[180,2048]{1,0:T(8,128)(2,1)}, bf16[180,2048]{1,0:T(8,128)(2,1)S(1)}, u32[]{:S(2)}, u32[]{:S(2)}) collective-permute-start(bf16[180,2048]{1,0:T(8,128)(2,1)} %collective-permute-done.20.refs_3_), channel_id=1, source_target_pairs={{24,28},{26,30},{28,24},{30,26},{25,29},{27,31},{29,25},{31,27}} | collective-permute-start | bytes 2211848 | tf_op jit(solution)/shard_map/ppermute | solution.py:356
  122.2 4.2 %collective-permute-start.18 = (bf16[2,3,180,256]{3,0,2,1:T(2,128)(2,1)S(1)}, bf16[2,3,180,256]{3,0,2,1:T(2,128)(2,1)S(1)}, u32[]{:S(2)}, u32[]{:S(2)}) collective-permute-start(bf16[2,3,180,256]{3,0,2,1:T(2,128)(2,1)S(1)} %copy.12), channel_id=1, source_target_pairs={{0,1},{1,0},{2,3},{3,2},{4,5},{5,4},{6,7},{7,6},{8,9},{9,8},{10,11... | collective-permute-start | bytes 1658888 | tf_op jit(solution)/shard_map/ppermute | solution.py:421
  125.0 12.1 %collective-permute-start.21 = (bf16[2,1,180,256]{3,2,1,0:T(8,128)(2,1)S(1)}, bf16[2,1,180,256]{3,2,1,0:T(8,128)(2,1)S(1)}, u32[]{:S(2)}, u32[]{:S(2)}) collective-permute-start(bf16[2,1,180,256]{3,2,1,0:T(8,128)(2,1)S(1)} %get-tuple-element.66), channel_id=1, source_target_pairs={{0,1},{1,0},{2,3},{3,2},{4,5},{5,4},{6,7},{7,6},{8,9},{9,8},{10,11... | collective-permute-start | bytes 552968 | tf_op jit(solution)/shard_map/ppermute | solution.py:421
  125.8 22.6 %collective-permute-start.25 = (bf16[3,180,256]{2,1,0:T(8,128)(2,1)S(1)}, bf16[3,180,256]{2,1,0:T(8,128)(2,1)S(1)}, u32[]{:S(2)}, u32[]{:S(2)}) collective-permute-start(bf16[3,180,256]{2,1,0:T(8,128)(2,1)S(1)} %get-tuple-element.71), channel_id=1, source_target_pairs={{0,2},{2,0},{4,6},{6,4},{8,10},{10,8},{12,14},{14,12},{16,18},{18,... | collective-permute-start | bytes 829448 | tf_op jit(solution)/shard_map/ppermute | solution.py:424
  136.5 2.4 %collective-permute-start.24 = (bf16[2,1,180,256]{3,2,1,0:T(8,128)(2,1)S(1)}, bf16[2,1,180,256]{3,2,1,0:T(8,128)(2,1)S(1)}, u32[]{:S(2)}, u32[]{:S(2)}) collective-permute-start(bf16[2,1,180,256]{3,2,1,0:T(8,128)(2,1)S(1)} %get-tuple-element.69), channel_id=1, source_target_pairs={{0,1},{1,0},{2,3},{3,2},{4,5},{5,4},{6,7},{7,6},{8,9},{9,8},{10,11... | collective-permute-start | bytes 552968 | tf_op jit(solution)/shard_map/ppermute | solution.py:421
  136.7 11.7 %collective-permute-start.26 = (bf16[3,180,256]{2,1,0:T(8,128)(2,1)S(1)}, bf16[3,180,256]{2,1,0:T(8,128)(2,1)S(1)}, u32[]{:S(2)}, u32[]{:S(2)}) collective-permute-start(bf16[3,180,256]{2,1,0:T(8,128)(2,1)S(1)} %get-tuple-element.72), channel_id=1, source_target_pairs={{0,2},{2,0},{4,6},{6,4},{8,10},{10,8},{12,14},{14,12},{16,18},{18,... | collective-permute-start | bytes 829448 | tf_op jit(solution)/shard_map/ppermute | solution.py:424
  137.1 11.3 %collective-permute-start.27 = (bf16[1,180,256]{2,1,0:T(8,128)(2,1)S(1)}, bf16[1,180,256]{2,1,0:T(8,128)(2,1)S(1)}, u32[]{:S(2)}, u32[]{:S(2)}) collective-permute-start(bf16[1,180,256]{2,1,0:T(8,128)(2,1)S(1)} %get-tuple-element.73), channel_id=1, source_target_pairs={{0,2},{2,0},{4,6},{6,4},{8,10},{10,8},{12,14},{14,12},{16,18},{18,... | collective-permute-start | bytes 276488 | tf_op jit(solution)/shard_map/ppermute | solution.py:424
  139.0 11.0 %collective-permute-start.28 = (bf16[1,180,256]{2,1,0:T(8,128)(2,1)S(1)}, bf16[1,180,256]{2,1,0:T(8,128)(2,1)S(1)}, u32[]{:S(2)}, u32[]{:S(2)}) collective-permute-start(bf16[1,180,256]{2,1,0:T(8,128)(2,1)S(1)} %get-tuple-element.74), channel_id=1, source_target_pairs={{0,2},{2,0},{4,6},{6,4},{8,10},{10,8},{12,14},{14,12},{16,18},{18,... | collective-permute-start | bytes 276488 | tf_op jit(solution)/shard_map/ppermute | solution.py:424
  (4 other events, 2.8 us)
where the time goes:
time: 153 us; the launch traced here: 152 us
  Pallas kernels  51.9 us (34%)
  starting transfers between devices  43.6 us (28%)
  waiting for transfers between devices  37.2 us (24%)
  local copies, waits for them, and re-layouts  18 us (12%)
    pallas_call x8, Pallas kernels, attend(): pl.pallas_call(functools.partial(attend_kernel, kv_head, first), out_shap...  34 us
    ppermute x6, starting transfers between devices, forward(): facing[way, step] = lax.ppermute(line[way, step], 'req', hops)  25.4 us
    unnamed x46, local copies, waits for them, and re-layouts  17 us
    pallas_call x4, Pallas kernels, project(): pl.pallas_call(functools.partial(project_kernel, [[p for _, p in candidat...  13.9 us
    ppermute x8, waiting for transfers between devices, per_device(): partner.append(lax.ppermute(chunk, 'req', swap))  13.3 us
    ppermute x4, waiting for transfers between devices, per_device(): other.append(lax.ppermute(given, 'req', swap))  10.6 us
    ppermute x6, waiting for transfers between devices, forward(): facing[way, step] = lax.ppermute(line[way, step], 'req', hops)  9.85 us
    ppermute x6, starting transfers between devices, forward(): line[way, step] = lax.ppermute(line[way, step - 1], 'req', hops)  9.33 us
  transfers between devices with their start and end apart: 29, of which 8 were waited for; matrix products, arithmetic and copies ran while one was open for 1% of the time, Pallas kernels for 33%

commit v1 on v0

v1 whole, which is shorter than its diff:
```python
import functools

import jax
import jax.numpy as jnp
from jax import lax
from jax.experimental import pallas as pl
from jax.experimental.pallas import tpu as pltpu
from jax.sharding import PartitionSpec as P


HEADS = 64
KV_HEADS = 8
HEAD_DIM = 64
TREE = 512
TILE = 128
WIDE = 2 * HEAD_DIM
LOG2_E = 1.4426950408889634
masked_score = -1e30


def product(left, right):
    return jnp.dot(left, right, preferred_element_type=jnp.float32)


def ancestry_kernel(parent_ref, bias_ref, seen):
    tiles = TREE // TILE
    lane = lax.broadcasted_iota(jnp.int32, (TILE, TILE), 1)
    key = lax.broadcasted_iota(jnp.int32, (TILE, TILE), 0)

    def hop(key_tile, row_tile):
        parent = parent_ref[:, row_tile * TILE : (row_tile + 1) * TILE]
        return jnp.broadcast_to(parent, (TILE, TILE)) == key + key_tile * TILE

    inner = [(hop(t, t) | (lane == key)).astype(jnp.bfloat16) for t in range(tiles)]
    reach = 1
    while reach < TILE:
        inner = [jnp.minimum(product(r, r), 1.0).astype(jnp.bfloat16) for r in inner]
        reach *= 2
    seen[...] = jnp.zeros_like(seen)
    for t in range(tiles):
        rows = slice(t * TILE, (t + 1) * TILE)
        if t:
            up = jnp.concatenate([hop(u, t).astype(jnp.bfloat16) for u in range(t)], 0)
            last = product(up, inner[t]).astype(jnp.bfloat16)
            seen[: t * TILE, rows] = product(seen[: t * TILE, : t * TILE], last).astype(jnp.bfloat16)
        seen[rows, rows] = inner[t]
    bias_ref[...] = jnp.where(seen[...].astype(jnp.float32) > 0.5, 0.0, masked_score)


def ancestry(parents):
    return pl.pallas_call(
        ancestry_kernel,
        out_shape=jax.ShapeDtypeStruct((TREE, TREE), jnp.float32),
        in_specs=[pl.BlockSpec(memory_space=pltpu.VMEM)],
        out_specs=pl.BlockSpec(memory_space=pltpu.VMEM),
        scratch_shapes=[pltpu.VMEM((TREE, TREE), jnp.bfloat16)],
        compiler_params=pltpu.CompilerParams(vmem_limit_bytes=8 << 20),
        name="ancestry",
        cost_estimate=pl.CostEstimate(
            flops=80 * TREE**3, bytes_accessed=4 * TREE * TREE, transcendentals=0
        ),
    )(parents)


ONES = 16


def attend_kernel(
    kv_head,
    first,
    live_ref,
    sink_ref,
    query_ref,
    tree_k_ref,
    tree_v_ref,
    cache_k_ref,
    cache_v_ref,
    bias_ref,
    out_ref,
    key_left,
    key_right,
    values,
    score_left,
    score_right,
):
    ctx = cache_k_ref.shape[0]
    pairs = out_ref.shape[0] // WIDE
    factor = LOG2_E * HEAD_DIM**-0.5
    sink_scale = HEAD_DIM**0.5
    near = kv_head % 2
    columns = slice(kv_head // 2 * WIDE, kv_head // 2 * WIDE + WIDE)
    for start, key_src, value_src in (
        (0, cache_k_ref, cache_v_ref),
        (ctx, tree_k_ref, tree_v_ref),
    ):
        rows = key_src.shape[0]
        span = slice(start, start + rows)
        right = lax.broadcasted_iota(jnp.int32, (rows, WIDE), 1) >= HEAD_DIM
        own = right if near else jnp.logical_not(right)
        key = jnp.where(own, key_src[:, columns].astype(jnp.float32), 0.0)
        moved = pltpu.roll(key, HEAD_DIM, 1)
        key_left[span] = (moved if near else key).astype(jnp.bfloat16)
        key_right[span] = (key if near else moved).astype(jnp.bfloat16)
        turned = value_src[:, columns].astype(jnp.float32).T
        values[:HEAD_DIM, span] = turned[near * HEAD_DIM : (near + 1) * HEAD_DIM].astype(jnp.bfloat16)
    values[HEAD_DIM:] = jnp.ones((ONES, values.shape[1]), jnp.bfloat16)
    live = live_ref[0]

    def score(tile, keys, store):
        rows = pl.ds(pl.multiple_of(tile * TILE, TILE), TILE)
        start = first * HEAD_DIM
        query = jnp.concatenate(
            [query_ref[rows, start + p * WIDE : start + (p + 1) * WIDE] for p in range(pairs)], 0
        )
        store[...] = lax.dot_general(
            keys[...], query, (((1,), (1,)), ((), ())), preferred_element_type=jnp.float32
        )

    def mix(tile, side, store):
        rows = pl.ds(pl.multiple_of(tile * TILE, TILE), TILE)
        bias = bias_ref[:, rows]
        bias = jnp.concatenate([bias] * pairs, 1)
        scores = jnp.concatenate([store[:ctx], store[ctx:] + bias], 0)
        sinks = [sink_ref[:, first + 2 * p + side : first + 2 * p + side + 1] for p in range(pairs)]
        sink = jnp.concatenate([jnp.broadcast_to(s, (1, TILE)) for s in sinks], 1) * sink_scale
        peak = jnp.maximum(scores.max(0, keepdims=True), sink)
        probs = jnp.exp2((scores - peak) * factor).astype(jnp.bfloat16)
        sums = product(values[...], probs)
        below = sums[HEAD_DIM : HEAD_DIM + 1] + jnp.exp2((sink - peak) * factor)
        mixed = (sums[:HEAD_DIM] / below).astype(out_ref.dtype)
        for p in range(pairs):
            top = p * WIDE + side * HEAD_DIM
            out_ref[top : top + HEAD_DIM, rows] = mixed[:, p * TILE : (p + 1) * TILE]

    out_ref[...] = jnp.zeros_like(out_ref)
    score(0, key_left, score_left)

    @pl.loop(0, live)
    def tile_step(tile):
        score(tile, key_right, score_right)
        mix(tile, 0, score_left)
        score(jnp.minimum(tile + 1, live - 1), key_left, score_left)
        mix(tile, 1, score_right)


def attend(part, parts, live, sinks, queries, tree_k, tree_v, cache_k, cache_v, bias):
    width = queries.shape[1] // parts
    first = part * width // HEAD_DIM
    kv_head = first // (HEADS // KV_HEADS)
    keys = cache_k.shape[0] + tree_k.shape[0]
    smem = pl.BlockSpec(memory_space=pltpu.SMEM)
    vmem = pl.BlockSpec(memory_space=pltpu.VMEM)
    rows = width // WIDE * TILE
    return pl.pallas_call(
        functools.partial(attend_kernel, kv_head, first),
        out_shape=jax.ShapeDtypeStruct((width, TREE), jnp.bfloat16),
        in_specs=[smem] + [vmem] * 7,
        out_specs=vmem,
        scratch_shapes=[
            pltpu.VMEM((keys, WIDE), jnp.bfloat16),
            pltpu.VMEM((keys, WIDE), jnp.bfloat16),
            pltpu.VMEM((HEAD_DIM + ONES, keys), jnp.bfloat16),
            pltpu.VMEM((keys, rows), jnp.float32),
            pltpu.VMEM((keys, rows), jnp.float32),
        ],
        compiler_params=pltpu.CompilerParams(vmem_limit_bytes=16 << 20),
        cost_estimate=pl.CostEstimate(
            flops=16 * TREE * keys * width, bytes_accessed=3 << 20, transcendentals=0
        ),
    )(live, sinks, queries, tree_k, tree_v, cache_k, cache_v, bias)


def project_kernel(blocks, requests, parts, start, ranks, final, whom_ref, *refs):
    weights, refs = refs[:blocks], refs[blocks:]
    attention, refs = refs[: requests * parts], refs[requests * parts :]
    outs, (held, sems) = refs[:-2], refs[-2:]
    base_ref = None
    if final and start:
        base_ref, *outs = outs
    depth = attention[0].shape[0]
    lanes = slice(start * depth, (start + parts) * depth)
    copies = [
        pltpu.make_async_copy(block.at[:, lanes], held.at[n], sems.at[n])
        for n, block in enumerate(weights)
    ]
    for copy in copies:
        copy.start()
    rank, rows = whom_ref[1], outs[0].shape[-1]
    for n, copy in enumerate(copies):
        copy.wait()
        for which in range(requests):
            for shift, out_ref in enumerate(outs):
                span = slice(None)
                if len(outs) > 1:
                    span = pl.ds(pl.multiple_of((rank + shift) % ranks * rows, rows), rows)
                total = 0.0 if base_ref is None else base_ref[which, n, :, span]
                for part in range(parts):
                    chunk = attention[which * parts + part]
                    block = held[n, :, part * depth : (part + 1) * depth]
                    total = total + product(block, chunk[:, span])
                out_ref[which, n] = total.astype(out_ref.dtype)


def project(whom, ranks, weights, requests, start=0, final=True, base=None):
    columns, width = weights[0].shape
    chunks = [chunk for request in requests for chunk in request]
    parts = len(requests[0])
    rows = TREE // ranks
    cut = final and rows % 128 == 0
    shape = (len(requests), len(weights), columns, rows if cut else TREE)
    kind = jax.ShapeDtypeStruct(shape, jnp.bfloat16 if final else jnp.float32)
    vmem = pl.BlockSpec(memory_space=pltpu.VMEM)
    count = ranks if cut else 1
    bases = [] if base is None else [base]
    outs = pl.pallas_call(
        functools.partial(
            project_kernel, len(weights), len(requests), parts, start, ranks, final
        ),
        out_shape=[kind] * count,
        in_specs=[pl.BlockSpec(memory_space=pltpu.SMEM)]
        + [pl.BlockSpec(memory_space=pl.ANY)] * len(weights)
        + [vmem] * (len(chunks) + len(bases)),
        out_specs=[vmem] * count,
        scratch_shapes=[
            pltpu.VMEM((len(weights), columns, parts * chunks[0].shape[0]), jnp.bfloat16),
            pltpu.SemaphoreType.DMA((len(weights),)),
        ],
        compiler_params=pltpu.CompilerParams(vmem_limit_bytes=20 << 20),
        cost_estimate=pl.CostEstimate(
            flops=4 * len(weights) * columns * chunks[0].shape[0] * len(chunks) * TREE,
            bytes_accessed=2 * len(weights) * columns * (width + 2 * TREE),
            transcendentals=0,
        ),
    )(whom, *weights, *chunks, *bases)
    if cut or not final:
        return list(outs)
    return [
        lax.dynamic_slice_in_dim(outs[0], (whom[1] + shift) % ranks * rows, rows, 3)
        for shift in range(ranks)
    ]


def settle_kernel(count, *refs):
    for which, out_ref in enumerate(refs[count:]):
        total = refs[0][which].astype(jnp.float32)
        for term in refs[1:count]:
            total = total + term[which].astype(jnp.float32)
        out_ref[...] = total.astype(jnp.bfloat16)


def settle(terms):
    vmem = pl.BlockSpec(memory_space=pltpu.VMEM)
    shape = jax.ShapeDtypeStruct(terms[0].shape[1:], jnp.bfloat16)
    requests = terms[0].shape[0]
    return pl.pallas_call(
        functools.partial(settle_kernel, len(terms)),
        out_shape=[shape] * requests,
        in_specs=[vmem] * len(terms),
        out_specs=[vmem] * requests,
        compiler_params=pltpu.CompilerParams(vmem_limit_bytes=16 << 20),
    )(*terms)


def arrange_kernel(whom_ref, slot_ref, *refs):
    parts, (out_ref, held) = refs[:-2], refs[-2:]
    request = whom_ref[0]
    at = 0
    for part in parts:
        held[at : at + part.shape[0]] = part[...]
        at += part.shape[0]
    slots, columns = at // 2, held.shape[1]

    def block(index):
        slot = slot_ref[request * slots + index // 2]
        return held[slot + jnp.where(request % 2 == index % 2, 0, slots)].astype(jnp.float32)

    for pair in range(slots):
        both = jnp.concatenate([block(2 * pair), block(2 * pair + 1)], 0)
        out_ref[2 * pair * columns : 2 * (pair + 1) * columns] = both.astype(out_ref.dtype)


def arrange(whom, slot_of, mine, other):
    vmem = pl.BlockSpec(memory_space=pltpu.VMEM)
    smem = pl.BlockSpec(memory_space=pltpu.SMEM)
    columns, rows = mine[0].shape[1:]
    parts = mine + other
    count = sum(part.shape[0] for part in parts)
    return pl.pallas_call(
        arrange_kernel,
        out_shape=jax.ShapeDtypeStruct((count * columns, rows), jnp.bfloat16),
        in_specs=[smem, smem] + [vmem] * len(parts),
        out_specs=vmem,
        scratch_shapes=[pltpu.VMEM((count, columns, rows), jnp.bfloat16)],
        compiler_params=pltpu.CompilerParams(vmem_limit_bytes=16 << 20),
        name="arrange",
    )(whom, slot_of, *parts)


def exchange(reqs):
    if reqs != 16:
        half = reqs // 2
        return [
            (0, [(i, (i + 2 * shift) % reqs) for i in range(reqs)]) for shift in range(1, half)
        ]
    outer = [(i, i ^ 4) for i in range(reqs)]
    inner = [(i, i ^ 12 if i // 4 in (1, 2) else i ^ 2) for i in range(reqs)]
    return [(0, outer), (0, inner), (1, inner), (2, outer), (3, outer), (4, inner), (5, inner)]


def slots_of(reqs, moves):
    held = [[i] for i in range(reqs)]
    for slot, hops in moves:
        sent = {there: held[here][slot] for here, there in hops}
        for i in range(reqs):
            held[i].append(sent[i])
    return [held[i].index(2 * j + i % 2) for i in range(reqs) for j in range(reqs // 2)]


def timetable(moves, parts):
    plan = {}
    calls = (0, 2, 5)
    for n in range(len(moves)):
        at = calls[n // 2] if n // 2 < len(calls) else parts
        plan.setdefault(min(at, parts), []).append(n)
    return plan


def per_device(
    reqs,
    ranks,
    tree_queries,
    tree_keys,
    tree_values,
    cache_keys,
    cache_values,
    sinks,
    parents,
    tile_counts,
    out_weight,
):
    whom = jnp.stack([lax.axis_index("req"), lax.axis_index("tp")]).astype(jnp.int32)
    swap = [(i, i ^ 1) for i in range(reqs)]
    moves = exchange(reqs)
    slots = [out_weight.T]

    kv_local = cache_keys.shape[2] // HEAD_DIM
    odd = kv_local % 2 * HEAD_DIM
    pad = ((0, 0), (0, odd))
    local = [jnp.pad(a[0], pad) for a in (tree_keys, tree_values, cache_keys, cache_values)]
    own, partner = [], []
    parts = 2 * kv_local
    plan = timetable(moves, parts)
    live = tile_counts
    whom, parents = lax.optimization_barrier((whom, parents))
    for part in range(parts + 1):
        for n in plan.get(part, []):
            slot, hops = moves[n]
            block = slots[slot]
            if 0 < part < parts:
                block, live = lax.optimization_barrier((block, live))
            slots.append(lax.ppermute(block, "req", hops))
        if part == parts:
            break
        if part == 0:
            bias = ancestry(parents)
        chunk = attend(part, parts, live, sinks[None], tree_queries[0], *local, bias)
        live, chunk = lax.optimization_barrier((live, chunk))
        own.append(chunk)
        partner.append(lax.ppermute(chunk, "req", swap))

    def share(terms):
        for shift in range(1, ranks):
            hops = [(r, (r + shift) % ranks) for r in range(ranks)]
            terms[shift] = lax.ppermute(terms[shift], "tp", hops)
        return settle(terms)

    def multiply(weights, requests, **how):
        return project(whom, ranks, weights, requests, **how)

    early, late = slots[:-1], slots[-1:]
    (base,) = multiply(early, [partner[:-1]], final=False)
    last = multiply(early, [partner[-1:]], start=parts - 1, base=base)
    (given,) = share(last)
    other = [lax.ppermute(given, "req", swap)]
    mine = []
    for weights in (early[:2], early[2:]):
        mine += share(multiply(weights, [own]))
    kept, given = share(multiply(late, [own, partner]))
    mine.append(kept)
    other.append(lax.ppermute(given, "req", swap))
    slot_of = jnp.asarray(slots_of(reqs, moves), jnp.int32)
    return arrange(whom, slot_of, mine, other).T[None]


def solution(mesh):
    in_specs = (
        P("req", None, "tp"),
        P("req", None, "tp"),
        P("req", None, "tp"),
        P("req", None, "tp"),
        P("req", None, "tp"),
        P("tp"),
        P("req", None),
        P("req"),
        P("tp", "req"),
    )
    out_specs = P("req", "tp", None)
    return jax.shard_map(
        functools.partial(per_device, mesh.shape["req"], mesh.shape["tp"]),
        mesh=mesh,
        in_specs=in_specs,
        out_specs=out_specs,
        check_vma=False,
    )
```

time: 153 us -> 115 us (0.75)
  the two profiles are of different devices: /device:TPU:28 before, /device:TPU:0 now
where the time goes in v1:
time: 115 us
  Pallas kernels  44.3 us (39%)
  waiting for transfers between devices  43.2 us (38%)
  starting transfers between devices  25.7 us (22%)
    pallas_call x8, Pallas kernels, attend(): pl.pallas_call(functools.partial(attend_kernel, kv_head, first), out_shap...  23.9 us
    ppermute x7, waiting for transfers between devices, per_device(): slots.append(lax.ppermute(block, 'req', hops))  22.6 us
    pallas_call x5, Pallas kernels, project(): pl.pallas_call(functools.partial(project_kernel, len(weights), len(reques...  16.5 us
    ppermute x8, waiting for transfers between devices, per_device(): partner.append(lax.ppermute(chunk, 'req', swap))  16.3 us
    ppermute x7, starting transfers between devices, per_device(): slots.append(lax.ppermute(block, 'req', hops))  11.6 us
    ppermute x8, starting transfers between devices, per_device(): partner.append(lax.ppermute(chunk, 'req', swap))  10.3 us
    ppermute x1, waiting for transfers between devices, per_device(): other.append(lax.ppermute(given, 'req', swap))  2.95 us
  transfers between devices with their start and end apart: 21, of which 10 were waited for; matrix products, arithmetic and copies ran while one was open for 0% of the time, Pallas kernels for 35%

profile of v1, /device:TPU:0, one launch (start us, length us, event | category | flops | bytes accessed | tf_op | source)
XLA Modules:
  0.0 115.0 jit_solution(18212728531197875246)
XLA Ops:
  0.0 3.0 %collective-permute-start.1 = (bf16[180,2048]{1,0:T(8,128)(2,1)}, bf16[180,2048]{1,0:T(8,128)(2,1)S(1)}, u32[]{:S(2)}, u32[]{:S(2)}) collective-permute-start(bf16[180,2048]{1,0:T(8,128)(2,1)} %bitcast.12), channel_id=1, source_target_pairs={{0,4},{2,6},{4,0},{6,2},{8,16},{10,18},{12,20},{14,22},{16,8},{18,... | collective-permute-start | bytes 2211848 | tf_op jit(solution)/shard_map/ppermute | solution.py:361
  3.0 1.6 %collective-permute-start = (bf16[180,2048]{1,0:T(8,128)(2,1)}, bf16[180,2048]{1,0:T(8,128)(2,1)S(1)}, u32[]{:S(2)}, u32[]{:S(2)}) collective-permute-start(bf16[180,2048]{1,0:T(8,128)(2,1)} %bitcast.13), channel_id=1, source_target_pairs={{0,8},{2,10},{4,12},{6,14},{8,0},{10,2},{12,4},{14,6},{16,24},{18,... | collective-permute-start | bytes 2211848 | tf_op jit(solution)/shard_map/ppermute | solution.py:361
  4.6 0.1 pad_add_fusion.whom_ref
  4.7 0.7 copy-done.7
  5.4 1.6 %ancestry.1.bias_ref = f32[512,512]{1,0:T(8,128)S(1)} custom-call(s32[1,512]{1,0:T(1,128)S(1)} %copy-done.7), custom_call_target="tpu_custom_call" | custom-call | flops 10737418240 | bytes 1048576 | tf_op jit(solution)/shard_map/ancestry/pallas_call | solution.py:51
  7.8 2.9 %shard_map.100.refs_2_.refs_5_.refs_1_ = bf16[256,512]{1,0:T(8,128)(2,1)S(1)} custom-call(s32[1]{0:T(128)S(6)} %copy.11.live_ref, f32[1,32]{1,0:T(1,128)S(1)} %bitcast.57, bf16[512,2048]{1,0:T(8,128)(2,1)S(1)} %bitcast.17, bf16[512,256]{1,0:T(8,128)(2,1)S(1)} %bitcast.41, bf16[512,256]{1,0:T(8,128)(2,1)S(1)} %bitcast.49, bf16[1024,256]{1,0:T(8,128)(2,1)S(1)} %bitcast.25, ...), custom_call_target="tpu_custom_call" | custom-call | flops 3221225472 | bytes 3145728 | tf_op jit(solution)/shard_map/pallas_call | solution.py:154
  10.7 2.9 %shard_map.101.refs_3_.refs_6_.refs_2_ = bf16[256,512]{1,0:T(8,128)(2,1)S(1)} custom-call(s32[1]{0:T(128)S(6)} %copy.11.live_ref, f32[1,32]{1,0:T(1,128)S(1)} %bitcast.58, bf16[512,2048]{1,0:T(8,128)(2,1)S(1)} %bitcast.18, bf16[512,256]{1,0:T(8,128)(2,1)S(1)} %bitcast.42, bf16[512,256]{1,0:T(8,128)(2,1)S(1)} %bitcast.50, bf16[1024,256]{1,0:T(8,128)(2,1)S(1)} %bitcast.26, ...), custom_call_target="tpu_custom_call" | custom-call | flops 3221225472 | bytes 3145728 | tf_op jit(solution)/shard_map/pallas_call | solution.py:154
  13.6 1.6 %collective-permute-start.10 = (bf16[256,512]{1,0:T(8,128)(2,1)S(1)}, bf16[256,512]{1,0:T(8,128)(2,1)S(1)}, u32[]{:S(2)}, u32[]{:S(2)}) collective-permute-start(bf16[256,512]{1,0:T(8,128)(2,1)S(1)} %shard_map.101.refs_3_.refs_6_.refs_2_), channel_id=1, source_target_pairs={{0,2},{2,0},{4,6},{6,4},{8,10},{10,8},{12,14},{14,12},{16,18},{18,... | collective-permute-start | bytes 786440 | tf_op jit(solution)/shard_map/ppermute | solution.py:369
  15.2 0.5 collective-permute-start.9
  15.7 5.8 %collective-permute-done.refs_1_ = bf16[180,2048]{1,0:T(8,128)(2,1)S(1)} collective-permute-done((bf16[180,2048]{1,0:T(8,128)(2,1)}, bf16[180,2048]{1,0:T(8,128)(2,1)S(1)}, u32[]{:S(2)}, u32[]{:S(2)}) %collective-permute-start) | collective-permute-done | bytes 737312 | tf_op jit(solution)/shard_map/ppermute | solution.py:361
  21.5 1.6 %collective-permute-start.2 = (bf16[180,2048]{1,0:T(8,128)(2,1)S(1)}, bf16[180,2048]{1,0:T(8,128)(2,1)S(1)}, u32[]{:S(2)}, u32[]{:S(2)}) collective-permute-start(bf16[180,2048]{1,0:T(8,128)(2,1)S(1)} %collective-permute-done.1.refs_0_.refs_2_), channel_id=1, source_target_pairs={{0,8},{2,10},{4,12},{6,14},{8,0},{10,2},{12,4},{14,6},{16,24},{18,... | collective-permute-start | bytes 2211848 | tf_op jit(solution)/shard_map/ppermute | solution.py:361
  23.1 1.5 %collective-permute-start.3 = (bf16[180,2048]{1,0:T(8,128)(2,1)S(1)}, bf16[180,2048]{1,0:T(8,128)(2,1)S(1)}, u32[]{:S(2)}, u32[]{:S(2)}) collective-permute-start(bf16[180,2048]{1,0:T(8,128)(2,1)S(1)} %collective-permute-done.refs_1_), channel_id=1, source_target_pairs={{0,4},{2,6},{4,0},{6,2},{8,16},{10,18},{12,20},{14,22},{16,8},{18,... | collective-permute-start | bytes 2211848 | tf_op jit(solution)/shard_map/ppermute | solution.py:361
  24.7 2.9 %shard_map.104.refs_6_.refs_9_.refs_5_ = bf16[256,512]{1,0:T(8,128)(2,1)S(1)} custom-call(s32[1]{0:T(128)S(6)} %copy.11.live_ref, f32[1,32]{1,0:T(1,128)S(1)} %bitcast.59, bf16[512,2048]{1,0:T(8,128)(2,1)S(1)} %bitcast.19, bf16[512,256]{1,0:T(8,128)(2,1)S(1)} %bitcast.43, bf16[512,256]{1,0:T(8,128)(2,1)S(1)} %bitcast.51, bf16[1024,256]{1,0:T(8,128)(2,1)S(1)} %bitcast.27, ...), custom_call_target="tpu_custom_call" | custom-call | flops 3221225472 | bytes 3145728 | tf_op jit(solution)/shard_map/pallas_call | solution.py:154
  27.6 3.0 %shard_map.103.refs_5_.refs_8_.refs_4_ = bf16[256,512]{1,0:T(8,128)(2,1)S(1)} custom-call(s32[1]{0:T(128)S(6)} %copy.11.live_ref, f32[1,32]{1,0:T(1,128)S(1)} %bitcast.60, bf16[512,2048]{1,0:T(8,128)(2,1)S(1)} %bitcast.20, bf16[512,256]{1,0:T(8,128)(2,1)S(1)} %bitcast.44, bf16[512,256]{1,0:T(8,128)(2,1)S(1)} %bitcast.52, bf16[1024,256]{1,0:T(8,128)(2,1)S(1)} %bitcast.28, ...), custom_call_target="tpu_custom_call" | custom-call | flops 3221225472 | bytes 3145728 | tf_op jit(solution)/shard_map/pallas_call | solution.py:154
  30.6 3.0 %shard_map.102.refs_4_.refs_7_.refs_3_ = bf16[256,512]{1,0:T(8,128)(2,1)S(1)} custom-call(s32[1]{0:T(128)S(6)} %copy.11.live_ref, f32[1,32]{1,0:T(1,128)S(1)} %bitcast.61, bf16[512,2048]{1,0:T(8,128)(2,1)S(1)} %bitcast.21, bf16[512,256]{1,0:T(8,128)(2,1)S(1)} %bitcast.45, bf16[512,256]{1,0:T(8,128)(2,1)S(1)} %bitcast.53, bf16[1024,256]{1,0:T(8,128)(2,1)S(1)} %bitcast.29, ...), custom_call_target="tpu_custom_call" | custom-call | flops 3221225472 | bytes 3145728 | tf_op jit(solution)/shard_map/pallas_call | solution.py:154
  33.6 6.7 %collective-permute-done.3.refs_1_.refs_3_ = bf16[180,2048]{1,0:T(8,128)(2,1)S(1)} collective-permute-done((bf16[180,2048]{1,0:T(8,128)(2,1)S(1)}, bf16[180,2048]{1,0:T(8,128)(2,1)S(1)}, u32[]{:S(2)}, u32[]{:S(2)}) %collective-permute-start.3) | collective-permute-done | bytes 737312 | tf_op jit(solution)/shard_map/ppermute | solution.py:361
  40.3 1.5 %collective-permute-start.6 = (bf16[180,2048]{1,0:T(8,128)(2,1)S(1)}, bf16[180,2048]{1,0:T(8,128)(2,1)S(1)}, u32[]{:S(2)}, u32[]{:S(2)}) collective-permute-start(bf16[180,2048]{1,0:T(8,128)(2,1)S(1)} %collective-permute-done.2.refs_2_.refs_4_), channel_id=1, source_target_pairs={{0,4},{2,6},{4,0},{6,2},{8,16},{10,18},{12,20},{14,22},{16,8},{18,... | collective-permute-start | bytes 2211848 | tf_op jit(solution)/shard_map/ppermute | solution.py:361
  41.8 1.6 %collective-permute-start.5 = (bf16[180,2048]{1,0:T(8,128)(2,1)S(1)}, bf16[180,2048]{1,0:T(8,128)(2,1)S(1)}, u32[]{:S(2)}, u32[]{:S(2)}) collective-permute-start(bf16[180,2048]{1,0:T(8,128)(2,1)S(1)} %collective-permute-done.3.refs_1_.refs_3_), channel_id=1, source_target_pairs={{0,8},{2,10},{4,12},{6,14},{8,0},{10,2},{12,4},{14,6},{16,24},{18,... | collective-permute-start | bytes 2211848 | tf_op jit(solution)/shard_map/ppermute | solution.py:361
  43.4 3.0 %shard_map.106.refs_8_.refs_11_.refs_7_ = bf16[256,512]{1,0:T(8,128)(2,1)S(1)} custom-call(s32[1]{0:T(128)S(6)} %copy.11.live_ref, f32[1,32]{1,0:T(1,128)S(1)} %bitcast.62, bf16[512,2048]{1,0:T(8,128)(2,1)S(1)} %bitcast.22, bf16[512,256]{1,0:T(8,128)(2,1)S(1)} %bitcast.46, bf16[512,256]{1,0:T(8,128)(2,1)S(1)} %bitcast.54, bf16[1024,256]{1,0:T(8,128)(2,1)S(1)} %bitcast.30, ...), custom_call_target="tpu_custom_call" | custom-call | flops 3221225472 | bytes 3145728 | tf_op jit(solution)/shard_map/pallas_call | solution.py:154
  46.4 1.6 %collective-permute-start.13 = (bf16[256,512]{1,0:T(8,128)(2,1)S(1)}, bf16[256,512]{1,0:T(8,128)(2,1)S(1)}, u32[]{:S(2)}, u32[]{:S(2)}) collective-permute-start(bf16[256,512]{1,0:T(8,128)(2,1)S(1)} %shard_map.104.refs_6_.refs_9_.refs_5_), channel_id=1, source_target_pairs={{0,2},{2,0},{4,6},{6,4},{8,10},{10,8},{12,14},{14,12},{16,18},{18,... | collective-permute-start | bytes 786440 | tf_op jit(solution)/shard_map/ppermute | solution.py:369
  48.0 0.5 collective-permute-start.12
  48.5 3.1 %shard_map.105.refs_7_.refs_10_.refs_6_ = bf16[256,512]{1,0:T(8,128)(2,1)S(1)} custom-call(s32[1]{0:T(128)S(6)} %copy.11.live_ref, f32[1,32]{1,0:T(1,128)S(1)} %bitcast.63, bf16[512,2048]{1,0:T(8,128)(2,1)S(1)} %bitcast.23, bf16[512,256]{1,0:T(8,128)(2,1)S(1)} %bitcast.47, bf16[512,256]{1,0:T(8,128)(2,1)S(1)} %bitcast.55, bf16[1024,256]{1,0:T(8,128)(2,1)S(1)} %bitcast.31, ...), custom_call_target="tpu_custom_call" | custom-call | flops 3221225472 | bytes 3145728 | tf_op jit(solution)/shard_map/pallas_call | solution.py:154
  51.6 1.6 %collective-permute-start.11 = (bf16[256,512]{1,0:T(8,128)(2,1)S(1)}, bf16[256,512]{1,0:T(8,128)(2,1)S(1)}, u32[]{:S(2)}, u32[]{:S(2)}) collective-permute-start(bf16[256,512]{1,0:T(8,128)(2,1)S(1)} %shard_map.102.refs_4_.refs_7_.refs_3_), channel_id=1, source_target_pairs={{0,2},{2,0},{4,6},{6,4},{8,10},{10,8},{12,14},{14,12},{16,18},{18,... | collective-permute-start | bytes 786440 | tf_op jit(solution)/shard_map/ppermute | solution.py:369
  53.2 2.5 %collective-permute-done.13.refs_13_.refs_11_ = bf16[256,512]{1,0:T(8,128)(2,1)S(1)} collective-permute-done((bf16[256,512]{1,0:T(8,128)(2,1)S(1)}, bf16[256,512]{1,0:T(8,128)(2,1)S(1)}, u32[]{:S(2)}, u32[]{:S(2)}) %collective-permute-start.13) | collective-permute-done | bytes 262176 | tf_op jit(solution)/shard_map/ppermute | solution.py:369
  55.7 1.5 %collective-permute-start.15 = (bf16[256,512]{1,0:T(8,128)(2,1)S(1)}, bf16[256,512]{1,0:T(8,128)(2,1)S(1)}, u32[]{:S(2)}, u32[]{:S(2)}) collective-permute-start(bf16[256,512]{1,0:T(8,128)(2,1)S(1)} %shard_map.106.refs_8_.refs_11_.refs_7_), channel_id=1, source_target_pairs={{0,2},{2,0},{4,6},{6,4},{8,10},{10,8},{12,14},{14,12},{16,18},{18,... | collective-permute-start | bytes 786440 | tf_op jit(solution)/shard_map/ppermute | solution.py:369
  57.2 4.1 %collective-permute-done.12.refs_12_.refs_10_ = bf16[256,512]{1,0:T(8,128)(2,1)S(1)} collective-permute-done((bf16[256,512]{1,0:T(8,128)(2,1)S(1)}, bf16[256,512]{1,0:T(8,128)(2,1)S(1)}, u32[]{:S(2)}, u32[]{:S(2)}) %collective-permute-start.12) | collective-permute-done | bytes 262176 | tf_op jit(solution)/shard_map/ppermute | solution.py:369
  61.3 1.5 %collective-permute-start.14 = (bf16[256,512]{1,0:T(8,128)(2,1)S(1)}, bf16[256,512]{1,0:T(8,128)(2,1)S(1)}, u32[]{:S(2)}, u32[]{:S(2)}) collective-permute-start(bf16[256,512]{1,0:T(8,128)(2,1)S(1)} %shard_map.105.refs_7_.refs_10_.refs_6_), channel_id=1, source_target_pairs={{0,2},{2,0},{4,6},{6,4},{8,10},{10,8},{12,14},{14,12},{16,18},{18,... | collective-permute-start | bytes 786440 | tf_op jit(solution)/shard_map/ppermute | solution.py:369
  62.8 3.0 %shard_map.107.refs_9_.refs_12_.refs_8_ = bf16[256,512]{1,0:T(8,128)(2,1)S(1)} custom-call(s32[1]{0:T(128)S(6)} %copy.11.live_ref, f32[1,32]{1,0:T(1,128)S(1)} %bitcast.64, bf16[512,2048]{1,0:T(8,128)(2,1)S(1)} %bitcast.24, bf16[512,256]{1,0:T(8,128)(2,1)S(1)} %bitcast.48, bf16[512,256]{1,0:T(8,128)(2,1)S(1)} %bitcast.56, bf16[1024,256]{1,0:T(8,128)(2,1)S(1)} %bitcast.32, ...), custom_call_target="tpu_custom_call" | custom-call | flops 3221225472 | bytes 3145728 | tf_op jit(solution)/shard_map/pallas_call | solution.py:154
  65.8 1.1 collective-permute-done.11.refs_11_.refs_9_
  66.9 1.5 %collective-permute-start.16 = (bf16[256,512]{1,0:T(8,128)(2,1)S(1)}, bf16[256,512]{1,0:T(8,128)(2,1)S(1)}, u32[]{:S(2)}, u32[]{:S(2)}) collective-permute-start(bf16[256,512]{1,0:T(8,128)(2,1)S(1)} %shard_map.107.refs_9_.refs_12_.refs_8_), channel_id=1, source_target_pairs={{0,2},{2,0},{4,6},{6,4},{8,10},{10,8},{12,14},{14,12},{16,18},{18,... | collective-permute-start | bytes 786440 | tf_op jit(solution)/shard_map/ppermute | solution.py:369
  68.4 4.1 %collective-permute-done.15.refs_15_.refs_13_ = bf16[256,512]{1,0:T(8,128)(2,1)S(1)} collective-permute-done((bf16[256,512]{1,0:T(8,128)(2,1)S(1)}, bf16[256,512]{1,0:T(8,128)(2,1)S(1)}, u32[]{:S(2)}, u32[]{:S(2)}) %collective-permute-start.15) | collective-permute-done | bytes 262176 | tf_op jit(solution)/shard_map/ppermute | solution.py:369
  72.5 4.5 %collective-permute-done.14.refs_14_.refs_12_ = bf16[256,512]{1,0:T(8,128)(2,1)S(1)} collective-permute-done((bf16[256,512]{1,0:T(8,128)(2,1)S(1)}, bf16[256,512]{1,0:T(8,128)(2,1)S(1)}, u32[]{:S(2)}, u32[]{:S(2)}) %collective-permute-start.14) | collective-permute-done | bytes 262176 | tf_op jit(solution)/shard_map/ppermute | solution.py:369
  77.0 4.7 %shard_map.114.refs_8_ = f32[1,7,180,512]{3,2,1,0:T(8,128)S(1)} custom-call(s32[2]{0:T(128)S(1)} %pad_add_fusion.whom_ref, bf16[180,2048]{1,0:T(8,128)(2,1)S(1)} %bitcast.14, bf16[180,2048]{1,0:T(8,128)(2,1)S(1)} %collective-permute-done.refs_1_, bf16[180,2048]{1,0:T(8,128)(2,1)S(1)} %collective-permute-done.1.refs_0_.refs_2_, ...), custom_call_target="tpu_custom_call" | custom-call | flops 4624220160 | bytes 7741440 | tf_op jit(solution)/shard_map/pallas_call | solution.py:215
  81.7 2.2 %shard_map.115 = (bf16[1,7,180,256]{3,2,1,0:T(8,128)(2,1)S(1)}, bf16[1,7,180,256]{3,2,1,0:T(8,128)(2,1)S(1)}) custom-call(s32[2]{0:T(128)S(1)} %pad_add_fusion.whom_ref, bf16[180,2048]{1,0:T(8,128)(2,1)S(1)} %bitcast.15, bf16[180,2048]{1,0:T(8,128)(2,1)S(1)} %collective-permute-done.refs_1_, bf16[180,2048]{1,0:T(8,128)(2,1)S(1)} %collective-permute-done.1.refs_0_.refs_2_, ...), custom_call_target="tpu_custom_call" | custom-call | flops 660602880 | bytes 7741440 | tf_op jit(solution)/shard_map/pallas_call | solution.py:215
  83.9 0.1 collective-permute-start.18
  84.0 0.7 collective-permute-start.8
  84.7 1.4 %collective-permute-done.18.refs_1_ = bf16[1,7,180,256]{3,2,1,0:T(8,128)(2,1)S(1)} collective-permute-done((bf16[1,7,180,256]{3,2,1,0:T(8,128)(2,1)S(1)}, bf16[1,7,180,256]{3,2,1,0:T(8,128)(2,1)S(1)}, u32[]{:S(2)}, u32[]{:S(2)}) %collective-permute-start.18) | collective-permute-done | bytes 645152 | tf_op jit(solution)/shard_map/ppermute | solution.py:374
  86.1 0.2 shard_map.116
  86.2 1.6 %collective-permute-start.19 = (bf16[7,180,256]{2,1,0:T(8,128)(2,1)S(1)}, bf16[7,180,256]{2,1,0:T(8,128)(2,1)S(1)}, u32[]{:S(2)}, u32[]{:S(2)}) collective-permute-start(bf16[7,180,256]{2,1,0:T(8,128)(2,1)S(1)} %shard_map.116), channel_id=1, source_target_pairs={{0,2},{2,0},{4,6},{6,4},{8,10},{10,8},{12,14},{14,12},{16,18},{18,... | collective-permute-start | bytes 1935368 | tf_op jit(solution)/shard_map/ppermute | solution.py:384
  87.8 5.2 %shard_map.110 = (bf16[1,5,180,256]{3,2,1,0:T(8,128)(2,1)S(1)}, bf16[1,5,180,256]{3,2,1,0:T(8,128)(2,1)S(1)}) custom-call(s32[2]{0:T(128)S(1)} %pad_add_fusion.whom_ref, bf16[180,2048]{1,0:T(8,128)(2,1)S(1)} %collective-permute-done.1.refs_0_.refs_2_, bf16[180,2048]{1,0:T(8,128)(2,1)S(1)} %collective-permute-done.3.refs_1_.refs_3_, ...), custom_call_target="tpu_custom_call" | custom-call | flops 3774873600 | bytes 5529600 | tf_op jit(solution)/shard_map/pallas_call | solution.py:215
  93.1 10.1 %collective-permute-done.8.refs_0_ = bf16[180,2048]{1,0:T(8,128)(2,1)S(1)} collective-permute-done((bf16[180,2048]{1,0:T(8,128)(2,1)S(1)}, bf16[180,2048]{1,0:T(8,128)(2,1)S(1)}, u32[]{:S(2)}, u32[]{:S(2)}) %collective-permute-start.8) | collective-permute-done | bytes 737312 | tf_op jit(solution)/shard_map/ppermute | solution.py:361
  103.2 2.0 %shard_map.112 = (bf16[2,1,180,256]{3,2,1,0:T(8,128)(2,1)S(1)}, bf16[2,1,180,256]{3,2,1,0:T(8,128)(2,1)S(1)}) custom-call(s32[2]{0:T(128)S(1)} %pad_add_fusion.whom_ref, bf16[180,2048]{1,0:T(8,128)(2,1)S(1)} %collective-permute-done.8.refs_0_, bf16[256,512]{1,0:T(8,128)(2,1)S(1)} %shard_map.100.refs_2_.refs_5_.refs_1_, ...), custom_call_target="tpu_custom_call" | custom-call | flops 1509949440 | bytes 1105920 | tf_op jit(solution)/shard_map/pallas_call | solution.py:215
  105.3 2.4 %shard_map.108 = (bf16[1,2,180,256]{3,2,1,0:T(8,128)(2,1)S(1)}, bf16[1,2,180,256]{3,2,1,0:T(8,128)(2,1)S(1)}) custom-call(s32[2]{0:T(128)S(1)} %pad_add_fusion.whom_ref, bf16[180,2048]{1,0:T(8,128)(2,1)S(1)} %bitcast.16, bf16[180,2048]{1,0:T(8,128)(2,1)S(1)} %collective-permute-done.refs_1_, bf16[256,512]{1,0:T(8,128)(2,1)S(1)} %shard_map.100.refs_2_.refs_5_.refs_1_, ...), custom_call_target="tpu_custom_call" | custom-call | flops 1509949440 | bytes 2211840 | tf_op jit(solution)/shard_map/pallas_call | solution.py:215
  107.7 0.6 collective-permute-start.4
  108.3 1.6 %collective-permute-start.20 = (bf16[1,180,256]{2,1,0:T(8,128)(2,1)S(1)}, bf16[1,180,256]{2,1,0:T(8,128)(2,1)S(1)}, u32[]{:S(2)}, u32[]{:S(2)}) collective-permute-start(bf16[1,180,256]{2,1,0:T(8,128)(2,1)S(1)} %get-tuple-element.74), channel_id=1, source_target_pairs={{0,2},{2,0},{4,6},{6,4},{8,10},{10,8},{12,14},{14,12},{16,18},{18,... | collective-permute-start | bytes 276488 | tf_op jit(solution)/shard_map/ppermute | solution.py:390
  109.9 0.1 shard_map.111.refs_1_
  110.1 2.9 %collective-permute-done.20.refs_4_ = bf16[1,180,256]{2,1,0:T(8,128)(2,1)S(1)} collective-permute-done((bf16[1,180,256]{2,1,0:T(8,128)(2,1)S(1)}, bf16[1,180,256]{2,1,0:T(8,128)(2,1)S(1)}, u32[]{:S(2)}, u32[]{:S(2)}) %collective-permute-start.20) | collective-permute-done | bytes 92192 | tf_op jit(solution)/shard_map/ppermute | solution.py:390
  113.0 1.9 %arrange.1 = bf16[2880,256]{1,0:T(8,128)(2,1)} custom-call(s32[2]{0:T(128)S(1)} %pad_add_fusion.whom_ref, s32[128]{0:T(128)S(1)} %copy-done.1, bf16[2,180,256]{2,1,0:T(8,128)(2,1)S(1)} %shard_map.109.refs_0_, bf16[5,180,256]{2,1,0:T(8,128)(2,1)S(1)} %shard_map.111.refs_1_, bf16[1,180,256]{2,1,0:T(8,128)(2,1)S(1)} %get-tuple-element.71.refs_2_, ...), custom_call_target="tpu_custom_call" | custom-call | tf_op jit(solution)/shard_map/arrange/pallas_call | solution.py:288
  (32 shorter events, 0.3 us)
Async XLA Ops:
  0.0 21.5 %collective-permute-start.1 = (bf16[180,2048]{1,0:T(8,128)(2,1)}, bf16[180,2048]{1,0:T(8,128)(2,1)S(1)}, u32[]{:S(2)}, u32[]{:S(2)}) collective-permute-start(bf16[180,2048]{1,0:T(8,128)(2,1)} %bitcast.12), channel_id=1, source_target_pairs={{0,4},{2,6},{4,0},{6,2},{8,16},{10,18},{12,20},{14,22},{16,8},{18,... | collective-permute-start | bytes 2211848 | tf_op jit(solution)/shard_map/ppermute | solution.py:361
  3.0 18.5 %collective-permute-start = (bf16[180,2048]{1,0:T(8,128)(2,1)}, bf16[180,2048]{1,0:T(8,128)(2,1)S(1)}, u32[]{:S(2)}, u32[]{:S(2)}) collective-permute-start(bf16[180,2048]{1,0:T(8,128)(2,1)} %bitcast.13), channel_id=1, source_target_pairs={{0,8},{2,10},{4,12},{6,14},{8,0},{10,2},{12,4},{14,6},{16,24},{18,... | collective-permute-start | bytes 2211848 | tf_op jit(solution)/shard_map/ppermute | solution.py:361
  4.7 0.7 copy-start.7
  5.4 2.3 %copy-start.2 = (bf16[1,512,2048]{2,1,0:T(8,128)(2,1)S(1)}, bf16[1,512,2048]{2,1,0:T(8,128)(2,1)}, u32[]{:S(2)}) copy-start(bf16[1,512,2048]{2,1,0:T(8,128)(2,1)} %param.10) | copy-start | bytes 6291460
  5.4 2.3 %copy-start.3 = (bf16[1,1024,256]{2,1,0:T(8,128)(2,1)S(1)}, bf16[1,1024,256]{2,1,0:T(8,128)(2,1)}, u32[]{:S(2)}) copy-start(bf16[1,1024,256]{2,1,0:T(8,128)(2,1)} %param.13) | copy-start | bytes 1572868
  5.4 2.3 %copy-start.4 = (bf16[1,1024,256]{2,1,0:T(8,128)(2,1)S(1)}, bf16[1,1024,256]{2,1,0:T(8,128)(2,1)}, u32[]{:S(2)}) copy-start(bf16[1,1024,256]{2,1,0:T(8,128)(2,1)} %param.14) | copy-start | bytes 1572868
  5.4 2.3 %copy-start.5 = (bf16[1,512,256]{2,1,0:T(8,128)(2,1)S(1)}, bf16[1,512,256]{2,1,0:T(8,128)(2,1)}, u32[]{:S(2)}) copy-start(bf16[1,512,256]{2,1,0:T(8,128)(2,1)} %param.11) | copy-start | bytes 786436
  5.4 2.4 %copy-start.6 = (bf16[1,512,256]{2,1,0:T(8,128)(2,1)S(1)}, bf16[1,512,256]{2,1,0:T(8,128)(2,1)}, u32[]{:S(2)}) copy-start(bf16[1,512,256]{2,1,0:T(8,128)(2,1)} %param.12) | copy-start | bytes 786436
  5.4 2.4 %copy-start.8 = (f32[32]{0:T(128)S(1)}, f32[32]{0:T(128)}, u32[]{:S(2)}) copy-start(f32[32]{0:T(128)} %param.15) | copy-start | bytes 388
  13.6 34.3 %collective-permute-start.10 = (bf16[256,512]{1,0:T(8,128)(2,1)S(1)}, bf16[256,512]{1,0:T(8,128)(2,1)S(1)}, u32[]{:S(2)}, u32[]{:S(2)}) collective-permute-start(bf16[256,512]{1,0:T(8,128)(2,1)S(1)} %shard_map.101.refs_3_.refs_6_.refs_2_), channel_id=1, source_target_pairs={{0,2},{2,0},{4,6},{6,4},{8,10},{10,8},{12,14},{14,12},{16,18},{18,... | collective-permute-start | bytes 786440 | tf_op jit(solution)/shard_map/ppermute | solution.py:369
  15.2 36.4 %collective-permute-start.9 = (bf16[256,512]{1,0:T(8,128)(2,1)S(1)}, bf16[256,512]{1,0:T(8,128)(2,1)S(1)}, u32[]{:S(2)}, u32[]{:S(2)}) collective-permute-start(bf16[256,512]{1,0:T(8,128)(2,1)S(1)} %shard_map.100.refs_2_.refs_5_.refs_1_), channel_id=1, source_target_pairs={{0,2},{2,0},{4,6},{6,4},{8,10},{10,8},{12,14},{14,12},{16,18},{18,... | collective-permute-start | bytes 786440 | tf_op jit(solution)/shard_map/ppermute | solution.py:369
  21.5 18.8 %collective-permute-start.2 = (bf16[180,2048]{1,0:T(8,128)(2,1)S(1)}, bf16[180,2048]{1,0:T(8,128)(2,1)S(1)}, u32[]{:S(2)}, u32[]{:S(2)}) collective-permute-start(bf16[180,2048]{1,0:T(8,128)(2,1)S(1)} %collective-permute-done.1.refs_0_.refs_2_), channel_id=1, source_target_pairs={{0,8},{2,10},{4,12},{6,14},{8,0},{10,2},{12,4},{14,6},{16,24},{18,... | collective-permute-start | bytes 2211848 | tf_op jit(solution)/shard_map/ppermute | solution.py:361
  23.1 17.2 %collective-permute-start.3 = (bf16[180,2048]{1,0:T(8,128)(2,1)S(1)}, bf16[180,2048]{1,0:T(8,128)(2,1)S(1)}, u32[]{:S(2)}, u32[]{:S(2)}) collective-permute-start(bf16[180,2048]{1,0:T(8,128)(2,1)S(1)} %collective-permute-done.refs_1_), channel_id=1, source_target_pairs={{0,4},{2,6},{4,0},{6,2},{8,16},{10,18},{12,20},{14,22},{16,8},{18,... | collective-permute-start | bytes 2211848 | tf_op jit(solution)/shard_map/ppermute | solution.py:361
  40.3 36.7 %collective-permute-start.6 = (bf16[180,2048]{1,0:T(8,128)(2,1)S(1)}, bf16[180,2048]{1,0:T(8,128)(2,1)S(1)}, u32[]{:S(2)}, u32[]{:S(2)}) collective-permute-start(bf16[180,2048]{1,0:T(8,128)(2,1)S(1)} %collective-permute-done.2.refs_2_.refs_4_), channel_id=1, source_target_pairs={{0,4},{2,6},{4,0},{6,2},{8,16},{10,18},{12,20},{14,22},{16,8},{18,... | collective-permute-start | bytes 2211848 | tf_op jit(solution)/shard_map/ppermute | solution.py:361
  41.8 35.1 %collective-permute-start.5 = (bf16[180,2048]{1,0:T(8,128)(2,1)S(1)}, bf16[180,2048]{1,0:T(8,128)(2,1)S(1)}, u32[]{:S(2)}, u32[]{:S(2)}) collective-permute-start(bf16[180,2048]{1,0:T(8,128)(2,1)S(1)} %collective-permute-done.3.refs_1_.refs_3_), channel_id=1, source_target_pairs={{0,8},{2,10},{4,12},{6,14},{8,0},{10,2},{12,4},{14,6},{16,24},{18,... | collective-permute-start | bytes 2211848 | tf_op jit(solution)/shard_map/ppermute | solution.py:361
  46.4 9.2 %collective-permute-start.13 = (bf16[256,512]{1,0:T(8,128)(2,1)S(1)}, bf16[256,512]{1,0:T(8,128)(2,1)S(1)}, u32[]{:S(2)}, u32[]{:S(2)}) collective-permute-start(bf16[256,512]{1,0:T(8,128)(2,1)S(1)} %shard_map.104.refs_6_.refs_9_.refs_5_), channel_id=1, source_target_pairs={{0,2},{2,0},{4,6},{6,4},{8,10},{10,8},{12,14},{14,12},{16,18},{18,... | collective-permute-start | bytes 786440 | tf_op jit(solution)/shard_map/ppermute | solution.py:369
  48.0 13.3 %collective-permute-start.12 = (bf16[256,512]{1,0:T(8,128)(2,1)S(1)}, bf16[256,512]{1,0:T(8,128)(2,1)S(1)}, u32[]{:S(2)}, u32[]{:S(2)}) collective-permute-start(bf16[256,512]{1,0:T(8,128)(2,1)S(1)} %shard_map.103.refs_5_.refs_8_.refs_4_), channel_id=1, source_target_pairs={{0,2},{2,0},{4,6},{6,4},{8,10},{10,8},{12,14},{14,12},{16,18},{18,... | collective-permute-start | bytes 786440 | tf_op jit(solution)/shard_map/ppermute | solution.py:369
  51.6 25.4 %copy-start = (bf16[2048,180]{0,1:T(8,128)(2,1)S(1)}, bf16[2048,180]{0,1:T(8,128)(2,1)}, u32[]{:S(2)}) copy-start(bf16[2048,180]{0,1:T(8,128)(2,1)} %param.18) | copy-start | bytes 2211844
  51.6 15.3 %collective-permute-start.11 = (bf16[256,512]{1,0:T(8,128)(2,1)S(1)}, bf16[256,512]{1,0:T(8,128)(2,1)S(1)}, u32[]{:S(2)}, u32[]{:S(2)}) collective-permute-start(bf16[256,512]{1,0:T(8,128)(2,1)S(1)} %shard_map.102.refs_4_.refs_7_.refs_3_), channel_id=1, source_target_pairs={{0,2},{2,0},{4,6},{6,4},{8,10},{10,8},{12,14},{14,12},{16,18},{18,... | collective-permute-start | bytes 786440 | tf_op jit(solution)/shard_map/ppermute | solution.py:369
  55.7 16.9 %collective-permute-start.15 = (bf16[256,512]{1,0:T(8,128)(2,1)S(1)}, bf16[256,512]{1,0:T(8,128)(2,1)S(1)}, u32[]{:S(2)}, u32[]{:S(2)}) collective-permute-start(bf16[256,512]{1,0:T(8,128)(2,1)S(1)} %shard_map.106.refs_8_.refs_11_.refs_7_), channel_id=1, source_target_pairs={{0,2},{2,0},{4,6},{6,4},{8,10},{10,8},{12,14},{14,12},{16,18},{18,... | collective-permute-start | bytes 786440 | tf_op jit(solution)/shard_map/ppermute | solution.py:369
  61.3 15.7 %collective-permute-start.14 = (bf16[256,512]{1,0:T(8,128)(2,1)S(1)}, bf16[256,512]{1,0:T(8,128)(2,1)S(1)}, u32[]{:S(2)}, u32[]{:S(2)}) collective-permute-start(bf16[256,512]{1,0:T(8,128)(2,1)S(1)} %shard_map.105.refs_7_.refs_10_.refs_6_), channel_id=1, source_target_pairs={{0,2},{2,0},{4,6},{6,4},{8,10},{10,8},{12,14},{14,12},{16,18},{18,... | collective-permute-start | bytes 786440 | tf_op jit(solution)/shard_map/ppermute | solution.py:369
  66.9 14.8 %collective-permute-start.16 = (bf16[256,512]{1,0:T(8,128)(2,1)S(1)}, bf16[256,512]{1,0:T(8,128)(2,1)S(1)}, u32[]{:S(2)}, u32[]{:S(2)}) collective-permute-start(bf16[256,512]{1,0:T(8,128)(2,1)S(1)} %shard_map.107.refs_9_.refs_12_.refs_8_), channel_id=1, source_target_pairs={{0,2},{2,0},{4,6},{6,4},{8,10},{10,8},{12,14},{14,12},{16,18},{18,... | collective-permute-start | bytes 786440 | tf_op jit(solution)/shard_map/ppermute | solution.py:369
  83.9 2.2 %collective-permute-start.18 = (bf16[1,7,180,256]{3,2,1,0:T(8,128)(2,1)S(1)}, bf16[1,7,180,256]{3,2,1,0:T(8,128)(2,1)S(1)}, u32[]{:S(2)}, u32[]{:S(2)}) collective-permute-start(bf16[1,7,180,256]{3,2,1,0:T(8,128)(2,1)S(1)} %get-tuple-element.73), channel_id=1, source_target_pairs={{0,1},{1,0},{2,3},{3,2},{4,5},{5,4},{6,7},{7,6},{8,9},{9,8},{10,11... | collective-permute-start | bytes 1935368 | tf_op jit(solution)/shard_map/ppermute | solution.py:374
  84.0 19.2 %collective-permute-start.8 = (bf16[180,2048]{1,0:T(8,128)(2,1)S(1)}, bf16[180,2048]{1,0:T(8,128)(2,1)S(1)}, u32[]{:S(2)}, u32[]{:S(2)}) collective-permute-start(bf16[180,2048]{1,0:T(8,128)(2,1)S(1)} %collective-permute-done.5.refs_3_.refs_5_), channel_id=1, source_target_pairs={{0,4},{2,6},{4,0},{6,2},{8,16},{10,18},{12,20},{14,22},{16,8},{18,... | collective-permute-start | bytes 2211848 | tf_op jit(solution)/shard_map/ppermute | solution.py:361
  86.2 26.8 %collective-permute-start.19 = (bf16[7,180,256]{2,1,0:T(8,128)(2,1)S(1)}, bf16[7,180,256]{2,1,0:T(8,128)(2,1)S(1)}, u32[]{:S(2)}, u32[]{:S(2)}) collective-permute-start(bf16[7,180,256]{2,1,0:T(8,128)(2,1)S(1)} %shard_map.116), channel_id=1, source_target_pairs={{0,2},{2,0},{4,6},{6,4},{8,10},{10,8},{12,14},{14,12},{16,18},{18,... | collective-permute-start | bytes 1935368 | tf_op jit(solution)/shard_map/ppermute | solution.py:384
  93.0 16.9 %collective-permute-start.7 = (bf16[1,5,180,256]{3,2,1,0:T(8,128)(2,1)S(1)}, bf16[1,5,180,256]{3,2,1,0:T(8,128)(2,1)S(1)}, u32[]{:S(2)}, u32[]{:S(2)}) collective-permute-start(bf16[1,5,180,256]{3,2,1,0:T(8,128)(2,1)S(1)} %get-tuple-element.68), channel_id=1, source_target_pairs={{0,1},{1,0},{2,3},{3,2},{4,5},{5,4},{6,7},{7,6},{8,9},{9,8},{10,11... | collective-permute-start | bytes 1382408 | tf_op jit(solution)/shard_map/ppermute | solution.py:374
  105.2 3.1 %collective-permute-start.17 = (bf16[2,1,180,256]{3,2,1,0:T(8,128)(2,1)S(1)}, bf16[2,1,180,256]{3,2,1,0:T(8,128)(2,1)S(1)}, u32[]{:S(2)}, u32[]{:S(2)}) collective-permute-start(bf16[2,1,180,256]{3,2,1,0:T(8,128)(2,1)S(1)} %get-tuple-element.70), channel_id=1, source_target_pairs={{0,1},{1,0},{2,3},{3,2},{4,5},{5,4},{6,7},{7,6},{8,9},{9,8},{10,11... | collective-permute-start | bytes 552968 | tf_op jit(solution)/shard_map/ppermute | solution.py:374
  107.7 5.3 %copy-start.1 = (s32[128]{0:T(128)S(1)}, s32[128]{0:T(128)}, u32[]{:S(2)}) copy-start(s32[128]{0:T(128)} %constant.11.clone.slot_ref) | copy-start | bytes 1540
  107.7 2.2 %collective-permute-start.4 = (bf16[1,2,180,256]{3,2,1,0:T(8,128)(2,1)S(1)}, bf16[1,2,180,256]{3,2,1,0:T(8,128)(2,1)S(1)}, u32[]{:S(2)}, u32[]{:S(2)}) collective-permute-start(bf16[1,2,180,256]{3,2,1,0:T(8,128)(2,1)S(1)} %get-tuple-element.64), channel_id=1, source_target_pairs={{0,1},{1,0},{2,3},{3,2},{4,5},{5,4},{6,7},{7,6},{8,9},{9,8},{10,11... | collective-permute-start | bytes 552968 | tf_op jit(solution)/shard_map/ppermute | solution.py:374
  108.3 4.7 %collective-permute-start.20 = (bf16[1,180,256]{2,1,0:T(8,128)(2,1)S(1)}, bf16[1,180,256]{2,1,0:T(8,128)(2,1)S(1)}, u32[]{:S(2)}, u32[]{:S(2)}) collective-permute-start(bf16[1,180,256]{2,1,0:T(8,128)(2,1)S(1)} %get-tuple-element.74), channel_id=1, source_target_pairs={{0,2},{2,0},{4,6},{6,4},{8,10},{10,8},{12,14},{14,12},{16,18},{18,... | collective-permute-start | bytes 276488 | tf_op jit(solution)/shard_map/ppermute | solution.py:390

commit v2 on v1

--- a/solution.py
+++ b/solution.py
@@ -118,14 +118,24 @@
 
     def mix(tile, side, store):
         rows = pl.ds(pl.multiple_of(tile * TILE, TILE), TILE)
-        bias = bias_ref[:, rows]
-        bias = jnp.concatenate([bias] * pairs, 1)
-        scores = jnp.concatenate([store[:ctx], store[ctx:] + bias], 0)
+        step = 256
+        total_keys = store.shape[0]
+        peak = None
+        for at in range(0, total_keys, step):
+            part = store[at : at + step]
+            if at >= ctx:
+                bias = bias_ref[at - ctx : at - ctx + step, rows]
+                part = part + jnp.concatenate([bias] * pairs, 1)
+                store[at : at + step] = part
+            high = part.max(0, keepdims=True)
+            peak = high if peak is None else jnp.maximum(peak, high)
         sinks = [sink_ref[:, first + 2 * p + side : first + 2 * p + side + 1] for p in range(pairs)]
         sink = jnp.concatenate([jnp.broadcast_to(s, (1, TILE)) for s in sinks], 1) * sink_scale
-        peak = jnp.maximum(scores.max(0, keepdims=True), sink)
-        probs = jnp.exp2((scores - peak) * factor).astype(jnp.bfloat16)
-        sums = product(values[...], probs)
+        peak = jnp.maximum(peak, sink)
+        sums = 0.0
+        for at in range(0, total_keys, step):
+            probs = jnp.exp2((store[at : at + step] - peak) * factor).astype(jnp.bfloat16)
+            sums = sums + product(values[:, at : at + step], probs)
         below = sums[HEAD_DIM : HEAD_DIM + 1] + jnp.exp2((sink - peak) * factor)
         mixed = (sums[:HEAD_DIM] / below).astype(out_ref.dtype)
         for p in range(pairs):
@@ -170,8 +180,8 @@
     )(live, sinks, queries, tree_k, tree_v, cache_k, cache_v, bias)
 
 
-def project_kernel(blocks, requests, parts, start, ranks, final, whom_ref, *refs):
-    weights, refs = refs[:blocks], refs[blocks:]
+def project_kernel(pieces, requests, parts, start, skip, ranks, final, whom_ref, *refs):
+    weights, refs = refs[: sum(pieces)], refs[sum(pieces) :]
     attention, refs = refs[: requests * parts], refs[requests * parts :]
     outs, (held, sems) = refs[:-2], refs[-2:]
     base_ref = None
@@ -179,21 +189,33 @@
         base_ref, *outs = outs
     depth = attention[0].shape[0]
     lanes = slice(start * depth, (start + parts) * depth)
-    copies = [
-        pltpu.make_async_copy(block.at[:, lanes], held.at[n], sems.at[n])
-        for n, block in enumerate(weights)
-    ]
-    for copy in copies:
+    copies = []
+    for n, count in enumerate(pieces):
+        block = weights[sum(pieces[:n]) : sum(pieces[: n + 1])]
+        if count == 1:
+            copies.append([pltpu.make_async_copy(block[0].at[:, lanes], held.at[n], sems.at[n, 0])])
+            continue
+        width = block[0].shape[1]
+        copies.append(
+            [
+                pltpu.make_async_copy(
+                    piece, held.at[n, :, i * width : (i + 1) * width], sems.at[n, i]
+                )
+                for i, piece in enumerate(block)
+            ]
+        )
+    for copy in sum(copies, []):
         copy.start()
     rank, rows = whom_ref[1], outs[0].shape[-1]
-    for n, copy in enumerate(copies):
-        copy.wait()
+    for n, group in enumerate(copies):
+        for copy in group:
+            copy.wait()
         for which in range(requests):
             for shift, out_ref in enumerate(outs):
                 span = slice(None)
                 if len(outs) > 1:
                     span = pl.ds(pl.multiple_of((rank + shift) % ranks * rows, rows), rows)
-                total = 0.0 if base_ref is None else base_ref[which, n, :, span]
+                total = 0.0 if base_ref is None else base_ref[which, skip + n, :, span]
                 for part in range(parts):
                     chunk = attention[which * parts + part]
                     block = held[n, :, part * depth : (part + 1) * depth]
@@ -201,8 +223,11 @@
                 out_ref[which, n] = total.astype(out_ref.dtype)
 
 
-def project(whom, ranks, weights, requests, start=0, final=True, base=None):
-    columns, width = weights[0].shape
+def project(whom, ranks, weights, requests, start=0, final=True, base=None, skip=0):
+    blocks = [block if isinstance(block, tuple) else (block,) for block in weights]
+    pieces = [piece for block in blocks for piece in block]
+    columns = pieces[0].shape[0]
+    width = sum(piece.shape[1] for piece in blocks[0])
     chunks = [chunk for request in requests for chunk in request]
     parts = len(requests[0])
     rows = TREE // ranks
@@ -214,16 +239,23 @@
     bases = [] if base is None else [base]
     outs = pl.pallas_call(
         functools.partial(
-            project_kernel, len(weights), len(requests), parts, start, ranks, final
+            project_kernel,
+            [len(block) for block in blocks],
+            len(requests),
+            parts,
+            start,
+            skip,
+            ranks,
+            final,
         ),
         out_shape=[kind] * count,
         in_specs=[pl.BlockSpec(memory_space=pltpu.SMEM)]
-        + [pl.BlockSpec(memory_space=pl.ANY)] * len(weights)
+        + [pl.BlockSpec(memory_space=pl.ANY)] * len(pieces)
         + [vmem] * (len(chunks) + len(bases)),
         out_specs=[vmem] * count,
         scratch_shapes=[
             pltpu.VMEM((len(weights), columns, parts * chunks[0].shape[0]), jnp.bfloat16),
-            pltpu.SemaphoreType.DMA((len(weights),)),
+            pltpu.SemaphoreType.DMA((len(weights), max(map(len, blocks)))),
         ],
         compiler_params=pltpu.CompilerParams(vmem_limit_bytes=20 << 20),
         cost_estimate=pl.CostEstimate(
@@ -231,13 +263,36 @@
             bytes_accessed=2 * len(weights) * columns * (width + 2 * TREE),
             transcendentals=0,
         ),
-    )(whom, *weights, *chunks, *bases)
+    )(whom, *pieces, *chunks, *bases)
     if cut or not final:
         return list(outs)
     return [
         lax.dynamic_slice_in_dim(outs[0], (whom[1] + shift) % ranks * rows, rows, 3)
         for shift in range(ranks)
     ]
+
+
+def halve_kernel(low_ref, high_ref, low_half, high_half, sems):
+    width = low_half.shape[1]
+    low = pltpu.make_async_copy(low_ref.at[:, :width], low_half, sems.at[0])
+    high = pltpu.make_async_copy(high_ref.at[:, width:], high_half, sems.at[1])
+    low.start()
+    high.start()
+    low.wait()
+    high.wait()
+
+
+def halve(low, high):
+    half = jax.ShapeDtypeStruct((low.shape[0], low.shape[1] // 2), low.dtype)
+    return pl.pallas_call(
+        halve_kernel,
+        out_shape=[half] * 2,
+        in_specs=[pl.BlockSpec(memory_space=pl.ANY)] * 2,
+        out_specs=[pl.BlockSpec(memory_space=pltpu.VMEM)] * 2,
+        scratch_shapes=[pltpu.SemaphoreType.DMA((2,))],
+        compiler_params=pltpu.CompilerParams(vmem_limit_bytes=8 << 20),
+        name="halve",
+    )(low, high)
 
 
 def settle_kernel(count, *refs):
@@ -304,12 +359,22 @@
         ]
     outer = [(i, i ^ 4) for i in range(reqs)]
     inner = [(i, i ^ 12 if i // 4 in (1, 2) else i ^ 2) for i in range(reqs)]
-    return [(0, outer), (0, inner), (1, inner), (2, outer), (3, outer), (4, inner), (5, inner)]
+    return [
+        (0, outer),
+        (0, inner),
+        (1, inner),
+        (2, outer),
+        (3, outer),
+        (4, inner),
+        ((5, 6), (inner, outer)),
+    ]
 
 
 def slots_of(reqs, moves):
     held = [[i] for i in range(reqs)]
     for slot, hops in moves:
+        if isinstance(slot, tuple):
+            slot, hops = slot[0], hops[0]
         sent = {there: held[here][slot] for here, there in hops}
         for i in range(reqs):
             held[i].append(sent[i])
@@ -318,10 +383,10 @@
 
 def timetable(moves, parts):
     plan = {}
-    calls = (0, 2, 5)
+    calls = (0, 3, 6)
     for n in range(len(moves)):
-        at = calls[n // 2] if n // 2 < len(calls) else parts
-        plan.setdefault(min(at, parts), []).append(n)
+        at = calls[n // 2] if n // 2 < len(calls) else parts + 1
+        plan.setdefault(min(at, parts + 1), []).append(n)
     return plan
 
 
@@ -356,7 +421,7 @@
         for n in plan.get(part, []):
             slot, hops = moves[n]
             block = slots[slot]
-            if 0 < part < parts:
+            if part:
                 block, live = lax.optimization_barrier((block, live))
             slots.append(lax.ppermute(block, "req", hops))
         if part == parts:
@@ -377,17 +442,29 @@
     def multiply(weights, requests, **how):
         return project(whom, ranks, weights, requests, **how)
 
-    early, late = slots[:-1], slots[-1:]
+    early = slots[:5]
     (base,) = multiply(early, [partner[:-1]], final=False)
-    last = multiply(early, [partner[-1:]], start=parts - 1, base=base)
-    (given,) = share(last)
-    other = [lax.ppermute(given, "req", swap)]
-    mine = []
-    for weights in (early[:2], early[2:]):
-        mine += share(multiply(weights, [own]))
-    kept, given = share(multiply(late, [own, partner]))
-    mine.append(kept)
-    other.append(lax.ppermute(given, "req", swap))
+    for n in plan.get(parts + 1, []):
+        slot, hops = moves[n]
+        if isinstance(slot, tuple):
+            low, high, base = lax.optimization_barrier((slots[slot[0]], slots[slot[1]], base))
+            halves = halve(low, high)
+            halves = [lax.ppermute(h, "req", hop) for h, hop in zip(halves, hops)]
+            slots.append(tuple(halves))
+            continue
+        block, base = lax.optimization_barrier((slots[slot], base))
+        slots.append(lax.ppermute(block, "req", hops))
+    mine, other = [], []
+    for span in (slice(0, 2), slice(2, None)):
+        ready = multiply(early[span], [partner[-1:]], start=parts - 1, base=base, skip=span.start)
+        (given,) = share(ready)
+        other.append(lax.ppermute(given, "req", swap))
+    for late in (slots[len(early) : -1], slots[-1:]):
+        kept, given = share(multiply(late, [own, partner]))
+        mine.append(kept)
+        other.append(lax.ppermute(given, "req", swap))
+    owned = [*share(multiply(early[:2], [own])), *share(multiply(early[2:], [own]))]
+    mine = owned + mine
     slot_of = jnp.asarray(slots_of(reqs, moves), jnp.int32)
     return arrange(whom, slot_of, mine, other).T[None]
 

time: 115 us -> 111 us (0.965)
  waiting for transfers between devices: 43.2 us -> 32.8 us
  starting transfers between devices: 25.7 us -> 31.9 us
    ppermute x7 -> x6, waiting for transfers between devices: 22.6 us -> 7.1 us  [per_device(): slots.append(lax.ppermute(block, 'req', hops))]
    ppermute x1 -> x4, waiting for transfers between devices: 2.95 us -> 14.2 us  [per_device(): other.append(lax.ppermute(given, 'req', swap))]
    ppermute x8, waiting for transfers between devices: 16.3 us -> 11.6 us  [per_device(): partner.append(lax.ppermute(chunk, 'req', swap))]
    ppermute x1 -> x4, starting transfers between devices: 1.57 us -> 4.31 us  [per_device(): other.append(lax.ppermute(given, 'req', swap))]
    ppermute x4 -> x6, waiting for transfers between devices: 1.41 us -> 0.02 us  [share(): terms[shift] = lax.ppermute(terms[shift], 'tp', hops)]
    ppermute x7 -> x6, starting transfers between devices: 11.6 us -> 12.7 us  [per_device(): slots.append(lax.ppermute(block, 'req', hops))]
    ppermute x1 -> x2, starting transfers between devices: 1.57 us -> 2.56 us  [per_device(): halves = [lax.ppermute(h, 'req', hop) for h, hop in zip(halves, hops)]]
    pallas_call x5 -> x8, Pallas kernels: 16.5 us -> 16.7 us  [the longest x7 16.6 us: project(): pl.pallas_call(functools.partial(project_kernel, [len(block) for block in...]
  transfers between devices with their start and end apart: 21 -> 26, of which waited for: 10 -> 9; matrix products, arithmetic and copies ran while one was open for 0% -> 0% of each run, Pallas kernels for 35% -> 38%
where the time goes in v2:
time: 111 us
  Pallas kernels  44.1 us (40%)
  waiting for transfers between devices  32.8 us (30%)
  starting transfers between devices  31.9 us (29%)
    pallas_call x8, Pallas kernels, attend(): pl.pallas_call(functools.partial(attend_kernel, kv_head, first), out_shap...  23.5 us
    pallas_call x7, Pallas kernels, project(): pl.pallas_call(functools.partial(project_kernel, [len(block) for block in...  16.6 us
    ppermute x4, waiting for transfers between devices, per_device(): other.append(lax.ppermute(given, 'req', swap))  14.2 us
    ppermute x6, starting transfers between devices, per_device(): slots.append(lax.ppermute(block, 'req', hops))  12.7 us
    ppermute x8, waiting for transfers between devices, per_device(): partner.append(lax.ppermute(chunk, 'req', swap))  11.6 us
    ppermute x8, starting transfers between devices, per_device(): partner.append(lax.ppermute(chunk, 'req', swap))  10.4 us
    ppermute x6, waiting for transfers between devices, per_device(): slots.append(lax.ppermute(block, 'req', hops))  7.1 us
    ppermute x4, starting transfers between devices, per_device(): other.append(lax.ppermute(given, 'req', swap))  4.31 us
  transfers between devices with their start and end apart: 26, of which 9 were waited for; matrix products, arithmetic and copies ran while one was open for 0% of the time, Pallas kernels for 38%

profile of v2, /device:TPU:0, one launch (start us, length us, event | category | flops | bytes accessed | tf_op | source)
XLA Modules:
  0.0 110.6 jit_solution(9356007131797891636)
XLA Ops:
  0.0 3.1 %collective-permute-start = (bf16[180,2048]{1,0:T(8,128)(2,1)}, bf16[180,2048]{1,0:T(8,128)(2,1)S(1)}, u32[]{:S(2)}, u32[]{:S(2)}) collective-permute-start(bf16[180,2048]{1,0:T(8,128)(2,1)} %bitcast.12), channel_id=1, source_target_pairs={{0,8},{2,10},{4,12},{6,14},{8,0},{10,2},{12,4},{14,6},{16,24},{18,... | collective-permute-start | bytes 2211848 | tf_op jit(solution)/shard_map/ppermute | solution.py:426
  3.1 1.5 %collective-permute-start.1 = (bf16[180,2048]{1,0:T(8,128)(2,1)}, bf16[180,2048]{1,0:T(8,128)(2,1)S(1)}, u32[]{:S(2)}, u32[]{:S(2)}) collective-permute-start(bf16[180,2048]{1,0:T(8,128)(2,1)} %bitcast.13), channel_id=1, source_target_pairs={{0,4},{2,6},{4,0},{6,2},{8,16},{10,18},{12,20},{14,22},{16,8},{18,... | collective-permute-start | bytes 2211848 | tf_op jit(solution)/shard_map/ppermute | solution.py:426
  4.7 0.7 copy-done.7
  5.4 1.6 %ancestry.1.bias_ref = f32[512,512]{1,0:T(8,128)S(1)} custom-call(s32[1,512]{1,0:T(1,128)S(1)} %copy-done.7), custom_call_target="tpu_custom_call" | custom-call | flops 10737418240 | bytes 1048576 | tf_op jit(solution)/shard_map/ancestry/pallas_call | solution.py:51
  7.7 2.9 %shard_map.100.refs_2_.refs_3_ = bf16[256,512]{1,0:T(8,128)(2,1)S(1)} custom-call(s32[1]{0:T(128)S(6)} %copy.11.live_ref, f32[1,32]{1,0:T(1,128)S(1)} %bitcast.57, bf16[512,2048]{1,0:T(8,128)(2,1)S(1)} %bitcast.17, bf16[512,256]{1,0:T(8,128)(2,1)S(1)} %bitcast.41, bf16[512,256]{1,0:T(8,128)(2,1)S(1)} %bitcast.49, bf16[1024,256]{1,0:T(8,128)(2,1)S(1)} %bitcast.25, ...), custom_call_target="tpu_custom_call" | custom-call | flops 3221225472 | bytes 3145728 | tf_op jit(solution)/shard_map/pallas_call | solution.py:164
  10.6 2.9 %shard_map.101.refs_3_.refs_4_ = bf16[256,512]{1,0:T(8,128)(2,1)S(1)} custom-call(s32[1]{0:T(128)S(6)} %copy.11.live_ref, f32[1,32]{1,0:T(1,128)S(1)} %bitcast.58, bf16[512,2048]{1,0:T(8,128)(2,1)S(1)} %bitcast.18, bf16[512,256]{1,0:T(8,128)(2,1)S(1)} %bitcast.42, bf16[512,256]{1,0:T(8,128)(2,1)S(1)} %bitcast.50, bf16[1024,256]{1,0:T(8,128)(2,1)S(1)} %bitcast.26, ...), custom_call_target="tpu_custom_call" | custom-call | flops 3221225472 | bytes 3145728 | tf_op jit(solution)/shard_map/pallas_call | solution.py:164
  13.5 3.0 %shard_map.102.refs_4_.refs_5_ = bf16[256,512]{1,0:T(8,128)(2,1)S(1)} custom-call(s32[1]{0:T(128)S(6)} %copy.11.live_ref, f32[1,32]{1,0:T(1,128)S(1)} %bitcast.59, bf16[512,2048]{1,0:T(8,128)(2,1)S(1)} %bitcast.19, bf16[512,256]{1,0:T(8,128)(2,1)S(1)} %bitcast.43, bf16[512,256]{1,0:T(8,128)(2,1)S(1)} %bitcast.51, bf16[1024,256]{1,0:T(8,128)(2,1)S(1)} %bitcast.27, ...), custom_call_target="tpu_custom_call" | custom-call | flops 3221225472 | bytes 3145728 | tf_op jit(solution)/shard_map/pallas_call | solution.py:164
  16.4 1.6 %collective-permute-start.10 = (bf16[256,512]{1,0:T(8,128)(2,1)S(1)}, bf16[256,512]{1,0:T(8,128)(2,1)S(1)}, u32[]{:S(2)}, u32[]{:S(2)}) collective-permute-start(bf16[256,512]{1,0:T(8,128)(2,1)S(1)} %shard_map.102.refs_4_.refs_5_), channel_id=1, source_target_pairs={{0,2},{2,0},{4,6},{6,4},{8,10},{10,8},{12,14},{14,12},{16,18},{18,... | collective-permute-start | bytes 786440 | tf_op jit(solution)/shard_map/ppermute | solution.py:434
  18.0 0.5 collective-permute-start.9
  18.5 1.5 %collective-permute-start.8 = (bf16[256,512]{1,0:T(8,128)(2,1)S(1)}, bf16[256,512]{1,0:T(8,128)(2,1)S(1)}, u32[]{:S(2)}, u32[]{:S(2)}) collective-permute-start(bf16[256,512]{1,0:T(8,128)(2,1)S(1)} %shard_map.100.refs_2_.refs_3_), channel_id=1, source_target_pairs={{0,2},{2,0},{4,6},{6,4},{8,10},{10,8},{12,14},{14,12},{16,18},{18,... | collective-permute-start | bytes 786440 | tf_op jit(solution)/shard_map/ppermute | solution.py:434
  20.1 1.5 %collective-permute-done.1.refs_0_.refs_2_ = bf16[180,2048]{1,0:T(8,128)(2,1)S(1)} collective-permute-done((bf16[180,2048]{1,0:T(8,128)(2,1)}, bf16[180,2048]{1,0:T(8,128)(2,1)S(1)}, u32[]{:S(2)}, u32[]{:S(2)}) %collective-permute-start.1) | collective-permute-done | bytes 737312 | tf_op jit(solution)/shard_map/ppermute | solution.py:426
  21.6 1.5 %collective-permute-start.3 = (bf16[180,2048]{1,0:T(8,128)(2,1)S(1)}, bf16[180,2048]{1,0:T(8,128)(2,1)S(1)}, u32[]{:S(2)}, u32[]{:S(2)}) collective-permute-start(bf16[180,2048]{1,0:T(8,128)(2,1)S(1)} %collective-permute-done.refs_1_), channel_id=1, source_target_pairs={{0,4},{2,6},{4,0},{6,2},{8,16},{10,18},{12,20},{14,22},{16,8},{18,... | collective-permute-start | bytes 2211848 | tf_op jit(solution)/shard_map/ppermute | solution.py:426
  23.1 1.6 %collective-permute-start.2 = (bf16[180,2048]{1,0:T(8,128)(2,1)S(1)}, bf16[180,2048]{1,0:T(8,128)(2,1)S(1)}, u32[]{:S(2)}, u32[]{:S(2)}) collective-permute-start(bf16[180,2048]{1,0:T(8,128)(2,1)S(1)} %collective-permute-done.1.refs_0_.refs_2_), channel_id=1, source_target_pairs={{0,8},{2,10},{4,12},{6,14},{8,0},{10,2},{12,4},{14,6},{16,24},{18,... | collective-permute-start | bytes 2211848 | tf_op jit(solution)/shard_map/ppermute | solution.py:426
  24.7 2.9 %shard_map.103.refs_5_.refs_6_ = bf16[256,512]{1,0:T(8,128)(2,1)S(1)} custom-call(s32[1]{0:T(128)S(6)} %copy.11.live_ref, f32[1,32]{1,0:T(1,128)S(1)} %bitcast.60, bf16[512,2048]{1,0:T(8,128)(2,1)S(1)} %bitcast.20, bf16[512,256]{1,0:T(8,128)(2,1)S(1)} %bitcast.44, bf16[512,256]{1,0:T(8,128)(2,1)S(1)} %bitcast.52, bf16[1024,256]{1,0:T(8,128)(2,1)S(1)} %bitcast.28, ...), custom_call_target="tpu_custom_call" | custom-call | flops 3221225472 | bytes 3145728 | tf_op jit(solution)/shard_map/pallas_call | solution.py:164
  27.7 2.9 %shard_map.104.refs_6_.refs_7_ = bf16[256,512]{1,0:T(8,128)(2,1)S(1)} custom-call(s32[1]{0:T(128)S(6)} %copy.11.live_ref, f32[1,32]{1,0:T(1,128)S(1)} %bitcast.61, bf16[512,2048]{1,0:T(8,128)(2,1)S(1)} %bitcast.21, bf16[512,256]{1,0:T(8,128)(2,1)S(1)} %bitcast.45, bf16[512,256]{1,0:T(8,128)(2,1)S(1)} %bitcast.53, bf16[1024,256]{1,0:T(8,128)(2,1)S(1)} %bitcast.29, ...), custom_call_target="tpu_custom_call" | custom-call | flops 3221225472 | bytes 3145728 | tf_op jit(solution)/shard_map/pallas_call | solution.py:164
  30.6 2.9 %shard_map.105.refs_7_.refs_8_ = bf16[256,512]{1,0:T(8,128)(2,1)S(1)} custom-call(s32[1]{0:T(128)S(6)} %copy.11.live_ref, f32[1,32]{1,0:T(1,128)S(1)} %bitcast.62, bf16[512,2048]{1,0:T(8,128)(2,1)S(1)} %bitcast.22, bf16[512,256]{1,0:T(8,128)(2,1)S(1)} %bitcast.46, bf16[512,256]{1,0:T(8,128)(2,1)S(1)} %bitcast.54, bf16[1024,256]{1,0:T(8,128)(2,1)S(1)} %bitcast.30, ...), custom_call_target="tpu_custom_call" | custom-call | flops 3221225472 | bytes 3145728 | tf_op jit(solution)/shard_map/pallas_call | solution.py:164
  33.4 5.6 %collective-permute-done.3.refs_1_.refs_3_ = bf16[180,2048]{1,0:T(8,128)(2,1)S(1)} collective-permute-done((bf16[180,2048]{1,0:T(8,128)(2,1)S(1)}, bf16[180,2048]{1,0:T(8,128)(2,1)S(1)}, u32[]{:S(2)}, u32[]{:S(2)}) %collective-permute-start.3) | collective-permute-done | bytes 737312 | tf_op jit(solution)/shard_map/ppermute | solution.py:426
  39.0 1.5 %collective-permute-start.13 = (bf16[256,512]{1,0:T(8,128)(2,1)S(1)}, bf16[256,512]{1,0:T(8,128)(2,1)S(1)}, u32[]{:S(2)}, u32[]{:S(2)}) collective-permute-start(bf16[256,512]{1,0:T(8,128)(2,1)S(1)} %shard_map.105.refs_7_.refs_8_), channel_id=1, source_target_pairs={{0,2},{2,0},{4,6},{6,4},{8,10},{10,8},{12,14},{14,12},{16,18},{18,... | collective-permute-start | bytes 786440 | tf_op jit(solution)/shard_map/ppermute | solution.py:434
  40.5 1.5 %collective-permute-start.7 = (bf16[180,2048]{1,0:T(8,128)(2,1)S(1)}, bf16[180,2048]{1,0:T(8,128)(2,1)S(1)}, u32[]{:S(2)}, u32[]{:S(2)}) collective-permute-start(bf16[180,2048]{1,0:T(8,128)(2,1)S(1)} %collective-permute-done.2.refs_2_.refs_4_), channel_id=1, source_target_pairs={{0,4},{2,6},{4,0},{6,2},{8,16},{10,18},{12,20},{14,22},{16,8},{18,... | collective-permute-start | bytes 2211848 | tf_op jit(solution)/shard_map/ppermute | solution.py:426
  42.0 3.4 %collective-permute-start.6 = (bf16[180,2048]{1,0:T(8,128)(2,1)S(1)}, bf16[180,2048]{1,0:T(8,128)(2,1)S(1)}, u32[]{:S(2)}, u32[]{:S(2)}) collective-permute-start(bf16[180,2048]{1,0:T(8,128)(2,1)S(1)} %collective-permute-done.3.refs_1_.refs_3_), channel_id=1, source_target_pairs={{0,8},{2,10},{4,12},{6,14},{8,0},{10,2},{12,4},{14,6},{16,24},{18,... | collective-permute-start | bytes 2211848 | tf_op jit(solution)/shard_map/ppermute | solution.py:426
  45.5 3.1 %shard_map.106.refs_8_.refs_9_ = bf16[256,512]{1,0:T(8,128)(2,1)S(1)} custom-call(s32[1]{0:T(128)S(6)} %copy.11.live_ref, f32[1,32]{1,0:T(1,128)S(1)} %bitcast.63, bf16[512,2048]{1,0:T(8,128)(2,1)S(1)} %bitcast.23, bf16[512,256]{1,0:T(8,128)(2,1)S(1)} %bitcast.47, bf16[512,256]{1,0:T(8,128)(2,1)S(1)} %bitcast.55, bf16[1024,256]{1,0:T(8,128)(2,1)S(1)} %bitcast.31, ...), custom_call_target="tpu_custom_call" | custom-call | flops 3221225472 | bytes 3145728 | tf_op jit(solution)/shard_map/pallas_call | solution.py:164
  48.6 1.7 %collective-permute-start.12 = (bf16[256,512]{1,0:T(8,128)(2,1)S(1)}, bf16[256,512]{1,0:T(8,128)(2,1)S(1)}, u32[]{:S(2)}, u32[]{:S(2)}) collective-permute-start(bf16[256,512]{1,0:T(8,128)(2,1)S(1)} %shard_map.104.refs_6_.refs_7_), channel_id=1, source_target_pairs={{0,2},{2,0},{4,6},{6,4},{8,10},{10,8},{12,14},{14,12},{16,18},{18,... | collective-permute-start | bytes 786440 | tf_op jit(solution)/shard_map/ppermute | solution.py:434
  50.3 0.4 collective-permute-start.11
  50.7 1.6 %collective-permute-start.14 = (bf16[256,512]{1,0:T(8,128)(2,1)S(1)}, bf16[256,512]{1,0:T(8,128)(2,1)S(1)}, u32[]{:S(2)}, u32[]{:S(2)}) collective-permute-start(bf16[256,512]{1,0:T(8,128)(2,1)S(1)} %shard_map.106.refs_8_.refs_9_), channel_id=1, source_target_pairs={{0,2},{2,0},{4,6},{6,4},{8,10},{10,8},{12,14},{14,12},{16,18},{18,... | collective-permute-start | bytes 786440 | tf_op jit(solution)/shard_map/ppermute | solution.py:434
  52.4 3.0 %shard_map.107.refs_9_.refs_10_ = bf16[256,512]{1,0:T(8,128)(2,1)S(1)} custom-call(s32[1]{0:T(128)S(6)} %copy.11.live_ref, f32[1,32]{1,0:T(1,128)S(1)} %bitcast.64, bf16[512,2048]{1,0:T(8,128)(2,1)S(1)} %bitcast.24, bf16[512,256]{1,0:T(8,128)(2,1)S(1)} %bitcast.48, bf16[512,256]{1,0:T(8,128)(2,1)S(1)} %bitcast.56, bf16[1024,256]{1,0:T(8,128)(2,1)S(1)} %bitcast.32, ...), custom_call_target="tpu_custom_call" | custom-call | flops 3221225472 | bytes 3145728 | tf_op jit(solution)/shard_map/pallas_call | solution.py:164
  55.3 2.5 %collective-permute-done.12.refs_14_.refs_9_ = bf16[256,512]{1,0:T(8,128)(2,1)S(1)} collective-permute-done((bf16[256,512]{1,0:T(8,128)(2,1)S(1)}, bf16[256,512]{1,0:T(8,128)(2,1)S(1)}, u32[]{:S(2)}, u32[]{:S(2)}) %collective-permute-start.12) | collective-permute-done | bytes 262176 | tf_op jit(solution)/shard_map/ppermute | solution.py:434
  57.9 1.6 %collective-permute-start.15 = (bf16[256,512]{1,0:T(8,128)(2,1)S(1)}, bf16[256,512]{1,0:T(8,128)(2,1)S(1)}, u32[]{:S(2)}, u32[]{:S(2)}) collective-permute-start(bf16[256,512]{1,0:T(8,128)(2,1)S(1)} %shard_map.107.refs_9_.refs_10_), channel_id=1, source_target_pairs={{0,2},{2,0},{4,6},{6,4},{8,10},{10,8},{12,14},{14,12},{16,18},{18,... | collective-permute-start | bytes 786440 | tf_op jit(solution)/shard_map/ppermute | solution.py:434
  59.5 4.0 %collective-permute-done.11.refs_13_.refs_8_ = bf16[256,512]{1,0:T(8,128)(2,1)S(1)} collective-permute-done((bf16[256,512]{1,0:T(8,128)(2,1)S(1)}, bf16[256,512]{1,0:T(8,128)(2,1)S(1)}, u32[]{:S(2)}, u32[]{:S(2)}) %collective-permute-start.11) | collective-permute-done | bytes 262176 | tf_op jit(solution)/shard_map/ppermute | solution.py:434
  63.5 5.0 %collective-permute-done.14.refs_16_.refs_11_ = bf16[256,512]{1,0:T(8,128)(2,1)S(1)} collective-permute-done((bf16[256,512]{1,0:T(8,128)(2,1)S(1)}, bf16[256,512]{1,0:T(8,128)(2,1)S(1)}, u32[]{:S(2)}, u32[]{:S(2)}) %collective-permute-start.14) | collective-permute-done | bytes 262176 | tf_op jit(solution)/shard_map/ppermute | solution.py:434
  68.5 3.5 %shard_map.114.refs_3_.refs_4_ = f32[1,5,180,512]{3,2,1,0:T(8,128)S(1)} custom-call(s32[2]{0:T(128)S(1)} %pad_add_fusion.whom_ref, bf16[180,2048]{1,0:T(8,128)(2,1)S(1)} %bitcast.14, bf16[180,2048]{1,0:T(8,128)(2,1)S(1)} %collective-permute-done.refs_1_, bf16[180,2048]{1,0:T(8,128)(2,1)S(1)} %collective-permute-done.1.refs_0_.refs_2_, ...), custom_call_target="tpu_custom_call" | custom-call | flops 3303014400 | bytes 5529600 | tf_op jit(solution)/shard_map/pallas_call | solution.py:240
  72.1 1.4 %collective-permute-start.17 = (bf16[180,1024]{1,0:T(8,128)(2,1)S(1)}, bf16[180,1024]{1,0:T(8,128)(2,1)S(1)}, u32[]{:S(2)}, u32[]{:S(2)}) collective-permute-start(bf16[180,1024]{1,0:T(8,128)(2,1)S(1)} %get-tuple-element.85), channel_id=1, source_target_pairs={{0,4},{2,6},{4,0},{6,2},{8,16},{10,18},{12,20},{14,22},{16,8},{18,... | collective-permute-start | bytes 1105928 | tf_op jit(solution)/shard_map/ppermute | solution.py:452
  73.6 1.1 %collective-permute-start.18 = (bf16[180,1024]{1,0:T(8,128)(2,1)S(1)}, bf16[180,1024]{1,0:T(8,128)(2,1)S(1)}, u32[]{:S(2)}, u32[]{:S(2)}) collective-permute-start(bf16[180,1024]{1,0:T(8,128)(2,1)S(1)} %get-tuple-element.86), channel_id=1, source_target_pairs={{0,8},{2,10},{4,12},{6,14},{8,0},{10,2},{12,4},{14,6},{16,24},{18,... | collective-permute-start | bytes 1105928 | tf_op jit(solution)/shard_map/ppermute | solution.py:452
  74.7 3.4 %shard_map.110 = (bf16[1,3,180,256]{3,2,1,0:T(8,128)(2,1)S(1)}, bf16[1,3,180,256]{3,2,1,0:T(8,128)(2,1)S(1)}) custom-call(s32[2]{0:T(128)S(1)} %pad_add_fusion.whom_ref, bf16[180,2048]{1,0:T(8,128)(2,1)S(1)} %collective-permute-done.1.refs_0_.refs_2_, bf16[180,2048]{1,0:T(8,128)(2,1)S(1)} %collective-permute-done.3.refs_1_.refs_3_, ...), custom_call_target="tpu_custom_call" | custom-call | flops 2264924160 | bytes 3317760 | tf_op jit(solution)/shard_map/pallas_call | solution.py:240
  78.1 1.3 %shard_map.119 = (bf16[1,3,180,256]{3,2,1,0:T(8,128)(2,1)S(1)}, bf16[1,3,180,256]{3,2,1,0:T(8,128)(2,1)S(1)}) custom-call(s32[2]{0:T(128)S(1)} %pad_add_fusion.whom_ref, bf16[180,2048]{1,0:T(8,128)(2,1)S(1)} %collective-permute-done.1.refs_0_.refs_2_, bf16[180,2048]{1,0:T(8,128)(2,1)S(1)} %collective-permute-done.3.refs_1_.refs_3_, ...), custom_call_target="tpu_custom_call" | custom-call | flops 283115520 | bytes 3317760 | tf_op jit(solution)/shard_map/pallas_call | solution.py:240
  79.4 0.6 collective-permute-start.22
  80.0 1.0 shard_map.117
  81.1 3.4 %shard_map.112 = (bf16[2,2,180,256]{3,2,1,0:T(8,128)(2,1)S(1)}, bf16[2,2,180,256]{3,2,1,0:T(8,128)(2,1)S(1)}) custom-call(s32[2]{0:T(128)S(1)} %pad_add_fusion.whom_ref, bf16[180,2048]{1,0:T(8,128)(2,1)S(1)} %collective-permute-done.6.refs_0_.low_ref, bf16[180,2048]{1,0:T(8,128)(2,1)S(1)} %collective-permute-done.7.refs_1_.high_ref, ...), custom_call_target="tpu_custom_call" | custom-call | flops 3019898880 | bytes 2211840 | tf_op jit(solution)/shard_map/pallas_call | solution.py:240
  84.5 0.5 collective-permute-start.16
  85.0 1.6 %shard_map.115 = (bf16[2,1,180,256]{3,2,1,0:T(8,128)(2,1)S(1)}, bf16[2,1,180,256]{3,2,1,0:T(8,128)(2,1)S(1)}) custom-call(s32[2]{0:T(128)S(1)} %pad_add_fusion.whom_ref, bf16[180,1024]{1,0:T(8,128)(2,1)S(1)} %collective-permute-done.17.refs_0_, bf16[180,1024]{1,0:T(8,128)(2,1)S(1)} %collective-permute-done.18.refs_1_, ...), custom_call_target="tpu_custom_call" | custom-call | flops 1509949440 | bytes 1105920 | tf_op jit(solution)/shard_map/pallas_call | solution.py:240
  86.8 2.4 %shard_map.108 = (bf16[1,2,180,256]{3,2,1,0:T(8,128)(2,1)S(1)}, bf16[1,2,180,256]{3,2,1,0:T(8,128)(2,1)S(1)}) custom-call(s32[2]{0:T(128)S(1)} %pad_add_fusion.whom_ref, bf16[180,2048]{1,0:T(8,128)(2,1)S(1)} %bitcast.16, bf16[180,2048]{1,0:T(8,128)(2,1)S(1)} %collective-permute-done.refs_1_, bf16[256,512]{1,0:T(8,128)(2,1)S(1)} %shard_map.100.refs_2_.refs_3_, ...), custom_call_target="tpu_custom_call" | custom-call | flops 1509949440 | bytes 2211840 | tf_op jit(solution)/shard_map/pallas_call | solution.py:240
  89.2 0.5 collective-permute-start.4
  89.8 1.8 %collective-permute-start.23 = (bf16[3,180,256]{2,1,0:T(8,128)(2,1)S(1)}, bf16[3,180,256]{2,1,0:T(8,128)(2,1)S(1)}, u32[]{:S(2)}, u32[]{:S(2)}) collective-permute-start(bf16[3,180,256]{2,1,0:T(8,128)(2,1)S(1)} %shard_map.120), channel_id=1, source_target_pairs={{0,2},{2,0},{4,6},{6,4},{8,10},{10,8},{12,14},{14,12},{16,18},{18,... | collective-permute-start | bytes 829448 | tf_op jit(solution)/shard_map/ppermute | solution.py:461
  91.7 0.3 collective-permute-start.21
  92.2 1.8 %collective-permute-start.24 = (bf16[2,180,256]{2,1,0:T(8,128)(2,1)S(1)}, bf16[2,180,256]{2,1,0:T(8,128)(2,1)S(1)}, u32[]{:S(2)}, u32[]{:S(2)}) collective-permute-start(bf16[2,180,256]{2,1,0:T(8,128)(2,1)S(1)} %get-tuple-element.95), channel_id=1, source_target_pairs={{0,2},{2,0},{4,6},{6,4},{8,10},{10,8},{12,14},{14,12},{16,18},{18,... | collective-permute-start | bytes 552968 | tf_op jit(solution)/shard_map/ppermute | solution.py:465
  94.5 9.0 %collective-permute-done.21.refs_4_ = bf16[2,180,256]{2,1,0:T(8,128)(2,1)S(1)} collective-permute-done((bf16[2,180,256]{2,1,0:T(8,128)(2,1)S(1)}, bf16[2,180,256]{2,1,0:T(8,128)(2,1)S(1)}, u32[]{:S(2)}, u32[]{:S(2)}) %collective-permute-start.21) | collective-permute-done | bytes 184352 | tf_op jit(solution)/shard_map/ppermute | solution.py:461
  103.6 4.0 %collective-permute-done.24.refs_6_ = bf16[2,180,256]{2,1,0:T(8,128)(2,1)S(1)} collective-permute-done((bf16[2,180,256]{2,1,0:T(8,128)(2,1)S(1)}, bf16[2,180,256]{2,1,0:T(8,128)(2,1)S(1)}, u32[]{:S(2)}, u32[]{:S(2)}) %collective-permute-start.24) | collective-permute-done | bytes 184352 | tf_op jit(solution)/shard_map/ppermute | solution.py:465
  107.6 1.1 collective-permute-done.25.refs_7_
  108.7 1.9 %arrange.1 = bf16[2880,256]{1,0:T(8,128)(2,1)} custom-call(s32[2]{0:T(128)S(1)} %pad_add_fusion.whom_ref, s32[128]{0:T(128)S(1)} %copy-done.1, bf16[2,180,256]{2,1,0:T(8,128)(2,1)S(1)} %shard_map.109.refs_0_, bf16[3,180,256]{2,1,0:T(8,128)(2,1)S(1)} %shard_map.111.refs_1_, bf16[2,180,256]{2,1,0:T(8,128)(2,1)S(1)} %get-tuple-element.82.refs_2_, ...), custom_call_target="tpu_custom_call" | custom-call | tf_op jit(solution)/shard_map/arrange/pallas_call | solution.py:343
  (47 shorter events, 1.3 us)
Async XLA Ops:
  0.0 20.1 %collective-permute-start = (bf16[180,2048]{1,0:T(8,128)(2,1)}, bf16[180,2048]{1,0:T(8,128)(2,1)S(1)}, u32[]{:S(2)}, u32[]{:S(2)}) collective-permute-start(bf16[180,2048]{1,0:T(8,128)(2,1)} %bitcast.12), channel_id=1, source_target_pairs={{0,8},{2,10},{4,12},{6,14},{8,0},{10,2},{12,4},{14,6},{16,24},{18,... | collective-permute-start | bytes 2211848 | tf_op jit(solution)/shard_map/ppermute | solution.py:426
  3.1 18.5 %collective-permute-start.1 = (bf16[180,2048]{1,0:T(8,128)(2,1)}, bf16[180,2048]{1,0:T(8,128)(2,1)S(1)}, u32[]{:S(2)}, u32[]{:S(2)}) collective-permute-start(bf16[180,2048]{1,0:T(8,128)(2,1)} %bitcast.13), channel_id=1, source_target_pairs={{0,4},{2,6},{4,0},{6,2},{8,16},{10,18},{12,20},{14,22},{16,8},{18,... | collective-permute-start | bytes 2211848 | tf_op jit(solution)/shard_map/ppermute | solution.py:426
  4.6 0.7 copy-start.7
  5.3 2.3 %copy-start.2 = (bf16[1,512,2048]{2,1,0:T(8,128)(2,1)S(1)}, bf16[1,512,2048]{2,1,0:T(8,128)(2,1)}, u32[]{:S(2)}) copy-start(bf16[1,512,2048]{2,1,0:T(8,128)(2,1)} %param.10) | copy-start | bytes 6291460
  5.3 2.3 %copy-start.3 = (bf16[1,1024,256]{2,1,0:T(8,128)(2,1)S(1)}, bf16[1,1024,256]{2,1,0:T(8,128)(2,1)}, u32[]{:S(2)}) copy-start(bf16[1,1024,256]{2,1,0:T(8,128)(2,1)} %param.13) | copy-start | bytes 1572868
  5.3 2.3 %copy-start.4 = (bf16[1,1024,256]{2,1,0:T(8,128)(2,1)S(1)}, bf16[1,1024,256]{2,1,0:T(8,128)(2,1)}, u32[]{:S(2)}) copy-start(bf16[1,1024,256]{2,1,0:T(8,128)(2,1)} %param.14) | copy-start | bytes 1572868
  5.3 2.3 %copy-start.5 = (bf16[1,512,256]{2,1,0:T(8,128)(2,1)S(1)}, bf16[1,512,256]{2,1,0:T(8,128)(2,1)}, u32[]{:S(2)}) copy-start(bf16[1,512,256]{2,1,0:T(8,128)(2,1)} %param.11) | copy-start | bytes 786436
  5.3 2.4 %copy-start.6 = (bf16[1,512,256]{2,1,0:T(8,128)(2,1)S(1)}, bf16[1,512,256]{2,1,0:T(8,128)(2,1)}, u32[]{:S(2)}) copy-start(bf16[1,512,256]{2,1,0:T(8,128)(2,1)} %param.12) | copy-start | bytes 786436
  5.4 2.4 %copy-start.8 = (f32[32]{0:T(128)S(1)}, f32[32]{0:T(128)}, u32[]{:S(2)}) copy-start(f32[32]{0:T(128)} %param.15) | copy-start | bytes 388
  16.4 25.6 %collective-permute-start.10 = (bf16[256,512]{1,0:T(8,128)(2,1)S(1)}, bf16[256,512]{1,0:T(8,128)(2,1)S(1)}, u32[]{:S(2)}, u32[]{:S(2)}) collective-permute-start(bf16[256,512]{1,0:T(8,128)(2,1)S(1)} %shard_map.102.refs_4_.refs_5_), channel_id=1, source_target_pairs={{0,2},{2,0},{4,6},{6,4},{8,10},{10,8},{12,14},{14,12},{16,18},{18,... | collective-permute-start | bytes 786440 | tf_op jit(solution)/shard_map/ppermute | solution.py:434
  18.0 30.6 %collective-permute-start.9 = (bf16[256,512]{1,0:T(8,128)(2,1)S(1)}, bf16[256,512]{1,0:T(8,128)(2,1)S(1)}, u32[]{:S(2)}, u32[]{:S(2)}) collective-permute-start(bf16[256,512]{1,0:T(8,128)(2,1)S(1)} %shard_map.101.refs_3_.refs_4_), channel_id=1, source_target_pairs={{0,2},{2,0},{4,6},{6,4},{8,10},{10,8},{12,14},{14,12},{16,18},{18,... | collective-permute-start | bytes 786440 | tf_op jit(solution)/shard_map/ppermute | solution.py:434
  18.5 31.8 %collective-permute-start.8 = (bf16[256,512]{1,0:T(8,128)(2,1)S(1)}, bf16[256,512]{1,0:T(8,128)(2,1)S(1)}, u32[]{:S(2)}, u32[]{:S(2)}) collective-permute-start(bf16[256,512]{1,0:T(8,128)(2,1)S(1)} %shard_map.100.refs_2_.refs_3_), channel_id=1, source_target_pairs={{0,2},{2,0},{4,6},{6,4},{8,10},{10,8},{12,14},{14,12},{16,18},{18,... | collective-permute-start | bytes 786440 | tf_op jit(solution)/shard_map/ppermute | solution.py:434
  21.6 17.4 %collective-permute-start.3 = (bf16[180,2048]{1,0:T(8,128)(2,1)S(1)}, bf16[180,2048]{1,0:T(8,128)(2,1)S(1)}, u32[]{:S(2)}, u32[]{:S(2)}) collective-permute-start(bf16[180,2048]{1,0:T(8,128)(2,1)S(1)} %collective-permute-done.refs_1_), channel_id=1, source_target_pairs={{0,4},{2,6},{4,0},{6,2},{8,16},{10,18},{12,20},{14,22},{16,8},{18,... | collective-permute-start | bytes 2211848 | tf_op jit(solution)/shard_map/ppermute | solution.py:426
  23.1 17.4 %collective-permute-start.2 = (bf16[180,2048]{1,0:T(8,128)(2,1)S(1)}, bf16[180,2048]{1,0:T(8,128)(2,1)S(1)}, u32[]{:S(2)}, u32[]{:S(2)}) collective-permute-start(bf16[180,2048]{1,0:T(8,128)(2,1)S(1)} %collective-permute-done.1.refs_0_.refs_2_), channel_id=1, source_target_pairs={{0,8},{2,10},{4,12},{6,14},{8,0},{10,2},{12,4},{14,6},{16,24},{18,... | collective-permute-start | bytes 2211848 | tf_op jit(solution)/shard_map/ppermute | solution.py:426
  39.0 11.7 %collective-permute-start.13 = (bf16[256,512]{1,0:T(8,128)(2,1)S(1)}, bf16[256,512]{1,0:T(8,128)(2,1)S(1)}, u32[]{:S(2)}, u32[]{:S(2)}) collective-permute-start(bf16[256,512]{1,0:T(8,128)(2,1)S(1)} %shard_map.105.refs_7_.refs_8_), channel_id=1, source_target_pairs={{0,2},{2,0},{4,6},{6,4},{8,10},{10,8},{12,14},{14,12},{16,18},{18,... | collective-permute-start | bytes 786440 | tf_op jit(solution)/shard_map/ppermute | solution.py:434
  40.5 31.5 %collective-permute-start.7 = (bf16[180,2048]{1,0:T(8,128)(2,1)S(1)}, bf16[180,2048]{1,0:T(8,128)(2,1)S(1)}, u32[]{:S(2)}, u32[]{:S(2)}) collective-permute-start(bf16[180,2048]{1,0:T(8,128)(2,1)S(1)} %collective-permute-done.2.refs_2_.refs_4_), channel_id=1, source_target_pairs={{0,4},{2,6},{4,0},{6,2},{8,16},{10,18},{12,20},{14,22},{16,8},{18,... | collective-permute-start | bytes 2211848 | tf_op jit(solution)/shard_map/ppermute | solution.py:426
  42.0 30.0 %collective-permute-start.6 = (bf16[180,2048]{1,0:T(8,128)(2,1)S(1)}, bf16[180,2048]{1,0:T(8,128)(2,1)S(1)}, u32[]{:S(2)}, u32[]{:S(2)}) collective-permute-start(bf16[180,2048]{1,0:T(8,128)(2,1)S(1)} %collective-permute-done.3.refs_1_.refs_3_), channel_id=1, source_target_pairs={{0,8},{2,10},{4,12},{6,14},{8,0},{10,2},{12,4},{14,6},{16,24},{18,... | collective-permute-start | bytes 2211848 | tf_op jit(solution)/shard_map/ppermute | solution.py:426
  48.6 19.9 %copy-start = (bf16[2048,180]{0,1:T(8,128)(2,1)S(1)}, bf16[2048,180]{0,1:T(8,128)(2,1)}, u32[]{:S(2)}) copy-start(bf16[2048,180]{0,1:T(8,128)(2,1)} %param.18) | copy-start | bytes 2211844
  48.6 9.2 %collective-permute-start.12 = (bf16[256,512]{1,0:T(8,128)(2,1)S(1)}, bf16[256,512]{1,0:T(8,128)(2,1)S(1)}, u32[]{:S(2)}, u32[]{:S(2)}) collective-permute-start(bf16[256,512]{1,0:T(8,128)(2,1)S(1)} %shard_map.104.refs_6_.refs_7_), channel_id=1, source_target_pairs={{0,2},{2,0},{4,6},{6,4},{8,10},{10,8},{12,14},{14,12},{16,18},{18,... | collective-permute-start | bytes 786440 | tf_op jit(solution)/shard_map/ppermute | solution.py:434
  50.3 13.1 %collective-permute-start.11 = (bf16[256,512]{1,0:T(8,128)(2,1)S(1)}, bf16[256,512]{1,0:T(8,128)(2,1)S(1)}, u32[]{:S(2)}, u32[]{:S(2)}) collective-permute-start(bf16[256,512]{1,0:T(8,128)(2,1)S(1)} %shard_map.103.refs_5_.refs_6_), channel_id=1, source_target_pairs={{0,2},{2,0},{4,6},{6,4},{8,10},{10,8},{12,14},{14,12},{16,18},{18,... | collective-permute-start | bytes 786440 | tf_op jit(solution)/shard_map/ppermute | solution.py:434
  50.7 17.8 %collective-permute-start.14 = (bf16[256,512]{1,0:T(8,128)(2,1)S(1)}, bf16[256,512]{1,0:T(8,128)(2,1)S(1)}, u32[]{:S(2)}, u32[]{:S(2)}) collective-permute-start(bf16[256,512]{1,0:T(8,128)(2,1)S(1)} %shard_map.106.refs_8_.refs_9_), channel_id=1, source_target_pairs={{0,2},{2,0},{4,6},{6,4},{8,10},{10,8},{12,14},{14,12},{16,18},{18,... | collective-permute-start | bytes 786440 | tf_op jit(solution)/shard_map/ppermute | solution.py:434
  57.9 20.3 %collective-permute-start.15 = (bf16[256,512]{1,0:T(8,128)(2,1)S(1)}, bf16[256,512]{1,0:T(8,128)(2,1)S(1)}, u32[]{:S(2)}, u32[]{:S(2)}) collective-permute-start(bf16[256,512]{1,0:T(8,128)(2,1)S(1)} %shard_map.107.refs_9_.refs_10_), channel_id=1, source_target_pairs={{0,2},{2,0},{4,6},{6,4},{8,10},{10,8},{12,14},{14,12},{16,18},{18,... | collective-permute-start | bytes 786440 | tf_op jit(solution)/shard_map/ppermute | solution.py:434
  72.1 12.4 %collective-permute-start.17 = (bf16[180,1024]{1,0:T(8,128)(2,1)S(1)}, bf16[180,1024]{1,0:T(8,128)(2,1)S(1)}, u32[]{:S(2)}, u32[]{:S(2)}) collective-permute-start(bf16[180,1024]{1,0:T(8,128)(2,1)S(1)} %get-tuple-element.85), channel_id=1, source_target_pairs={{0,4},{2,6},{4,0},{6,2},{8,16},{10,18},{12,20},{14,22},{16,8},{18,... | collective-permute-start | bytes 1105928 | tf_op jit(solution)/shard_map/ppermute | solution.py:452
  73.6 11.5 %collective-permute-start.18 = (bf16[180,1024]{1,0:T(8,128)(2,1)S(1)}, bf16[180,1024]{1,0:T(8,128)(2,1)S(1)}, u32[]{:S(2)}, u32[]{:S(2)}) collective-permute-start(bf16[180,1024]{1,0:T(8,128)(2,1)S(1)} %get-tuple-element.86), channel_id=1, source_target_pairs={{0,8},{2,10},{4,12},{6,14},{8,0},{10,2},{12,4},{14,6},{16,24},{18,... | collective-permute-start | bytes 1105928 | tf_op jit(solution)/shard_map/ppermute | solution.py:452
  78.0 16.4 %collective-permute-start.5 = (bf16[1,3,180,256]{3,2,1,0:T(8,128)(2,1)S(1)}, bf16[1,3,180,256]{3,2,1,0:T(8,128)(2,1)S(1)}, u32[]{:S(2)}, u32[]{:S(2)}) collective-permute-start(bf16[1,3,180,256]{3,2,1,0:T(8,128)(2,1)S(1)} %get-tuple-element.77), channel_id=1, source_target_pairs={{0,1},{1,0},{2,3},{3,2},{4,5},{5,4},{6,7},{7,6},{8,9},{9,8},{10,11... | collective-permute-start | bytes 829448 | tf_op jit(solution)/shard_map/ppermute | solution.py:439
  79.4 9.8 %collective-permute-start.22 = (bf16[1,3,180,256]{3,2,1,0:T(8,128)(2,1)S(1)}, bf16[1,3,180,256]{3,2,1,0:T(8,128)(2,1)S(1)}, u32[]{:S(2)}, u32[]{:S(2)}) collective-permute-start(bf16[1,3,180,256]{3,2,1,0:T(8,128)(2,1)S(1)} %get-tuple-element.94), channel_id=1, source_target_pairs={{0,1},{1,0},{2,3},{3,2},{4,5},{5,4},{6,7},{7,6},{8,9},{9,8},{10,11... | collective-permute-start | bytes 829448 | tf_op jit(solution)/shard_map/ppermute | solution.py:439
  81.0 8.8 %collective-permute-start.20 = (bf16[1,2,180,256]{3,2,1,0:T(8,128)(2,1)S(1)}, bf16[1,2,180,256]{3,2,1,0:T(8,128)(2,1)S(1)}, u32[]{:S(2)}, u32[]{:S(2)}) collective-permute-start(bf16[1,2,180,256]{3,2,1,0:T(8,128)(2,1)S(1)} %get-tuple-element.92), channel_id=1, source_target_pairs={{0,1},{1,0},{2,3},{3,2},{4,5},{5,4},{6,7},{7,6},{8,9},{9,8},{10,11... | collective-permute-start | bytes 552968 | tf_op jit(solution)/shard_map/ppermute | solution.py:439
  84.5 7.2 %collective-permute-start.16 = (bf16[2,2,180,256]{3,2,1,0:T(8,128)(2,1)S(1)}, bf16[2,2,180,256]{3,2,1,0:T(8,128)(2,1)S(1)}, u32[]{:S(2)}, u32[]{:S(2)}) collective-permute-start(bf16[2,2,180,256]{3,2,1,0:T(8,128)(2,1)S(1)} %get-tuple-element.81), channel_id=1, source_target_pairs={{0,1},{1,0},{2,3},{3,2},{4,5},{5,4},{6,7},{7,6},{8,9},{9,8},{10,11... | collective-permute-start | bytes 1105928 | tf_op jit(solution)/shard_map/ppermute | solution.py:439
  86.7 5.5 %collective-permute-start.19 = (bf16[2,1,180,256]{3,2,1,0:T(8,128)(2,1)S(1)}, bf16[2,1,180,256]{3,2,1,0:T(8,128)(2,1)S(1)}, u32[]{:S(2)}, u32[]{:S(2)}) collective-permute-start(bf16[2,1,180,256]{3,2,1,0:T(8,128)(2,1)S(1)} %get-tuple-element.88), channel_id=1, source_target_pairs={{0,1},{1,0},{2,3},{3,2},{4,5},{5,4},{6,7},{7,6},{8,9},{9,8},{10,11... | collective-permute-start | bytes 552968 | tf_op jit(solution)/shard_map/ppermute | solution.py:439
  89.2 4.8 %collective-permute-start.4 = (bf16[1,2,180,256]{3,2,1,0:T(8,128)(2,1)S(1)}, bf16[1,2,180,256]{3,2,1,0:T(8,128)(2,1)S(1)}, u32[]{:S(2)}, u32[]{:S(2)}) collective-permute-start(bf16[1,2,180,256]{3,2,1,0:T(8,128)(2,1)S(1)} %get-tuple-element.75), channel_id=1, source_target_pairs={{0,1},{1,0},{2,3},{3,2},{4,5},{5,4},{6,7},{7,6},{8,9},{9,8},{10,11... | collective-permute-start | bytes 552968 | tf_op jit(solution)/shard_map/ppermute | solution.py:439
  89.8 18.9 %copy-start.1 = (s32[128]{0:T(128)S(1)}, s32[128]{0:T(128)}, u32[]{:S(2)}) copy-start(s32[128]{0:T(128)} %constant.11.clone.slot_ref) | copy-start | bytes 1540
  89.8 13.7 %collective-permute-start.23 = (bf16[3,180,256]{2,1,0:T(8,128)(2,1)S(1)}, bf16[3,180,256]{2,1,0:T(8,128)(2,1)S(1)}, u32[]{:S(2)}, u32[]{:S(2)}) collective-permute-start(bf16[3,180,256]{2,1,0:T(8,128)(2,1)S(1)} %shard_map.120), channel_id=1, source_target_pairs={{0,2},{2,0},{4,6},{6,4},{8,10},{10,8},{12,14},{14,12},{16,18},{18,... | collective-permute-start | bytes 829448 | tf_op jit(solution)/shard_map/ppermute | solution.py:461
  91.7 11.9 %collective-permute-start.21 = (bf16[2,180,256]{2,1,0:T(8,128)(2,1)S(1)}, bf16[2,180,256]{2,1,0:T(8,128)(2,1)S(1)}, u32[]{:S(2)}, u32[]{:S(2)}) collective-permute-start(bf16[2,180,256]{2,1,0:T(8,128)(2,1)S(1)} %shard_map.118), channel_id=1, source_target_pairs={{0,2},{2,0},{4,6},{6,4},{8,10},{10,8},{12,14},{14,12},{16,18},{18,... | collective-permute-start | bytes 552968 | tf_op jit(solution)/shard_map/ppermute | solution.py:461
  92.2 15.4 %collective-permute-start.24 = (bf16[2,180,256]{2,1,0:T(8,128)(2,1)S(1)}, bf16[2,180,256]{2,1,0:T(8,128)(2,1)S(1)}, u32[]{:S(2)}, u32[]{:S(2)}) collective-permute-start(bf16[2,180,256]{2,1,0:T(8,128)(2,1)S(1)} %get-tuple-element.95), channel_id=1, source_target_pairs={{0,2},{2,0},{4,6},{6,4},{8,10},{10,8},{12,14},{14,12},{16,18},{18,... | collective-permute-start | bytes 552968 | tf_op jit(solution)/shard_map/ppermute | solution.py:465
  94.0 14.7 %collective-permute-start.25 = (bf16[1,180,256]{2,1,0:T(8,128)(2,1)S(1)}, bf16[1,180,256]{2,1,0:T(8,128)(2,1)S(1)}, u32[]{:S(2)}, u32[]{:S(2)}) collective-permute-start(bf16[1,180,256]{2,1,0:T(8,128)(2,1)S(1)} %get-tuple-element.96), channel_id=1, source_target_pairs={{0,2},{2,0},{4,6},{6,4},{8,10},{10,8},{12,14},{14,12},{16,18},{18,... | collective-permute-start | bytes 276488 | tf_op jit(solution)/shard_map/ppermute | solution.py:465

commit v3 on v2

--- a/solution.py
+++ b/solution.py
@@ -145,12 +145,16 @@
     out_ref[...] = jnp.zeros_like(out_ref)
     score(0, key_left, score_left)
 
-    @pl.loop(0, live)
+    @pl.loop(0, live - 1)
     def tile_step(tile):
         score(tile, key_right, score_right)
         mix(tile, 0, score_left)
-        score(jnp.minimum(tile + 1, live - 1), key_left, score_left)
+        score(tile + 1, key_left, score_left)
         mix(tile, 1, score_right)
+
+    score(live - 1, key_right, score_right)
+    mix(live - 1, 0, score_left)
+    mix(live - 1, 1, score_right)
 
 
 def attend(part, parts, live, sinks, queries, tree_k, tree_v, cache_k, cache_v, bias):

time: 111 us -> 109 us (0.982)
  Pallas kernels: 44.1 us -> 42.6 us
    pallas_call x8, Pallas kernels: 23.5 us -> 22 us  [attend(): pl.pallas_call(functools.partial(attend_kernel, kv_head, first), out_shap...]
  transfers between devices with their start and end apart: 26 -> 26, of which waited for: 9 -> 9; matrix products, arithmetic and copies ran while one was open for 0% -> 0% of each run, Pallas kernels for 38% -> 37%
where the time goes in v3:
time: 109 us
  Pallas kernels  42.6 us (39%)
  waiting for transfers between devices  33.9 us (31%)
  starting transfers between devices  30.9 us (28%)
    pallas_call x8, Pallas kernels, attend(): pl.pallas_call(functools.partial(attend_kernel, kv_head, first), out_shap...  22 us
    pallas_call x7, Pallas kernels, project(): pl.pallas_call(functools.partial(project_kernel, [len(block) for block in...  16.6 us
    ppermute x4, waiting for transfers between devices, per_device(): other.append(lax.ppermute(given, 'req', swap))  14.2 us
    ppermute x6, starting transfers between devices, per_device(): slots.append(lax.ppermute(block, 'req', hops))  11.7 us
    ppermute x8, waiting for transfers between devices, per_device(): partner.append(lax.ppermute(chunk, 'req', swap))  11.6 us
    ppermute x8, starting transfers between devices, per_device(): partner.append(lax.ppermute(chunk, 'req', swap))  10.5 us
    ppermute x6, waiting for transfers between devices, per_device(): slots.append(lax.ppermute(block, 'req', hops))  8.2 us
    ppermute x4, starting transfers between devices, per_device(): other.append(lax.ppermute(given, 'req', swap))  4.31 us
  transfers between devices with their start and end apart: 26, of which 9 were waited for; matrix products, arithmetic and copies ran while one was open for 0% of the time, Pallas kernels for 37%

profile of v3, /device:TPU:0, one launch (start us, length us, event | category | flops | bytes accessed | tf_op | source)
XLA Modules:
  0.0 109.3 jit_solution(3225442063704953764)
XLA Ops:
  0.0 3.1 %collective-permute-start = (bf16[180,2048]{1,0:T(8,128)(2,1)}, bf16[180,2048]{1,0:T(8,128)(2,1)S(1)}, u32[]{:S(2)}, u32[]{:S(2)}) collective-permute-start(bf16[180,2048]{1,0:T(8,128)(2,1)} %bitcast.12), channel_id=1, source_target_pairs={{0,8},{2,10},{4,12},{6,14},{8,0},{10,2},{12,4},{14,6},{16,24},{18,... | collective-permute-start | bytes 2211848 | tf_op jit(solution)/shard_map/ppermute | solution.py:430
  3.1 1.5 %collective-permute-start.1 = (bf16[180,2048]{1,0:T(8,128)(2,1)}, bf16[180,2048]{1,0:T(8,128)(2,1)S(1)}, u32[]{:S(2)}, u32[]{:S(2)}) collective-permute-start(bf16[180,2048]{1,0:T(8,128)(2,1)} %bitcast.13), channel_id=1, source_target_pairs={{0,4},{2,6},{4,0},{6,2},{8,16},{10,18},{12,20},{14,22},{16,8},{18,... | collective-permute-start | bytes 2211848 | tf_op jit(solution)/shard_map/ppermute | solution.py:430
  4.7 0.7 copy-done.7
  5.4 1.6 %ancestry.1.bias_ref = f32[512,512]{1,0:T(8,128)S(1)} custom-call(s32[1,512]{1,0:T(1,128)S(1)} %copy-done.7), custom_call_target="tpu_custom_call" | custom-call | flops 10737418240 | bytes 1048576 | tf_op jit(solution)/shard_map/ancestry/pallas_call | solution.py:51
  7.7 2.7 %shard_map.100.refs_2_.refs_3_ = bf16[256,512]{1,0:T(8,128)(2,1)S(1)} custom-call(s32[1]{0:T(128)S(6)} %copy.11.live_ref, f32[1,32]{1,0:T(1,128)S(1)} %bitcast.57, bf16[512,2048]{1,0:T(8,128)(2,1)S(1)} %bitcast.17, bf16[512,256]{1,0:T(8,128)(2,1)S(1)} %bitcast.41, bf16[512,256]{1,0:T(8,128)(2,1)S(1)} %bitcast.49, bf16[1024,256]{1,0:T(8,128)(2,1)S(1)} %bitcast.25, ...), custom_call_target="tpu_custom_call" | custom-call | flops 3221225472 | bytes 3145728 | tf_op jit(solution)/shard_map/pallas_call | solution.py:168
  10.4 2.7 %shard_map.101.refs_3_.refs_4_ = bf16[256,512]{1,0:T(8,128)(2,1)S(1)} custom-call(s32[1]{0:T(128)S(6)} %copy.11.live_ref, f32[1,32]{1,0:T(1,128)S(1)} %bitcast.58, bf16[512,2048]{1,0:T(8,128)(2,1)S(1)} %bitcast.18, bf16[512,256]{1,0:T(8,128)(2,1)S(1)} %bitcast.42, bf16[512,256]{1,0:T(8,128)(2,1)S(1)} %bitcast.50, bf16[1024,256]{1,0:T(8,128)(2,1)S(1)} %bitcast.26, ...), custom_call_target="tpu_custom_call" | custom-call | flops 3221225472 | bytes 3145728 | tf_op jit(solution)/shard_map/pallas_call | solution.py:168
  13.1 2.7 %shard_map.102.refs_4_.refs_5_ = bf16[256,512]{1,0:T(8,128)(2,1)S(1)} custom-call(s32[1]{0:T(128)S(6)} %copy.11.live_ref, f32[1,32]{1,0:T(1,128)S(1)} %bitcast.59, bf16[512,2048]{1,0:T(8,128)(2,1)S(1)} %bitcast.19, bf16[512,256]{1,0:T(8,128)(2,1)S(1)} %bitcast.43, bf16[512,256]{1,0:T(8,128)(2,1)S(1)} %bitcast.51, bf16[1024,256]{1,0:T(8,128)(2,1)S(1)} %bitcast.27, ...), custom_call_target="tpu_custom_call" | custom-call | flops 3221225472 | bytes 3145728 | tf_op jit(solution)/shard_map/pallas_call | solution.py:168
  15.8 1.5 %collective-permute-start.10 = (bf16[256,512]{1,0:T(8,128)(2,1)S(1)}, bf16[256,512]{1,0:T(8,128)(2,1)S(1)}, u32[]{:S(2)}, u32[]{:S(2)}) collective-permute-start(bf16[256,512]{1,0:T(8,128)(2,1)S(1)} %shard_map.102.refs_4_.refs_5_), channel_id=1, source_target_pairs={{0,2},{2,0},{4,6},{6,4},{8,10},{10,8},{12,14},{14,12},{16,18},{18,... | collective-permute-start | bytes 786440 | tf_op jit(solution)/shard_map/ppermute | solution.py:438
  17.4 0.6 collective-permute-start.9
  17.9 1.5 %collective-permute-start.8 = (bf16[256,512]{1,0:T(8,128)(2,1)S(1)}, bf16[256,512]{1,0:T(8,128)(2,1)S(1)}, u32[]{:S(2)}, u32[]{:S(2)}) collective-permute-start(bf16[256,512]{1,0:T(8,128)(2,1)S(1)} %shard_map.100.refs_2_.refs_3_), channel_id=1, source_target_pairs={{0,2},{2,0},{4,6},{6,4},{8,10},{10,8},{12,14},{14,12},{16,18},{18,... | collective-permute-start | bytes 786440 | tf_op jit(solution)/shard_map/ppermute | solution.py:438
  19.4 0.7 collective-permute-done.refs_1_
  20.1 1.5 %collective-permute-done.1.refs_0_.refs_2_ = bf16[180,2048]{1,0:T(8,128)(2,1)S(1)} collective-permute-done((bf16[180,2048]{1,0:T(8,128)(2,1)}, bf16[180,2048]{1,0:T(8,128)(2,1)S(1)}, u32[]{:S(2)}, u32[]{:S(2)}) %collective-permute-start.1) | collective-permute-done | bytes 737312 | tf_op jit(solution)/shard_map/ppermute | solution.py:430
  21.6 1.5 %collective-permute-start.3 = (bf16[180,2048]{1,0:T(8,128)(2,1)S(1)}, bf16[180,2048]{1,0:T(8,128)(2,1)S(1)}, u32[]{:S(2)}, u32[]{:S(2)}) collective-permute-start(bf16[180,2048]{1,0:T(8,128)(2,1)S(1)} %collective-permute-done.refs_1_), channel_id=1, source_target_pairs={{0,4},{2,6},{4,0},{6,2},{8,16},{10,18},{12,20},{14,22},{16,8},{18,... | collective-permute-start | bytes 2211848 | tf_op jit(solution)/shard_map/ppermute | solution.py:430
  23.1 1.6 %collective-permute-start.2 = (bf16[180,2048]{1,0:T(8,128)(2,1)S(1)}, bf16[180,2048]{1,0:T(8,128)(2,1)S(1)}, u32[]{:S(2)}, u32[]{:S(2)}) collective-permute-start(bf16[180,2048]{1,0:T(8,128)(2,1)S(1)} %collective-permute-done.1.refs_0_.refs_2_), channel_id=1, source_target_pairs={{0,8},{2,10},{4,12},{6,14},{8,0},{10,2},{12,4},{14,6},{16,24},{18,... | collective-permute-start | bytes 2211848 | tf_op jit(solution)/shard_map/ppermute | solution.py:430
  24.7 2.7 %shard_map.103.refs_5_.refs_6_ = bf16[256,512]{1,0:T(8,128)(2,1)S(1)} custom-call(s32[1]{0:T(128)S(6)} %copy.11.live_ref, f32[1,32]{1,0:T(1,128)S(1)} %bitcast.60, bf16[512,2048]{1,0:T(8,128)(2,1)S(1)} %bitcast.20, bf16[512,256]{1,0:T(8,128)(2,1)S(1)} %bitcast.44, bf16[512,256]{1,0:T(8,128)(2,1)S(1)} %bitcast.52, bf16[1024,256]{1,0:T(8,128)(2,1)S(1)} %bitcast.28, ...), custom_call_target="tpu_custom_call" | custom-call | flops 3221225472 | bytes 3145728 | tf_op jit(solution)/shard_map/pallas_call | solution.py:168
  27.5 2.8 %shard_map.104.refs_6_.refs_7_ = bf16[256,512]{1,0:T(8,128)(2,1)S(1)} custom-call(s32[1]{0:T(128)S(6)} %copy.11.live_ref, f32[1,32]{1,0:T(1,128)S(1)} %bitcast.61, bf16[512,2048]{1,0:T(8,128)(2,1)S(1)} %bitcast.21, bf16[512,256]{1,0:T(8,128)(2,1)S(1)} %bitcast.45, bf16[512,256]{1,0:T(8,128)(2,1)S(1)} %bitcast.53, bf16[1024,256]{1,0:T(8,128)(2,1)S(1)} %bitcast.29, ...), custom_call_target="tpu_custom_call" | custom-call | flops 3221225472 | bytes 3145728 | tf_op jit(solution)/shard_map/pallas_call | solution.py:168
  30.3 2.7 %shard_map.105.refs_7_.refs_8_ = bf16[256,512]{1,0:T(8,128)(2,1)S(1)} custom-call(s32[1]{0:T(128)S(6)} %copy.11.live_ref, f32[1,32]{1,0:T(1,128)S(1)} %bitcast.62, bf16[512,2048]{1,0:T(8,128)(2,1)S(1)} %bitcast.22, bf16[512,256]{1,0:T(8,128)(2,1)S(1)} %bitcast.46, bf16[512,256]{1,0:T(8,128)(2,1)S(1)} %bitcast.54, bf16[1024,256]{1,0:T(8,128)(2,1)S(1)} %bitcast.30, ...), custom_call_target="tpu_custom_call" | custom-call | flops 3221225472 | bytes 3145728 | tf_op jit(solution)/shard_map/pallas_call | solution.py:168
  33.0 6.0 %collective-permute-done.3.refs_1_.refs_3_ = bf16[180,2048]{1,0:T(8,128)(2,1)S(1)} collective-permute-done((bf16[180,2048]{1,0:T(8,128)(2,1)S(1)}, bf16[180,2048]{1,0:T(8,128)(2,1)S(1)}, u32[]{:S(2)}, u32[]{:S(2)}) %collective-permute-start.3) | collective-permute-done | bytes 737312 | tf_op jit(solution)/shard_map/ppermute | solution.py:430
  39.0 1.5 %collective-permute-start.13 = (bf16[256,512]{1,0:T(8,128)(2,1)S(1)}, bf16[256,512]{1,0:T(8,128)(2,1)S(1)}, u32[]{:S(2)}, u32[]{:S(2)}) collective-permute-start(bf16[256,512]{1,0:T(8,128)(2,1)S(1)} %shard_map.105.refs_7_.refs_8_), channel_id=1, source_target_pairs={{0,2},{2,0},{4,6},{6,4},{8,10},{10,8},{12,14},{14,12},{16,18},{18,... | collective-permute-start | bytes 786440 | tf_op jit(solution)/shard_map/ppermute | solution.py:438
  40.5 1.5 %collective-permute-start.7 = (bf16[180,2048]{1,0:T(8,128)(2,1)S(1)}, bf16[180,2048]{1,0:T(8,128)(2,1)S(1)}, u32[]{:S(2)}, u32[]{:S(2)}) collective-permute-start(bf16[180,2048]{1,0:T(8,128)(2,1)S(1)} %collective-permute-done.2.refs_2_.refs_4_), channel_id=1, source_target_pairs={{0,4},{2,6},{4,0},{6,2},{8,16},{10,18},{12,20},{14,22},{16,8},{18,... | collective-permute-start | bytes 2211848 | tf_op jit(solution)/shard_map/ppermute | solution.py:430
  42.0 2.5 %collective-permute-start.6 = (bf16[180,2048]{1,0:T(8,128)(2,1)S(1)}, bf16[180,2048]{1,0:T(8,128)(2,1)S(1)}, u32[]{:S(2)}, u32[]{:S(2)}) collective-permute-start(bf16[180,2048]{1,0:T(8,128)(2,1)S(1)} %collective-permute-done.3.refs_1_.refs_3_), channel_id=1, source_target_pairs={{0,8},{2,10},{4,12},{6,14},{8,0},{10,2},{12,4},{14,6},{16,24},{18,... | collective-permute-start | bytes 2211848 | tf_op jit(solution)/shard_map/ppermute | solution.py:430
  44.5 2.7 %shard_map.106.refs_8_.refs_9_ = bf16[256,512]{1,0:T(8,128)(2,1)S(1)} custom-call(s32[1]{0:T(128)S(6)} %copy.11.live_ref, f32[1,32]{1,0:T(1,128)S(1)} %bitcast.63, bf16[512,2048]{1,0:T(8,128)(2,1)S(1)} %bitcast.23, bf16[512,256]{1,0:T(8,128)(2,1)S(1)} %bitcast.47, bf16[512,256]{1,0:T(8,128)(2,1)S(1)} %bitcast.55, bf16[1024,256]{1,0:T(8,128)(2,1)S(1)} %bitcast.31, ...), custom_call_target="tpu_custom_call" | custom-call | flops 3221225472 | bytes 3145728 | tf_op jit(solution)/shard_map/pallas_call | solution.py:168
  47.3 1.7 %collective-permute-start.12 = (bf16[256,512]{1,0:T(8,128)(2,1)S(1)}, bf16[256,512]{1,0:T(8,128)(2,1)S(1)}, u32[]{:S(2)}, u32[]{:S(2)}) collective-permute-start(bf16[256,512]{1,0:T(8,128)(2,1)S(1)} %shard_map.104.refs_6_.refs_7_), channel_id=1, source_target_pairs={{0,2},{2,0},{4,6},{6,4},{8,10},{10,8},{12,14},{14,12},{16,18},{18,... | collective-permute-start | bytes 786440 | tf_op jit(solution)/shard_map/ppermute | solution.py:438
  49.0 0.4 collective-permute-start.11
  49.4 1.7 %collective-permute-start.14 = (bf16[256,512]{1,0:T(8,128)(2,1)S(1)}, bf16[256,512]{1,0:T(8,128)(2,1)S(1)}, u32[]{:S(2)}, u32[]{:S(2)}) collective-permute-start(bf16[256,512]{1,0:T(8,128)(2,1)S(1)} %shard_map.106.refs_8_.refs_9_), channel_id=1, source_target_pairs={{0,2},{2,0},{4,6},{6,4},{8,10},{10,8},{12,14},{14,12},{16,18},{18,... | collective-permute-start | bytes 786440 | tf_op jit(solution)/shard_map/ppermute | solution.py:438
  51.0 2.9 %shard_map.107.refs_9_.refs_10_ = bf16[256,512]{1,0:T(8,128)(2,1)S(1)} custom-call(s32[1]{0:T(128)S(6)} %copy.11.live_ref, f32[1,32]{1,0:T(1,128)S(1)} %bitcast.64, bf16[512,2048]{1,0:T(8,128)(2,1)S(1)} %bitcast.24, bf16[512,256]{1,0:T(8,128)(2,1)S(1)} %bitcast.48, bf16[512,256]{1,0:T(8,128)(2,1)S(1)} %bitcast.56, bf16[1024,256]{1,0:T(8,128)(2,1)S(1)} %bitcast.32, ...), custom_call_target="tpu_custom_call" | custom-call | flops 3221225472 | bytes 3145728 | tf_op jit(solution)/shard_map/pallas_call | solution.py:168
  54.0 2.5 %collective-permute-done.12.refs_14_.refs_9_ = bf16[256,512]{1,0:T(8,128)(2,1)S(1)} collective-permute-done((bf16[256,512]{1,0:T(8,128)(2,1)S(1)}, bf16[256,512]{1,0:T(8,128)(2,1)S(1)}, u32[]{:S(2)}, u32[]{:S(2)}) %collective-permute-start.12) | collective-permute-done | bytes 262176 | tf_op jit(solution)/shard_map/ppermute | solution.py:438
  56.5 1.7 %collective-permute-start.15 = (bf16[256,512]{1,0:T(8,128)(2,1)S(1)}, bf16[256,512]{1,0:T(8,128)(2,1)S(1)}, u32[]{:S(2)}, u32[]{:S(2)}) collective-permute-start(bf16[256,512]{1,0:T(8,128)(2,1)S(1)} %shard_map.107.refs_9_.refs_10_), channel_id=1, source_target_pairs={{0,2},{2,0},{4,6},{6,4},{8,10},{10,8},{12,14},{14,12},{16,18},{18,... | collective-permute-start | bytes 786440 | tf_op jit(solution)/shard_map/ppermute | solution.py:438
  58.2 4.0 %collective-permute-done.11.refs_13_.refs_8_ = bf16[256,512]{1,0:T(8,128)(2,1)S(1)} collective-permute-done((bf16[256,512]{1,0:T(8,128)(2,1)S(1)}, bf16[256,512]{1,0:T(8,128)(2,1)S(1)}, u32[]{:S(2)}, u32[]{:S(2)}) %collective-permute-start.11) | collective-permute-done | bytes 262176 | tf_op jit(solution)/shard_map/ppermute | solution.py:438
  62.1 5.1 %collective-permute-done.14.refs_16_.refs_11_ = bf16[256,512]{1,0:T(8,128)(2,1)S(1)} collective-permute-done((bf16[256,512]{1,0:T(8,128)(2,1)S(1)}, bf16[256,512]{1,0:T(8,128)(2,1)S(1)}, u32[]{:S(2)}, u32[]{:S(2)}) %collective-permute-start.14) | collective-permute-done | bytes 262176 | tf_op jit(solution)/shard_map/ppermute | solution.py:438
  67.2 3.5 %shard_map.114.refs_3_.refs_4_ = f32[1,5,180,512]{3,2,1,0:T(8,128)S(1)} custom-call(s32[2]{0:T(128)S(1)} %pad_add_fusion.whom_ref, bf16[180,2048]{1,0:T(8,128)(2,1)S(1)} %bitcast.14, bf16[180,2048]{1,0:T(8,128)(2,1)S(1)} %collective-permute-done.refs_1_, bf16[180,2048]{1,0:T(8,128)(2,1)S(1)} %collective-permute-done.1.refs_0_.refs_2_, ...), custom_call_target="tpu_custom_call" | custom-call | flops 3303014400 | bytes 5529600 | tf_op jit(solution)/shard_map/pallas_call | solution.py:244
  70.8 1.4 %collective-permute-start.17 = (bf16[180,1024]{1,0:T(8,128)(2,1)S(1)}, bf16[180,1024]{1,0:T(8,128)(2,1)S(1)}, u32[]{:S(2)}, u32[]{:S(2)}) collective-permute-start(bf16[180,1024]{1,0:T(8,128)(2,1)S(1)} %get-tuple-element.85), channel_id=1, source_target_pairs={{0,4},{2,6},{4,0},{6,2},{8,16},{10,18},{12,20},{14,22},{16,8},{18,... | collective-permute-start | bytes 1105928 | tf_op jit(solution)/shard_map/ppermute | solution.py:456
  72.2 1.1 %collective-permute-start.18 = (bf16[180,1024]{1,0:T(8,128)(2,1)S(1)}, bf16[180,1024]{1,0:T(8,128)(2,1)S(1)}, u32[]{:S(2)}, u32[]{:S(2)}) collective-permute-start(bf16[180,1024]{1,0:T(8,128)(2,1)S(1)} %get-tuple-element.86), channel_id=1, source_target_pairs={{0,8},{2,10},{4,12},{6,14},{8,0},{10,2},{12,4},{14,6},{16,24},{18,... | collective-permute-start | bytes 1105928 | tf_op jit(solution)/shard_map/ppermute | solution.py:456
  73.3 3.3 %shard_map.110 = (bf16[1,3,180,256]{3,2,1,0:T(8,128)(2,1)S(1)}, bf16[1,3,180,256]{3,2,1,0:T(8,128)(2,1)S(1)}) custom-call(s32[2]{0:T(128)S(1)} %pad_add_fusion.whom_ref, bf16[180,2048]{1,0:T(8,128)(2,1)S(1)} %collective-permute-done.1.refs_0_.refs_2_, bf16[180,2048]{1,0:T(8,128)(2,1)S(1)} %collective-permute-done.3.refs_1_.refs_3_, ...), custom_call_target="tpu_custom_call" | custom-call | flops 2264924160 | bytes 3317760 | tf_op jit(solution)/shard_map/pallas_call | solution.py:244
  76.8 1.3 %shard_map.119 = (bf16[1,3,180,256]{3,2,1,0:T(8,128)(2,1)S(1)}, bf16[1,3,180,256]{3,2,1,0:T(8,128)(2,1)S(1)}) custom-call(s32[2]{0:T(128)S(1)} %pad_add_fusion.whom_ref, bf16[180,2048]{1,0:T(8,128)(2,1)S(1)} %collective-permute-done.1.refs_0_.refs_2_, bf16[180,2048]{1,0:T(8,128)(2,1)S(1)} %collective-permute-done.3.refs_1_.refs_3_, ...), custom_call_target="tpu_custom_call" | custom-call | flops 283115520 | bytes 3317760 | tf_op jit(solution)/shard_map/pallas_call | solution.py:244
  78.1 0.6 collective-permute-start.22
  78.6 1.0 shard_map.117
  79.7 3.4 %shard_map.112 = (bf16[2,2,180,256]{3,2,1,0:T(8,128)(2,1)S(1)}, bf16[2,2,180,256]{3,2,1,0:T(8,128)(2,1)S(1)}) custom-call(s32[2]{0:T(128)S(1)} %pad_add_fusion.whom_ref, bf16[180,2048]{1,0:T(8,128)(2,1)S(1)} %collective-permute-done.6.refs_0_.low_ref, bf16[180,2048]{1,0:T(8,128)(2,1)S(1)} %collective-permute-done.7.refs_1_.high_ref, ...), custom_call_target="tpu_custom_call" | custom-call | flops 3019898880 | bytes 2211840 | tf_op jit(solution)/shard_map/pallas_call | solution.py:244
  83.1 0.5 collective-permute-start.16
  83.7 1.6 %shard_map.115 = (bf16[2,1,180,256]{3,2,1,0:T(8,128)(2,1)S(1)}, bf16[2,1,180,256]{3,2,1,0:T(8,128)(2,1)S(1)}) custom-call(s32[2]{0:T(128)S(1)} %pad_add_fusion.whom_ref, bf16[180,1024]{1,0:T(8,128)(2,1)S(1)} %collective-permute-done.17.refs_0_, bf16[180,1024]{1,0:T(8,128)(2,1)S(1)} %collective-permute-done.18.refs_1_, ...), custom_call_target="tpu_custom_call" | custom-call | flops 1509949440 | bytes 1105920 | tf_op jit(solution)/shard_map/pallas_call | solution.py:244
  85.4 2.4 %shard_map.108 = (bf16[1,2,180,256]{3,2,1,0:T(8,128)(2,1)S(1)}, bf16[1,2,180,256]{3,2,1,0:T(8,128)(2,1)S(1)}) custom-call(s32[2]{0:T(128)S(1)} %pad_add_fusion.whom_ref, bf16[180,2048]{1,0:T(8,128)(2,1)S(1)} %bitcast.16, bf16[180,2048]{1,0:T(8,128)(2,1)S(1)} %collective-permute-done.refs_1_, bf16[256,512]{1,0:T(8,128)(2,1)S(1)} %shard_map.100.refs_2_.refs_3_, ...), custom_call_target="tpu_custom_call" | custom-call | flops 1509949440 | bytes 2211840 | tf_op jit(solution)/shard_map/pallas_call | solution.py:244
  87.9 0.5 collective-permute-start.4
  88.5 1.8 %collective-permute-start.23 = (bf16[3,180,256]{2,1,0:T(8,128)(2,1)S(1)}, bf16[3,180,256]{2,1,0:T(8,128)(2,1)S(1)}, u32[]{:S(2)}, u32[]{:S(2)}) collective-permute-start(bf16[3,180,256]{2,1,0:T(8,128)(2,1)S(1)} %shard_map.120), channel_id=1, source_target_pairs={{0,2},{2,0},{4,6},{6,4},{8,10},{10,8},{12,14},{14,12},{16,18},{18,... | collective-permute-start | bytes 829448 | tf_op jit(solution)/shard_map/ppermute | solution.py:465
  90.8 1.8 %collective-permute-start.24 = (bf16[2,180,256]{2,1,0:T(8,128)(2,1)S(1)}, bf16[2,180,256]{2,1,0:T(8,128)(2,1)S(1)}, u32[]{:S(2)}, u32[]{:S(2)}) collective-permute-start(bf16[2,180,256]{2,1,0:T(8,128)(2,1)S(1)} %get-tuple-element.95), channel_id=1, source_target_pairs={{0,2},{2,0},{4,6},{6,4},{8,10},{10,8},{12,14},{14,12},{16,18},{18,... | collective-permute-start | bytes 552968 | tf_op jit(solution)/shard_map/ppermute | solution.py:469
  93.2 9.0 %collective-permute-done.21.refs_4_ = bf16[2,180,256]{2,1,0:T(8,128)(2,1)S(1)} collective-permute-done((bf16[2,180,256]{2,1,0:T(8,128)(2,1)S(1)}, bf16[2,180,256]{2,1,0:T(8,128)(2,1)S(1)}, u32[]{:S(2)}, u32[]{:S(2)}) %collective-permute-start.21) | collective-permute-done | bytes 184352 | tf_op jit(solution)/shard_map/ppermute | solution.py:465
  102.2 4.0 %collective-permute-done.24.refs_6_ = bf16[2,180,256]{2,1,0:T(8,128)(2,1)S(1)} collective-permute-done((bf16[2,180,256]{2,1,0:T(8,128)(2,1)S(1)}, bf16[2,180,256]{2,1,0:T(8,128)(2,1)S(1)}, u32[]{:S(2)}, u32[]{:S(2)}) %collective-permute-start.24) | collective-permute-done | bytes 184352 | tf_op jit(solution)/shard_map/ppermute | solution.py:469
  106.3 1.1 collective-permute-done.25.refs_7_
  107.3 1.9 %arrange.1 = bf16[2880,256]{1,0:T(8,128)(2,1)} custom-call(s32[2]{0:T(128)S(1)} %pad_add_fusion.whom_ref, s32[128]{0:T(128)S(1)} %copy-done.1, bf16[2,180,256]{2,1,0:T(8,128)(2,1)S(1)} %shard_map.109.refs_0_, bf16[3,180,256]{2,1,0:T(8,128)(2,1)S(1)} %shard_map.111.refs_1_, bf16[2,180,256]{2,1,0:T(8,128)(2,1)S(1)} %get-tuple-element.82.refs_2_, ...), custom_call_target="tpu_custom_call" | custom-call | tf_op jit(solution)/shard_map/arrange/pallas_call | solution.py:347
  (47 shorter events, 1.6 us)
Async XLA Ops:
  0.0 20.1 %collective-permute-start = (bf16[180,2048]{1,0:T(8,128)(2,1)}, bf16[180,2048]{1,0:T(8,128)(2,1)S(1)}, u32[]{:S(2)}, u32[]{:S(2)}) collective-permute-start(bf16[180,2048]{1,0:T(8,128)(2,1)} %bitcast.12), channel_id=1, source_target_pairs={{0,8},{2,10},{4,12},{6,14},{8,0},{10,2},{12,4},{14,6},{16,24},{18,... | collective-permute-start | bytes 2211848 | tf_op jit(solution)/shard_map/ppermute | solution.py:430
  3.1 18.5 %collective-permute-start.1 = (bf16[180,2048]{1,0:T(8,128)(2,1)}, bf16[180,2048]{1,0:T(8,128)(2,1)S(1)}, u32[]{:S(2)}, u32[]{:S(2)}) collective-permute-start(bf16[180,2048]{1,0:T(8,128)(2,1)} %bitcast.13), channel_id=1, source_target_pairs={{0,4},{2,6},{4,0},{6,2},{8,16},{10,18},{12,20},{14,22},{16,8},{18,... | collective-permute-start | bytes 2211848 | tf_op jit(solution)/shard_map/ppermute | solution.py:430
  4.6 0.7 copy-start.7
  5.3 2.3 %copy-start.2 = (bf16[1,512,2048]{2,1,0:T(8,128)(2,1)S(1)}, bf16[1,512,2048]{2,1,0:T(8,128)(2,1)}, u32[]{:S(2)}) copy-start(bf16[1,512,2048]{2,1,0:T(8,128)(2,1)} %param.10) | copy-start | bytes 6291460
  5.3 2.3 %copy-start.3 = (bf16[1,1024,256]{2,1,0:T(8,128)(2,1)S(1)}, bf16[1,1024,256]{2,1,0:T(8,128)(2,1)}, u32[]{:S(2)}) copy-start(bf16[1,1024,256]{2,1,0:T(8,128)(2,1)} %param.13) | copy-start | bytes 1572868
  5.3 2.3 %copy-start.4 = (bf16[1,1024,256]{2,1,0:T(8,128)(2,1)S(1)}, bf16[1,1024,256]{2,1,0:T(8,128)(2,1)}, u32[]{:S(2)}) copy-start(bf16[1,1024,256]{2,1,0:T(8,128)(2,1)} %param.14) | copy-start | bytes 1572868
  5.3 2.3 %copy-start.5 = (bf16[1,512,256]{2,1,0:T(8,128)(2,1)S(1)}, bf16[1,512,256]{2,1,0:T(8,128)(2,1)}, u32[]{:S(2)}) copy-start(bf16[1,512,256]{2,1,0:T(8,128)(2,1)} %param.11) | copy-start | bytes 786436
  5.3 2.4 %copy-start.6 = (bf16[1,512,256]{2,1,0:T(8,128)(2,1)S(1)}, bf16[1,512,256]{2,1,0:T(8,128)(2,1)}, u32[]{:S(2)}) copy-start(bf16[1,512,256]{2,1,0:T(8,128)(2,1)} %param.12) | copy-start | bytes 786436
  5.4 2.4 %copy-start.8 = (f32[32]{0:T(128)S(1)}, f32[32]{0:T(128)}, u32[]{:S(2)}) copy-start(f32[32]{0:T(128)} %param.15) | copy-start | bytes 388
  15.8 26.2 %collective-permute-start.10 = (bf16[256,512]{1,0:T(8,128)(2,1)S(1)}, bf16[256,512]{1,0:T(8,128)(2,1)S(1)}, u32[]{:S(2)}, u32[]{:S(2)}) collective-permute-start(bf16[256,512]{1,0:T(8,128)(2,1)S(1)} %shard_map.102.refs_4_.refs_5_), channel_id=1, source_target_pairs={{0,2},{2,0},{4,6},{6,4},{8,10},{10,8},{12,14},{14,12},{16,18},{18,... | collective-permute-start | bytes 786440 | tf_op jit(solution)/shard_map/ppermute | solution.py:438
  17.4 29.9 %collective-permute-start.9 = (bf16[256,512]{1,0:T(8,128)(2,1)S(1)}, bf16[256,512]{1,0:T(8,128)(2,1)S(1)}, u32[]{:S(2)}, u32[]{:S(2)}) collective-permute-start(bf16[256,512]{1,0:T(8,128)(2,1)S(1)} %shard_map.101.refs_3_.refs_4_), channel_id=1, source_target_pairs={{0,2},{2,0},{4,6},{6,4},{8,10},{10,8},{12,14},{14,12},{16,18},{18,... | collective-permute-start | bytes 786440 | tf_op jit(solution)/shard_map/ppermute | solution.py:438
  17.9 31.1 %collective-permute-start.8 = (bf16[256,512]{1,0:T(8,128)(2,1)S(1)}, bf16[256,512]{1,0:T(8,128)(2,1)S(1)}, u32[]{:S(2)}, u32[]{:S(2)}) collective-permute-start(bf16[256,512]{1,0:T(8,128)(2,1)S(1)} %shard_map.100.refs_2_.refs_3_), channel_id=1, source_target_pairs={{0,2},{2,0},{4,6},{6,4},{8,10},{10,8},{12,14},{14,12},{16,18},{18,... | collective-permute-start | bytes 786440 | tf_op jit(solution)/shard_map/ppermute | solution.py:438
  21.6 17.4 %collective-permute-start.3 = (bf16[180,2048]{1,0:T(8,128)(2,1)S(1)}, bf16[180,2048]{1,0:T(8,128)(2,1)S(1)}, u32[]{:S(2)}, u32[]{:S(2)}) collective-permute-start(bf16[180,2048]{1,0:T(8,128)(2,1)S(1)} %collective-permute-done.refs_1_), channel_id=1, source_target_pairs={{0,4},{2,6},{4,0},{6,2},{8,16},{10,18},{12,20},{14,22},{16,8},{18,... | collective-permute-start | bytes 2211848 | tf_op jit(solution)/shard_map/ppermute | solution.py:430
  23.1 17.4 %collective-permute-start.2 = (bf16[180,2048]{1,0:T(8,128)(2,1)S(1)}, bf16[180,2048]{1,0:T(8,128)(2,1)S(1)}, u32[]{:S(2)}, u32[]{:S(2)}) collective-permute-start(bf16[180,2048]{1,0:T(8,128)(2,1)S(1)} %collective-permute-done.1.refs_0_.refs_2_), channel_id=1, source_target_pairs={{0,8},{2,10},{4,12},{6,14},{8,0},{10,2},{12,4},{14,6},{16,24},{18,... | collective-permute-start | bytes 2211848 | tf_op jit(solution)/shard_map/ppermute | solution.py:430
  39.0 10.4 %collective-permute-start.13 = (bf16[256,512]{1,0:T(8,128)(2,1)S(1)}, bf16[256,512]{1,0:T(8,128)(2,1)S(1)}, u32[]{:S(2)}, u32[]{:S(2)}) collective-permute-start(bf16[256,512]{1,0:T(8,128)(2,1)S(1)} %shard_map.105.refs_7_.refs_8_), channel_id=1, source_target_pairs={{0,2},{2,0},{4,6},{6,4},{8,10},{10,8},{12,14},{14,12},{16,18},{18,... | collective-permute-start | bytes 786440 | tf_op jit(solution)/shard_map/ppermute | solution.py:438
  40.5 30.2 %collective-permute-start.7 = (bf16[180,2048]{1,0:T(8,128)(2,1)S(1)}, bf16[180,2048]{1,0:T(8,128)(2,1)S(1)}, u32[]{:S(2)}, u32[]{:S(2)}) collective-permute-start(bf16[180,2048]{1,0:T(8,128)(2,1)S(1)} %collective-permute-done.2.refs_2_.refs_4_), channel_id=1, source_target_pairs={{0,4},{2,6},{4,0},{6,2},{8,16},{10,18},{12,20},{14,22},{16,8},{18,... | collective-permute-start | bytes 2211848 | tf_op jit(solution)/shard_map/ppermute | solution.py:430
  42.0 28.7 %collective-permute-start.6 = (bf16[180,2048]{1,0:T(8,128)(2,1)S(1)}, bf16[180,2048]{1,0:T(8,128)(2,1)S(1)}, u32[]{:S(2)}, u32[]{:S(2)}) collective-permute-start(bf16[180,2048]{1,0:T(8,128)(2,1)S(1)} %collective-permute-done.3.refs_1_.refs_3_), channel_id=1, source_target_pairs={{0,8},{2,10},{4,12},{6,14},{8,0},{10,2},{12,4},{14,6},{16,24},{18,... | collective-permute-start | bytes 2211848 | tf_op jit(solution)/shard_map/ppermute | solution.py:430
  47.2 19.9 %copy-start = (bf16[2048,180]{0,1:T(8,128)(2,1)S(1)}, bf16[2048,180]{0,1:T(8,128)(2,1)}, u32[]{:S(2)}) copy-start(bf16[2048,180]{0,1:T(8,128)(2,1)} %param.18) | copy-start | bytes 2211844
  47.3 9.2 %collective-permute-start.12 = (bf16[256,512]{1,0:T(8,128)(2,1)S(1)}, bf16[256,512]{1,0:T(8,128)(2,1)S(1)}, u32[]{:S(2)}, u32[]{:S(2)}) collective-permute-start(bf16[256,512]{1,0:T(8,128)(2,1)S(1)} %shard_map.104.refs_6_.refs_7_), channel_id=1, source_target_pairs={{0,2},{2,0},{4,6},{6,4},{8,10},{10,8},{12,14},{14,12},{16,18},{18,... | collective-permute-start | bytes 786440 | tf_op jit(solution)/shard_map/ppermute | solution.py:438
  49.0 13.1 %collective-permute-start.11 = (bf16[256,512]{1,0:T(8,128)(2,1)S(1)}, bf16[256,512]{1,0:T(8,128)(2,1)S(1)}, u32[]{:S(2)}, u32[]{:S(2)}) collective-permute-start(bf16[256,512]{1,0:T(8,128)(2,1)S(1)} %shard_map.103.refs_5_.refs_6_), channel_id=1, source_target_pairs={{0,2},{2,0},{4,6},{6,4},{8,10},{10,8},{12,14},{14,12},{16,18},{18,... | collective-permute-start | bytes 786440 | tf_op jit(solution)/shard_map/ppermute | solution.py:438
  49.4 17.8 %collective-permute-start.14 = (bf16[256,512]{1,0:T(8,128)(2,1)S(1)}, bf16[256,512]{1,0:T(8,128)(2,1)S(1)}, u32[]{:S(2)}, u32[]{:S(2)}) collective-permute-start(bf16[256,512]{1,0:T(8,128)(2,1)S(1)} %shard_map.106.refs_8_.refs_9_), channel_id=1, source_target_pairs={{0,2},{2,0},{4,6},{6,4},{8,10},{10,8},{12,14},{14,12},{16,18},{18,... | collective-permute-start | bytes 786440 | tf_op jit(solution)/shard_map/ppermute | solution.py:438
  56.5 20.3 %collective-permute-start.15 = (bf16[256,512]{1,0:T(8,128)(2,1)S(1)}, bf16[256,512]{1,0:T(8,128)(2,1)S(1)}, u32[]{:S(2)}, u32[]{:S(2)}) collective-permute-start(bf16[256,512]{1,0:T(8,128)(2,1)S(1)} %shard_map.107.refs_9_.refs_10_), channel_id=1, source_target_pairs={{0,2},{2,0},{4,6},{6,4},{8,10},{10,8},{12,14},{14,12},{16,18},{18,... | collective-permute-start | bytes 786440 | tf_op jit(solution)/shard_map/ppermute | solution.py:438
  70.8 12.3 %collective-permute-start.17 = (bf16[180,1024]{1,0:T(8,128)(2,1)S(1)}, bf16[180,1024]{1,0:T(8,128)(2,1)S(1)}, u32[]{:S(2)}, u32[]{:S(2)}) collective-permute-start(bf16[180,1024]{1,0:T(8,128)(2,1)S(1)} %get-tuple-element.85), channel_id=1, source_target_pairs={{0,4},{2,6},{4,0},{6,2},{8,16},{10,18},{12,20},{14,22},{16,8},{18,... | collective-permute-start | bytes 1105928 | tf_op jit(solution)/shard_map/ppermute | solution.py:456
  72.2 11.4 %collective-permute-start.18 = (bf16[180,1024]{1,0:T(8,128)(2,1)S(1)}, bf16[180,1024]{1,0:T(8,128)(2,1)S(1)}, u32[]{:S(2)}, u32[]{:S(2)}) collective-permute-start(bf16[180,1024]{1,0:T(8,128)(2,1)S(1)} %get-tuple-element.86), channel_id=1, source_target_pairs={{0,8},{2,10},{4,12},{6,14},{8,0},{10,2},{12,4},{14,6},{16,24},{18,... | collective-permute-start | bytes 1105928 | tf_op jit(solution)/shard_map/ppermute | solution.py:456
  76.7 16.4 %collective-permute-start.5 = (bf16[1,3,180,256]{3,2,1,0:T(8,128)(2,1)S(1)}, bf16[1,3,180,256]{3,2,1,0:T(8,128)(2,1)S(1)}, u32[]{:S(2)}, u32[]{:S(2)}) collective-permute-start(bf16[1,3,180,256]{3,2,1,0:T(8,128)(2,1)S(1)} %get-tuple-element.77), channel_id=1, source_target_pairs={{0,1},{1,0},{2,3},{3,2},{4,5},{5,4},{6,7},{7,6},{8,9},{9,8},{10,11... | collective-permute-start | bytes 829448 | tf_op jit(solution)/shard_map/ppermute | solution.py:443
  78.1 9.8 %collective-permute-start.22 = (bf16[1,3,180,256]{3,2,1,0:T(8,128)(2,1)S(1)}, bf16[1,3,180,256]{3,2,1,0:T(8,128)(2,1)S(1)}, u32[]{:S(2)}, u32[]{:S(2)}) collective-permute-start(bf16[1,3,180,256]{3,2,1,0:T(8,128)(2,1)S(1)} %get-tuple-element.94), channel_id=1, source_target_pairs={{0,1},{1,0},{2,3},{3,2},{4,5},{5,4},{6,7},{7,6},{8,9},{9,8},{10,11... | collective-permute-start | bytes 829448 | tf_op jit(solution)/shard_map/ppermute | solution.py:443
  79.7 8.8 %collective-permute-start.20 = (bf16[1,2,180,256]{3,2,1,0:T(8,128)(2,1)S(1)}, bf16[1,2,180,256]{3,2,1,0:T(8,128)(2,1)S(1)}, u32[]{:S(2)}, u32[]{:S(2)}) collective-permute-start(bf16[1,2,180,256]{3,2,1,0:T(8,128)(2,1)S(1)} %get-tuple-element.92), channel_id=1, source_target_pairs={{0,1},{1,0},{2,3},{3,2},{4,5},{5,4},{6,7},{7,6},{8,9},{9,8},{10,11... | collective-permute-start | bytes 552968 | tf_op jit(solution)/shard_map/ppermute | solution.py:443
  83.1 7.2 %collective-permute-start.16 = (bf16[2,2,180,256]{3,2,1,0:T(8,128)(2,1)S(1)}, bf16[2,2,180,256]{3,2,1,0:T(8,128)(2,1)S(1)}, u32[]{:S(2)}, u32[]{:S(2)}) collective-permute-start(bf16[2,2,180,256]{3,2,1,0:T(8,128)(2,1)S(1)} %get-tuple-element.81), channel_id=1, source_target_pairs={{0,1},{1,0},{2,3},{3,2},{4,5},{5,4},{6,7},{7,6},{8,9},{9,8},{10,11... | collective-permute-start | bytes 1105928 | tf_op jit(solution)/shard_map/ppermute | solution.py:443
  85.3 5.5 %collective-permute-start.19 = (bf16[2,1,180,256]{3,2,1,0:T(8,128)(2,1)S(1)}, bf16[2,1,180,256]{3,2,1,0:T(8,128)(2,1)S(1)}, u32[]{:S(2)}, u32[]{:S(2)}) collective-permute-start(bf16[2,1,180,256]{3,2,1,0:T(8,128)(2,1)S(1)} %get-tuple-element.88), channel_id=1, source_target_pairs={{0,1},{1,0},{2,3},{3,2},{4,5},{5,4},{6,7},{7,6},{8,9},{9,8},{10,11... | collective-permute-start | bytes 552968 | tf_op jit(solution)/shard_map/ppermute | solution.py:443
  87.9 4.8 %collective-permute-start.4 = (bf16[1,2,180,256]{3,2,1,0:T(8,128)(2,1)S(1)}, bf16[1,2,180,256]{3,2,1,0:T(8,128)(2,1)S(1)}, u32[]{:S(2)}, u32[]{:S(2)}) collective-permute-start(bf16[1,2,180,256]{3,2,1,0:T(8,128)(2,1)S(1)} %get-tuple-element.75), channel_id=1, source_target_pairs={{0,1},{1,0},{2,3},{3,2},{4,5},{5,4},{6,7},{7,6},{8,9},{9,8},{10,11... | collective-permute-start | bytes 552968 | tf_op jit(solution)/shard_map/ppermute | solution.py:443
  88.4 18.9 %copy-start.1 = (s32[128]{0:T(128)S(1)}, s32[128]{0:T(128)}, u32[]{:S(2)}) copy-start(s32[128]{0:T(128)} %constant.11.clone.slot_ref) | copy-start | bytes 1540
  88.5 13.7 %collective-permute-start.23 = (bf16[3,180,256]{2,1,0:T(8,128)(2,1)S(1)}, bf16[3,180,256]{2,1,0:T(8,128)(2,1)S(1)}, u32[]{:S(2)}, u32[]{:S(2)}) collective-permute-start(bf16[3,180,256]{2,1,0:T(8,128)(2,1)S(1)} %shard_map.120), channel_id=1, source_target_pairs={{0,2},{2,0},{4,6},{6,4},{8,10},{10,8},{12,14},{14,12},{16,18},{18,... | collective-permute-start | bytes 829448 | tf_op jit(solution)/shard_map/ppermute | solution.py:465
  90.4 11.9 %collective-permute-start.21 = (bf16[2,180,256]{2,1,0:T(8,128)(2,1)S(1)}, bf16[2,180,256]{2,1,0:T(8,128)(2,1)S(1)}, u32[]{:S(2)}, u32[]{:S(2)}) collective-permute-start(bf16[2,180,256]{2,1,0:T(8,128)(2,1)S(1)} %shard_map.118), channel_id=1, source_target_pairs={{0,2},{2,0},{4,6},{6,4},{8,10},{10,8},{12,14},{14,12},{16,18},{18,... | collective-permute-start | bytes 552968 | tf_op jit(solution)/shard_map/ppermute | solution.py:465
  90.8 15.4 %collective-permute-start.24 = (bf16[2,180,256]{2,1,0:T(8,128)(2,1)S(1)}, bf16[2,180,256]{2,1,0:T(8,128)(2,1)S(1)}, u32[]{:S(2)}, u32[]{:S(2)}) collective-permute-start(bf16[2,180,256]{2,1,0:T(8,128)(2,1)S(1)} %get-tuple-element.95), channel_id=1, source_target_pairs={{0,2},{2,0},{4,6},{6,4},{8,10},{10,8},{12,14},{14,12},{16,18},{18,... | collective-permute-start | bytes 552968 | tf_op jit(solution)/shard_map/ppermute | solution.py:469
  92.7 14.7 %collective-permute-start.25 = (bf16[1,180,256]{2,1,0:T(8,128)(2,1)S(1)}, bf16[1,180,256]{2,1,0:T(8,128)(2,1)S(1)}, u32[]{:S(2)}, u32[]{:S(2)}) collective-permute-start(bf16[1,180,256]{2,1,0:T(8,128)(2,1)S(1)} %get-tuple-element.96), channel_id=1, source_target_pairs={{0,2},{2,0},{4,6},{6,4},{8,10},{10,8},{12,14},{14,12},{16,18},{18,... | collective-permute-start | bytes 276488 | tf_op jit(solution)/shard_map/ppermute | solution.py:469
